TPU v7x, 128 devices: a whole 4x4x4 slice. The times are simulated.
128 devices in a mesh: tp: 16 (over z, y), dp: 8 (over x, core).
Axes of the slice: x: 4, y: 4, z: 4, core: 2. Of those that a mesh axis runs over, the one named last changes fastest.
Arguments:
- hidden: bfloat16 [2048, 2048], P('dp')
- embedding: bfloat16 [128256, 2048], P('tp')
- norm_weight: float32 [2048], replicated
- teach_ids: int32 [2048, 256], P('dp')
- teach_prob: float32 [2048, 256], P('dp')
- tok_mask: float32 [2048], P('dp')
Outputs:
- output 1: float32 [], replicated
- output 2: bfloat16 [2048, 2048], P('dp')
- output 3: float32 [128256, 2048], P('tp', 'dp')
- output 4: float32 [2048], replicated
All inputs are finite; a program needn't handle non-finite values.
Results may differ from a plain program's by a relative error of at most 0.001.
Values sent between devices are 32-bit elements.
A program may use at most 1 GiB of HBM per device.

v0:
```python
import jax
import jax.numpy as jnp
from jax import lax
from jax.sharding import PartitionSpec as P

EPS_NORM = 1e-6


def solution(mesh):
    def local_head(hidden, embedding, norm_weight, teach_ids, teach_prob, tok_mask):
        vocab_local = embedding.shape[0]
        tok_local = hidden.shape[0]
        shard_pos = lax.axis_index('tp')
        mask_total = lax.psum(jnp.sum(tok_mask), 'dp')
        scale_w = 1.0 + norm_weight
        h_f32 = hidden.astype(jnp.float32)
        inv_rms = lax.rsqrt(jnp.mean(h_f32 * h_f32, axis=1, keepdims=True) + EPS_NORM)
        normed = h_f32 * inv_rms
        normed_bf = (normed * scale_w).astype(jnp.bfloat16)
        logits = lax.dot_general(normed_bf, embedding, (((1,), (1,)), ((), ())), preferred_element_type=jnp.float32)
        row_max = lax.pmax(jnp.max(logits, axis=1, keepdims=True), 'tp')
        shifted = jnp.exp(logits - row_max)
        local_ids = teach_ids - shard_pos * vocab_local
        in_range = (local_ids >= 0) & (local_ids < vocab_local)
        safe_ids = jnp.where(in_range, local_ids, 0)
        picked = jnp.take_along_axis(logits, safe_ids, axis=1)
        teach_part = jnp.sum(jnp.where(in_range, teach_prob * picked, 0.0), axis=1)
        row_stats = lax.psum(jnp.stack([jnp.sum(shifted, axis=1), teach_part], axis=1), 'tp')
        sum_exp = row_stats[:, 0:1]
        log_norm = row_max + jnp.log(sum_exp)
        loss_sum = lax.psum(jnp.sum(tok_mask * (row_stats[:, 1] - log_norm[:, 0])), 'dp')
        loss_mean = -loss_sum / mask_total
        weight = (tok_mask / mask_total)[:, None]
        soft_prob = shifted * (1.0 / sum_exp)
        row_ids = jnp.arange(tok_local)[:, None]
        d_logits = (soft_prob * weight).at[row_ids, safe_ids].add(jnp.where(in_range, -teach_prob * weight, 0.0))
        dlogit_bf = d_logits.astype(jnp.bfloat16)
        grad_u = lax.psum(jnp.dot(dlogit_bf, embedding, preferred_element_type=jnp.float32), 'tp')
        embed_part = lax.dot_general(dlogit_bf, normed_bf, (((0,), (0,)), ((), ())), preferred_element_type=jnp.float32)
        grad_embed = lax.psum_scatter(embed_part, 'dp', scatter_dimension=1, tiled=True)
        d_normed = grad_u * scale_w
        grad_hidden = (inv_rms * (d_normed - normed * jnp.mean(d_normed * normed, axis=1, keepdims=True))).astype(jnp.bfloat16)
        grad_norm = lax.psum(jnp.sum(grad_u * normed, axis=0), 'dp')
        return loss_mean, grad_hidden, grad_embed, grad_norm

    return jax.shard_map(local_head, mesh=mesh, in_specs=(P('dp', None), P('tp', None), P(None), P('dp', None), P('dp', None), P('dp')), out_specs=(P(), P('dp', None), P('tp', 'dp'), P(None)), check_vma=False)
```

profile of v0, /device:TPU:1, one launch (start us, length us, event | category | flops | bytes accessed | tf_op | source)
XLA Modules:
  0.0 3764.1 jit_solution(15353758187678645673)
XLA Ops:
  8.0 0.0 all-reduce.3.cloned.1.call-start
  8.0 1.5 fusion.11
  9.6 0.0 copy-start.5
  9.6 0.7 broadcast_add_fusion
  10.3 0.0 copy-start.3
  10.3 1.1 or_bitcast_fusion
  11.4 0.1 copy.10
  11.5 0.8 and_reduce_fusion
  12.4 0.8 multiply_reduce_fusion
  13.2 0.1 copy.12
  13.3 18.3 fusion.19
  31.6 0.0 copy-done.5
  31.6 0.0 copy-done.3
  31.6 35.5 pmax.7
  67.1 2305.9 %gather_fusion = f32[65536]{0:T(1024)S(1)} fusion(f32[256,8016]{0,1:T(8,128)} %get-tuple-element.15, s32[65536]{0:T(1024)S(1)} %bitcast.28), kind=kCustom, calls=%fused_computation | custom fusion | bytes 1048576 | tf_op jit(solution)/shard_map/jit(take_along_axis)/gather | solution.py:26
  2373.0 0.0 copy-start.1
  2373.0 0.0 copy-start.2
  2373.1 0.0 copy-start.7
  2373.1 0.1 reshape.43
  2373.1 4.5 fusion
  2377.7 0.0 copy-done.1
  2377.7 0.0 copy-done.2
  2377.7 0.2 select_reduce_fusion
  2377.9 517.1 %psum.35 = f32[256,2]{0,1:T(2,128)S(1)} all-reduce(f32[256,2]{0,1:T(2,128)S(1)} %pad_maximum_fusion), channel_id=1, replica_groups=mesh['tp'=16,'dp'=8] {'tp'}, use_global_device_ids=true, to_apply=%region_5.6 | all-reduce | flops 512 | bytes 4096 | tf_op jit(solution)/shard_map/psum | solution.py:28
  2895.0 0.0 copy-done.7
  2895.0 0.6 fusion.17
  2895.6 27.7 psum.37
  2923.3 0.6 broadcast_divide_fusion
  2924.0 0.1 select_bitcast_fusion.1
  2924.1 4.7 multiply_bitcast_fusion
  2928.8 15.1 copy.11
  2943.8 0.1 copy.13
  2944.0 355.9 %scatter_fusion = f32[2052096]{0:T(1024)} fusion(f32[2052096]{0:T(1024)} %bitcast.27, s32[65536]{0:T(1024)S(1)} %bitcast.29, f32[65536]{0:T(1024)S(1)} %bitcast.30), kind=kCustom, calls=%fused_computation.1 | custom fusion | flops 65536 | bytes 1048576
  3299.9 5.0 convert_element_type.17
  3304.9 7.0 reshape.39
  3311.9 0.0 copy-start
  3311.9 0.0 copy-start.4
  3311.9 0.0 copy-start.6
  3311.9 17.2 fusion.20
  3329.0 0.0 all-reduce.3.cloned.1.call-update
  3329.1 0.0 reduce-scatter.2.cloned.1.call-start
  3329.1 0.0 copy-done
  3329.1 0.0 copy-done.4
  3329.1 0.0 copy-done.6
  3329.2 24.9 fusion.12
  3354.1 0.0 reduce-scatter.2.cloned.1.call-update
  3354.1 144.7 %all-reduce.3.cloned.1.call-done = f32[256,2048]{1,0:T(8,128)} async-done(((f32[256,2048]{1,0:T(8,128)}), f32[256,2048]{1,0:T(8,128)}) %all-reduce.3.cloned.1.call-update) | async-done | bytes 2097168 | tf_op jit(solution)/shard_map/psum | solution.py:38
  3498.8 2.2 fusion.10
  3501.0 15.2 all-reduce
  3517.6 3.1 fusion.9
  3520.7 234.8 %reduce-scatter.2.cloned.1.call-done = f32[8016,256]{1,0:T(8,128)} async-done(((f32[8016,2048]{1,0:T(8,128)}), f32[8016,256]{1,0:T(8,128)}) %reduce-scatter.2.cloned.1.call-update) | async-done | bytes 8208400 | tf_op jit(solution)/shard_map/reduce_scatter | solution.py:40
  (6 shorter events, 0.1 us)
Async XLA Ops:
  8.0 3490.8 %all-reduce.3.cloned.1.call-start = ((), (), s32[]{:S(2)}) async-start(), calls=%async_computation.1 | async-start | bytes 4194304 | tf_op jit(solution)/shard_map/psum | solution.py:38
  9.6 22.0 copy-start.5
  10.3 21.3 copy-start.3
  2373.0 4.6 copy-start.1
  2373.0 4.6 copy-start.2
  2373.1 521.9 %copy-start.7 = (f32[256]{0:T(256)S(1)}, f32[256]{0:T(256)}, u32[]{:S(2)}) copy-start(f32[256]{0:T(256)} %param.11) | copy-start | bytes 3076
  3311.9 17.2 copy-start
  3311.9 17.2 copy-start.4
  3311.9 17.3 copy-start.6
  3329.1 426.4 %reduce-scatter.2.cloned.1.call-start = ((), (), s32[]{:S(2)}) async-start(), calls=%async_computation.2 | async-start | bytes 73875456 | tf_op jit(solution)/shard_map/reduce_scatter | solution.py:40
Sparse Core Ops, SparseCore 0:
  3329.2 169.5 all-reduce.2
Sparse Core Ops, SparseCore 1:
  3354.2 401.2 reduce-scatter.1
where the time goes:
time: 3820 us; the launch traced here: 3760 us
  local copies, waits for them, and re-layouts  2330 us (61%)
  blocking collectives  596 us (16%)
  other arithmetic  382 us (10%)
  waiting for transfers between devices  380 us (10%)
  matrix products  60.3 us (2%)
    gather x3, local copies, waits for them, and re-layouts, local_head(): picked = jnp.take_along_axis(logits, safe_ids, axis=1)  2310 us
    psum x1, blocking collectives, local_head(): lax.psum(jnp.stack([jnp.sum(shifted, axis=1), teach_part], axis=1), 'tp')  517 us
    unnamed x7, other arithmetic  363 us
    reduce_scatter x1, waiting for transfers between devices, local_head(): lax.psum_scatter(embed_part, 'dp', scatter_dimension=1, tiled=True)  235 us
    psum x1, waiting for transfers between devices, local_head(): lax.psum(jnp.dot(dlogit_bf, embedding, preferred_element_type=jnp.float32...  145 us
  transfers between devices with their start and end apart: 2, of which 2 were waited for; matrix products, arithmetic and copies ran while one was open for 1% of the time, Pallas kernels for 0%

commit v1 on v0

v1 whole, which is shorter than its diff:
```python
import functools

import jax
import jax.numpy as jnp
import numpy as np
from jax import lax
from jax.experimental import pallas as pl
from jax.experimental.pallas import tpu as pltpu
from jax.sharding import Mesh
from jax.sharding import PartitionSpec as P


EPS_NORM = 1e-6
NEG = -1e30
BIG = 1e30
F32 = jnp.float32
BF16 = jnp.bfloat16
I32 = jnp.int32
SLOTS = 8
FAST = 2
VB = 256
VB1 = 512
VMEM_LIMIT = 60 * 1024 * 1024
MESH = pl.DeviceIdType.MESH


def params(**kw):
    return pltpu.CompilerParams(vmem_limit_bytes=VMEM_LIMIT, **kw)


def cost(flops, nbytes, trans=0):
    return pl.CostEstimate(flops=int(flops), bytes_accessed=int(nbytes), transcendentals=int(trans))


def sort_kernel(ids_ref, pt_ref, mask_ref, out_ref):
    n = ids_ref.shape[1]
    sub = lax.broadcasted_iota(I32, (8, 128), 0)
    for g in range(ids_ref.shape[0] // 128):
        cols = slice(g * 128, (g + 1) * 128)
        key = (ids_ref[cols, :] + 1).astype(F32).T
        prob = pt_ref[cols, :].T
        k = [key[8 * a:8 * a + 8, :] for a in range(n // 8)]
        p = [prob[8 * a:8 * a + 8, :] for a in range(n // 8)]
        size = 2
        while size <= n:
            j = size // 2
            while j >= 1:
                if j >= 8:
                    for a in range(n // 8):
                        if (8 * a) & j:
                            continue
                        b = a + j // 8
                        up = ((8 * a) & size) == 0
                        swap = k[a] > k[b] if up else k[a] < k[b]
                        lo, hi = jnp.minimum(k[a], k[b]), jnp.maximum(k[a], k[b])
                        k[a], k[b] = (lo, hi) if up else (hi, lo)
                        p[a], p[b] = jnp.where(swap, p[b], p[a]), jnp.where(swap, p[a], p[b])
                else:
                    low = (sub & j) == 0
                    for a in range(n // 8):
                        if size >= 8:
                            up = ((8 * a) & size) == 0
                            want_min = low if up else (sub & j) != 0
                        else:
                            want_min = ((sub & j) == 0) == ((sub & size) == 0)
                        ka = jnp.where(low, pltpu.roll(k[a], 8 - j, 0), pltpu.roll(k[a], j, 0))
                        pa = jnp.where(low, pltpu.roll(p[a], 8 - j, 0), pltpu.roll(p[a], j, 0))
                        new = jnp.where(want_min, jnp.minimum(k[a], ka), jnp.maximum(k[a], ka))
                        p[a] = jnp.where(new == ka, pa, p[a])
                        k[a] = new
                j //= 2
            size *= 2
        sign = jnp.where(mask_ref[:, cols] > 0, 1.0, -1.0)
        for a in range(n // 8):
            out_ref[8 * a:8 * a + 8, cols] = k[a] * sign
            out_ref[n + 8 * a:n + 8 * a + 8, cols] = p[a]


def sort_lists(ids, prob, mask):
    tokens, top = ids.shape
    return pl.pallas_call(
        sort_kernel,
        out_shape=jax.ShapeDtypeStruct((2 * top, tokens), F32),
        in_specs=[pl.BlockSpec(memory_space=pltpu.VMEM)] * 3,
        out_specs=pl.BlockSpec(memory_space=pltpu.VMEM),
        compiler_params=params(),
        cost_estimate=cost(4e9, 4 * 4 * tokens * top),
        name='sort_lists',
    )(ids, prob, mask[None, :])


def expand_kernel(nblk, sc_ref, list_ref, w_ref, tabr_ref, tabp_ref, cnt_ref, loc_ref, pw_ref):
    base, rows = sc_ref[0], sc_ref[1]
    top = list_ref.shape[0] // 2
    nq = top // 8
    sub = lax.broadcasted_iota(I32, (8, 128), 0)
    w = w_ref[...]
    over = jnp.zeros((8, 128), I32)
    prev = None
    for q in range(nq):
        ids = jnp.abs(list_ref[8 * q:8 * q + 8, :]).astype(I32) - 1 - base
        ok = (ids >= 0) & (ids < rows)
        loc = jnp.where(ok, ids, -1)
        loc_ref[8 * q:8 * q + 8, :] = loc
        pw_ref[8 * q:8 * q + 8, :] = list_ref[top + 8 * q:top + 8 * q + 8, :] * w
        blk = loc >> 7
        if prev is not None:
            over = jnp.where((blk == prev) & ok, 1, over)
        prev = blk
    for sh in (4, 2, 1):
        over = jnp.maximum(over, pltpu.roll(over, sh, 0))
    tile = min(nblk, 8)

    def body(bt, carry):
        b0 = bt * tile
        accc = [jnp.full((8, 128), -1, I32)] * tile
        accp = [jnp.zeros((8, 128), F32)] * tile
        for q in range(nq):
            loc = loc_ref[8 * q:8 * q + 8, :]
            blk = (loc >> 7) - b0
            code = (sub + 8 * q) * 128 + (loc & 127)
            p = pw_ref[8 * q:8 * q + 8, :]
            for i in range(tile):
                m = blk == i
                accc[i] = jnp.where(m, code, accc[i])
                accp[i] = jnp.where(m, p, accp[i])
        for i in range(tile):
            code, p = accc[i], accp[i]
            first = jnp.where(code >= 0, code, 1 << 24)
            for sh in (4, 2, 1):
                first = jnp.minimum(first, pltpu.roll(first, sh, 0))
            start = (first >> 7) & 7
            for sh in (1, 2, 4):
                move = (start & sh) != 0
                code = jnp.where(move, pltpu.roll(code, 8 - sh, 0), code)
                p = jnp.where(move, pltpu.roll(p, 8 - sh, 0), p)
            used = jnp.where(code >= 0, sub + 1, 0)
            for sh in (4, 2, 1):
                used = jnp.maximum(used, pltpu.roll(used, sh, 0))
            used = jnp.where(over > 0, SLOTS + 1, used)
            row = pl.multiple_of((b0 + i) * 8, 8)
            tabr_ref[pl.ds(row, 8), :] = jnp.where(code >= 0, code & 127, -1)
            tabp_ref[pl.ds(row, 8), :] = p
            cnt_ref[pl.ds(row, 8), :] = used
        return carry

    lax.fori_loop(0, nblk // tile, body, 0)


def expand(scal, lists, weight, nblk, list_map, groups):
    top = 256
    width = groups * 128
    full = jax.ShapeDtypeStruct((nblk * 8, width), F32)
    fulli = jax.ShapeDtypeStruct((nblk * 8, width), I32)
    tab = pl.BlockSpec((nblk * 8, 128), lambda g, s: (0, g))
    raw = pl.BlockSpec((top, 128), lambda g, s: (0, g))
    return pl.pallas_call(
        functools.partial(expand_kernel, nblk),
        out_shape=(fulli, full, fulli, jax.ShapeDtypeStruct((top, width), I32), jax.ShapeDtypeStruct((top, width), F32)),
        grid_spec=pltpu.PrefetchScalarGridSpec(
            num_scalar_prefetch=1,
            grid=(groups,),
            in_specs=[pl.BlockSpec((2 * top, 128), list_map), pl.BlockSpec((1, 128), lambda g, s: (0, g))],
            out_specs=(tab, tab, tab, raw, raw),
        ),
        compiler_params=params(),
        cost_estimate=cost(groups * 0.4e9, 4 * width * (4 * top + 3 * nblk * 8)),
    )(scal, lists, weight)


def fwd_kernel(own, sc_ref, *refs):
    ny = 2 if own else len(refs) - 6
    y_refs, (scale_ref, e_ref, z_ref, m_ref, s_ref, ut_ref) = refs[:ny], refs[ny:]
    i = pl.program_id(0)
    core, rows = sc_ref[3], sc_ref[1]
    step = 256

    @pl.when(i == 0)
    def _():
        scale = scale_ref[...]
        for a, y_ref in enumerate(y_refs):
            for r in range(0, y_ref.shape[0], step):
                u = (y_ref[r:r + step, :] * scale).astype(BF16).T
                if own:
                    slot = core if a == 0 else 1 - core
                    ut_ref[:, pl.ds(pl.multiple_of(slot * step, step), step)] = u
                else:
                    c0 = a * y_ref.shape[0] + r
                    ut_ref[:, c0:c0 + step] = u
        m_ref[...] = jnp.full(m_ref.shape, NEG, F32)
        s_ref[...] = jnp.zeros(s_ref.shape, F32)

    vb = e_ref.shape[0]
    left = rows - i * vb
    e = e_ref[...]
    nt = 512
    keep = lax.broadcasted_iota(I32, (vb, nt), 0) < left
    for c0 in range(0, ut_ref.shape[1], nt):
        cs = slice(c0, c0 + nt)
        z = jnp.dot(e, ut_ref[:, cs], preferred_element_type=F32)
        z = jnp.where(keep, z, NEG)
        z_ref[:, cs] = z
        z3 = z.reshape(vb // 8, 8, nt)
        old = m_ref[:, cs]
        new = jnp.maximum(old, jnp.max(z3, axis=0))
        m_ref[:, cs] = new
        s_ref[:, cs] = s_ref[:, cs] * jnp.exp(old - new) + jnp.sum(jnp.exp(z3 - new[None]), axis=0)


def forward(scal, ys, y_specs, scale, emb, half, width, own):
    dim = emb.shape[1]
    nb = half // VB
    stat = jax.ShapeDtypeStruct((8, width), F32)
    return pl.pallas_call(
        functools.partial(fwd_kernel, own),
        out_shape=(jax.ShapeDtypeStruct((half, width), F32), stat, stat),
        grid_spec=pltpu.PrefetchScalarGridSpec(
            num_scalar_prefetch=1,
            grid=(nb,),
            in_specs=list(y_specs) + [
                pl.BlockSpec((1, dim), lambda i, s: (0, 0)),
                pl.BlockSpec((VB, dim), lambda i, s: (s[3] * nb + i, 0)),
            ],
            out_specs=(
                pl.BlockSpec((VB, width), lambda i, s: (i, 0)),
                pl.BlockSpec((8, width), lambda i, s: (0, 0)),
                pl.BlockSpec((8, width), lambda i, s: (0, 0)),
            ),
            scratch_shapes=[pltpu.VMEM((dim, width), BF16)],
        ),
        compiler_params=params(dimension_semantics=('arbitrary',)),
        cost_estimate=cost(2.0 * half * width * dim, half * dim * 2 + half * width * 4 + width * dim * 4, half * width),
    )(scal, *ys, scale, emb)


def stats_kernel(tps, xs, groups, m_ref, s_ref, add_ref, lse_ref, tot_ref, send, recv, xrecv, ssem, rsem, xssem, xrsem):
    t, x, c = lax.axis_index('tp'), lax.axis_index('x'), lax.axis_index('core')
    me = t * 2 + c
    peers = tps * 2
    m = jnp.max(m_ref[...], axis=0, keepdims=True)
    s = jnp.sum(s_ref[...] * jnp.exp(m_ref[...] - m), axis=0, keepdims=True)
    send[...] = jnp.zeros(send.shape, F32)
    for g in range(groups):
        send[g:g + 1, :] = m[:, g * 128:(g + 1) * 128]
        send[groups + g:groups + g + 1, :] = s[:, g * 128:(g + 1) * 128]
    send[2 * groups:2 * groups + 1, :] = add_ref[...]

    barrier = pltpu.get_barrier_semaphore()

    def peer(j):
        r = lax.rem(me + j, peers)
        return {'tp': r // 2, 'core': lax.rem(r, 2)}

    def hello(j, carry):
        pl.semaphore_signal(barrier, inc=1, device_id=peer(j), device_id_type=MESH)
        return carry

    lax.fori_loop(1, peers, hello, 0)
    for j in range(1, xs):
        pl.semaphore_signal(barrier, inc=1, device_id={'x': lax.rem(x + j, xs)}, device_id_type=MESH)
    pl.semaphore_wait(barrier, peers - 1 + xs - 1)

    def copy(j):
        return pltpu.make_async_remote_copy(
            src_ref=send, dst_ref=recv.at[j], send_sem=ssem.at[j], recv_sem=rsem.at[j],
            device_id=peer(j), device_id_type=MESH)

    def xcopy(j):
        return pltpu.make_async_remote_copy(
            src_ref=send, dst_ref=xrecv.at[j], send_sem=xssem.at[j], recv_sem=xrsem.at[j],
            device_id={'x': lax.rem(x + j, xs)}, device_id_type=MESH)

    def start(j, carry):
        copy(j).start()
        return carry

    lax.fori_loop(1, peers, start, 0)
    for j in range(1, xs):
        xcopy(j).start()

    def finish(j, carry):
        copy(j).wait()
        return carry

    lax.fori_loop(1, peers, finish, 0)
    tot = send[2 * groups:2 * groups + 1, :]
    for j in range(1, xs):
        xcopy(j).wait()
        tot = tot + xrecv[j, 2 * groups:2 * groups + 1, :]
    tot_ref[...] = tot

    def most(j, best):
        return jnp.maximum(best, recv[j, 0:groups, :])

    best = lax.fori_loop(1, peers, most, send[0:groups, :])

    def add(j, acc):
        return acc + recv[j, groups:2 * groups, :] * jnp.exp(recv[j, 0:groups, :] - best)

    acc = lax.fori_loop(1, peers, add, send[groups:2 * groups, :] * jnp.exp(send[0:groups, :] - best))
    lse_ref[...] = best + jnp.log(acc)


def stats(m8, s8, add, tps, xs, cid):
    width = m8.shape[1]
    groups = width // 128
    rows = -(-(2 * groups + 1) // 8) * 8
    vm = pl.BlockSpec(memory_space=pltpu.VMEM)
    return pl.pallas_call(
        functools.partial(stats_kernel, tps, xs, groups),
        out_shape=(jax.ShapeDtypeStruct((groups, 128), F32), jax.ShapeDtypeStruct((1, 128), F32)),
        in_specs=[vm] * 3,
        out_specs=(vm, vm),
        scratch_shapes=[
            pltpu.VMEM((rows, 128), F32),
            pltpu.VMEM((2 * tps, rows, 128), F32),
            pltpu.VMEM((xs, rows, 128), F32),
            pltpu.SemaphoreType.DMA((2 * tps,)),
            pltpu.SemaphoreType.DMA((2 * tps,)),
            pltpu.SemaphoreType.DMA((xs,)),
            pltpu.SemaphoreType.DMA((xs,)),
        ],
        compiler_params=params(collective_id=cid, has_side_effects=True),
        cost_estimate=cost(2e9, 1 << 16),
    )(m8, s8, add)


def fill_teacher(cnt_ref, first, nrb, tabr_ref, tabp_ref, loc_hbm, pw_hbm, tm, loc_s, pw_s, sem):
    width = tm.shape[1]
    iota = lax.broadcasted_iota(I32, (128, 128), 0)
    for rb in range(nrb):
        n = cnt_ref[first + rb]

        def tile(g, carry):
            lanes = pl.ds(pl.multiple_of(g * 128, 128), 128)

            @pl.when(n <= SLOTS)
            def _():
                row = tabr_ref[8 * rb:8 * rb + 8, lanes]
                val = tabp_ref[8 * rb:8 * rb + 8, lanes]
                t = jnp.zeros((128, 128), F32)
                for s in range(SLOTS):
                    t = jnp.where(iota == row[s:s + 1, :], val[s:s + 1, :], t)
                tm[rb * 128:(rb + 1) * 128, lanes] = t

            @pl.when(n > SLOTS)
            def _():
                a = pltpu.make_async_copy(loc_hbm.at[:, lanes], loc_s, sem.at[0])
                b = pltpu.make_async_copy(pw_hbm.at[:, lanes], pw_s, sem.at[1])
                a.start()
                b.start()
                a.wait()
                b.wait()
                base = (first + rb) * 128

                def entries(k, t):
                    here = pl.ds(pl.multiple_of(k * 8, 8), 8)
                    row = loc_s[here, :] - base
                    val = pw_s[here, :]
                    for s in range(8):
                        t = jnp.where(iota == row[s:s + 1, :], val[s:s + 1, :], t)
                    return t

                tm[rb * 128:(rb + 1) * 128, lanes] = lax.fori_loop(
                    0, loc_s.shape[0] // 8, entries, jnp.zeros((128, 128), F32))

            return carry

        lax.fori_loop(0, width // 128, tile, 0)


def teacher_fast(tabr_ref, tabp_ref, rb, cs, n):
    iota = lax.broadcasted_iota(I32, (128, n), 0)
    t = jnp.zeros((128, n), F32)
    for s in range(FAST):
        row = tabr_ref[8 * rb + s:8 * rb + s + 1, cs]
        t = jnp.where(iota == row, tabp_ref[8 * rb + s:8 * rb + s + 1, cs], t)
    return t


def most_slots(cnt_ref, first, nrb):
    n = cnt_ref[first]
    for rb in range(1, nrb):
        n = jnp.maximum(n, cnt_ref[first + rb])
    return n


def du_kernel(sc_ref, cnt_ref, z_ref, c_ref, e_ref, tabr_ref, tabp_ref, loc_hbm, pw_hbm, du_ref, g_ref, tz_ref,
              tm, loc_s, pw_s, sem):
    i = pl.program_id(0)
    rows = sc_ref[1]
    vb, width = z_ref.shape
    nrb = vb // 128
    left = rows - i * vb

    @pl.when(i == 0)
    def _():
        du_ref[...] = jnp.zeros(du_ref.shape, F32)
        tz_ref[...] = jnp.zeros(tz_ref.shape, F32)

    slots = most_slots(cnt_ref, i * nrb, nrb)

    def make(teacher):
        for cs0 in range(0, width, 256):
            cs = slice(cs0, cs0 + 256)
            tz = jnp.zeros((8, 256), F32)
            for rb in range(nrb):
                rs = slice(rb * 128, (rb + 1) * 128)
                z = z_ref[rs, cs]
                t = teacher(rb, rs, cs)
                g_ref[rs, cs] = (jnp.exp(z - c_ref[:, cs]) - t).astype(BF16)
                tz = tz + jnp.sum((t * z).reshape(16, 8, 256), axis=0)
            tz_ref[:, cs] += tz

    @pl.when(slots <= FAST)
    def _():
        make(lambda rb, rs, cs: teacher_fast(tabr_ref, tabp_ref, rb, cs, 256))

    @pl.when(slots > FAST)
    def _():
        fill_teacher(cnt_ref, i * nrb, nrb, tabr_ref, tabp_ref, loc_hbm, pw_hbm, tm, loc_s, pw_s, sem)
        make(lambda rb, rs, cs: tm[rs, cs])

    keep = lax.broadcasted_iota(I32, e_ref.shape, 0) < left
    e = jnp.where(keep, e_ref[...], jnp.zeros((), BF16))
    du_ref[...] += lax.dot_general(g_ref[...], e, (((0,), (0,)), ((), ())), preferred_element_type=F32)


def du_call(scal, cnt, z, c, emb, tables, half):
    tabr, tabp, loc, pw = tables
    width, dim = z.shape[1], emb.shape[1]
    nb = half // VB1
    trows = VB1 // 128 * 8
    anyspace = pl.BlockSpec(memory_space=pl.ANY)
    return pl.pallas_call(
        du_kernel,
        out_shape=(
            jax.ShapeDtypeStruct((width, dim), F32),
            jax.ShapeDtypeStruct((half, width), BF16),
            jax.ShapeDtypeStruct((8, width), F32),
        ),
        grid_spec=pltpu.PrefetchScalarGridSpec(
            num_scalar_prefetch=2,
            grid=(nb,),
            in_specs=[
                pl.BlockSpec((VB1, width), lambda i, s, n: (i, 0)),
                pl.BlockSpec((1, width), lambda i, s, n: (0, 0)),
                pl.BlockSpec((VB1, dim), lambda i, s, n: (s[3] * nb + i, 0)),
                pl.BlockSpec((trows, width), lambda i, s, n: (i, 0)),
                pl.BlockSpec((trows, width), lambda i, s, n: (i, 0)),
                anyspace,
                anyspace,
            ],
            out_specs=(
                pl.BlockSpec((width, dim), lambda i, s, n: (0, 0)),
                pl.BlockSpec((VB1, width), lambda i, s, n: (i, 0)),
                pl.BlockSpec((8, width), lambda i, s, n: (0, 0)),
            ),
            scratch_shapes=[
                pltpu.VMEM((VB1, width), F32),
                pltpu.VMEM((loc.shape[0], 128), I32),
                pltpu.VMEM((loc.shape[0], 128), F32),
                pltpu.SemaphoreType.DMA((2,)),
            ],
        ),
        compiler_params=params(dimension_semantics=('arbitrary',)),
        cost_estimate=cost(2.0 * half * width * dim, half * dim * 2 + half * width * 6 + width * dim * 4, half * width),
        name='grad_u',
    )(scal, cnt, z, c, emb, tabr, tabp, loc, pw)


def de_kernel(b0, ny, aliased, sc_ref, cnt_ref, *refs):
    y_refs = refs[:ny]
    (scale_ref, z_ref, c_ref, gown_ref, tabr_ref, tabp_ref, loc_hbm, pw_hbm) = refs[ny:ny + 8]
    rest = refs[ny + 8 + (1 if aliased else 0):]
    out_ref, part_ref, u_ref, g_ref, tm, loc_s, pw_s, sem = rest
    i = pl.program_id(0)
    core = sc_ref[3]
    vb, width = z_ref.shape
    mine = gown_ref.shape[1]
    cols = out_ref.shape[1]
    nrb = vb // 128

    @pl.when(i == 0)
    def _():
        for a, y_ref in enumerate(y_refs):
            n = y_ref.shape[0]
            for k in range(2):
                src = pl.multiple_of((core if k == 0 else 1 - core) * cols, cols)
                u = y_ref[:, pl.ds(src, cols)] * scale_ref[:, pl.ds(src, cols)]
                u_ref[a * n:(a + 1) * n, k * cols:(k + 1) * cols] = u.astype(BF16)

    slots = most_slots(cnt_ref, (b0 + i) * nrb, nrb)

    def make(teacher):
        for cs0 in range(0, width, 256):
            cs = slice(cs0, cs0 + 256)
            for rb in range(nrb):
                rs = slice(rb * 128, (rb + 1) * 128)
                g = jnp.exp(z_ref[rs, cs] - c_ref[:, cs]) - teacher(rb, rs, cs)
                g_ref[rs, cs] = g.astype(BF16)

    @pl.when(slots <= FAST)
    def _():
        make(lambda rb, rs, cs: teacher_fast(tabr_ref, tabp_ref, rb, cs, 256))

    @pl.when(slots > FAST)
    def _():
        fill_teacher(cnt_ref, (b0 + i) * nrb, nrb, tabr_ref, tabp_ref, loc_hbm, pw_hbm, tm, loc_s, pw_s, sem)
        make(lambda rb, rs, cs: tm[rs, cs])

    acc = jnp.dot(gown_ref[...], u_ref[0:mine, :], preferred_element_type=F32)
    acc = acc + jnp.dot(g_ref[...], u_ref[mine:, :], preferred_element_type=F32)
    out_ref[...] = acc[:, :cols]
    part_ref[...] = acc[:, cols:]


def de_call(scal, cnt, y_all, xs, scale, z, c, gown, tables, half, vocab, b0, nb, prev):
    tabr, tabp, loc, pw = tables
    width, dim = z.shape[1], y_all.shape[1]
    mine = gown.shape[1]
    ccols = dim // xs
    cols = ccols // 2
    tot = half // VB
    trows = VB // 128 * 8
    anyspace = pl.BlockSpec(memory_space=pl.ANY)
    y_specs = [pl.BlockSpec((mine, ccols), functools.partial(lambda j, i, s, n: (lax.rem(s[2] + j, xs), s[2]), j))
               for j in range(xs)]
    in_specs = y_specs + [
        pl.BlockSpec((1, ccols), lambda i, s, n: (0, s[2])),
        pl.BlockSpec((VB, width), lambda i, s, n: (b0 + i, 0)),
        pl.BlockSpec((1, width), lambda i, s, n: (0, 0)),
        pl.BlockSpec((VB, mine), lambda i, s, n: (b0 + i, 0)),
        pl.BlockSpec((trows, width), lambda i, s, n: (b0 + i, 0)),
        pl.BlockSpec((trows, width), lambda i, s, n: (b0 + i, 0)),
        anyspace,
        anyspace,
    ]
    args = [y_all] * xs + [scale, z, c, gown, tabr, tabp, loc, pw]
    aliases = {}
    if prev is not None:
        aliases = {2 + len(args): 0}
        args.append(prev)
        in_specs.append(anyspace)
    return pl.pallas_call(
        functools.partial(de_kernel, b0, xs, prev is not None),
        out_shape=(jax.ShapeDtypeStruct((vocab, cols), F32), jax.ShapeDtypeStruct((nb * VB, cols), F32)),
        grid_spec=pltpu.PrefetchScalarGridSpec(
            num_scalar_prefetch=2,
            grid=(nb,),
            in_specs=in_specs,
            out_specs=(
                pl.BlockSpec((VB, cols), lambda i, s, n: (s[3] * tot + b0 + i, 0)),
                pl.BlockSpec((VB, cols), lambda i, s, n: (i, 0)),
            ),
            scratch_shapes=[
                pltpu.VMEM((width + mine, ccols), BF16),
                pltpu.VMEM((VB, width), BF16),
                pltpu.VMEM((VB, width), F32),
                pltpu.VMEM((loc.shape[0], 128), I32),
                pltpu.VMEM((loc.shape[0], 128), F32),
                pltpu.SemaphoreType.DMA((2,)),
            ],
        ),
        input_output_aliases=aliases,
        compiler_params=params(dimension_semantics=('arbitrary',)),
        cost_estimate=cost(3.0 * nb * VB * (width + mine) * ccols, nb * VB * (width * 4 + mine * 2 + ccols * 4), nb * VB * width),
    )(scal, cnt, *args)


def place_kernel(sc_ref, recv_ref, prev_ref, out_ref):
    out_ref[...] = recv_ref[...]


def place(scal, recv, out, half, row0):
    cols = out.shape[1]
    step = min(1024, recv.shape[0])
    return pl.pallas_call(
        place_kernel,
        out_shape=jax.ShapeDtypeStruct(out.shape, F32),
        grid_spec=pltpu.PrefetchScalarGridSpec(
            num_scalar_prefetch=1,
            grid=(recv.shape[0] // step,),
            in_specs=[pl.BlockSpec((step, cols), lambda i, s: (i, 0)), pl.BlockSpec(memory_space=pl.ANY)],
            out_specs=pl.BlockSpec((step, cols), lambda i, s: ((1 - s[3]) * (half // step) + row0 // step + i, 0)),
        ),
        input_output_aliases={2: 0},
        compiler_params=params(),
        cost_estimate=cost(1e8, recv.size * 8),
    )(scal, recv, out)


def solution(mesh):
    tps = mesh.shape['tp']
    xs = mesh.shape['dp'] // 2
    grid = Mesh(np.asarray(mesh.devices).reshape(tps, xs, 2), ('tp', 'x', 'core'))
    swap = [(0, 1), (1, 0)]
    everyone = ('x', 'core', 'tp')

    def local_head(hidden, embedding, norm_weight, teach_ids, teach_prob, tok_mask):
        vocab, dim = embedding.shape
        tok = hidden.shape[0]
        chip = 2 * tok
        top = teach_ids.shape[1]
        t, x, c = lax.axis_index('tp'), lax.axis_index('x'), lax.axis_index('core')
        half = -(-vocab // (2 * VB1)) * VB1
        nblk = half // 128
        part = tok // tps
        rows = jnp.where(c == 0, half, vocab - half)
        scal = jnp.stack([t * vocab + c * half, rows, x, c]).astype(I32)
        scale = (1.0 + norm_weight)[None, :]

        h_f32 = hidden.astype(F32)
        inv_rms = lax.rsqrt(jnp.mean(h_f32 * h_f32, axis=1, keepdims=True) + EPS_NORM)
        normed = h_f32 * inv_rms
        my_normed = lax.optimization_barrier(lax.dynamic_slice(normed, (t * part, 0), (part, dim)))
        y_all = lax.all_gather(my_normed, everyone, axis=0, tiled=True)
        y_part = lax.ppermute(normed, 'core', swap)
        lists = sort_lists(teach_ids, teach_prob, tok_mask)
        lists_part = lax.ppermute(lists, 'core', swap)
        lrows = 2 * top // tps
        lists_all = lax.all_gather(lax.dynamic_slice(lists, (t * lrows, 0), (lrows, tok)), everyone, axis=0, tiled=True)

        whole = pl.BlockSpec((tok, dim), lambda i, s: (0, 0))
        z0, m0, s0 = forward(scal, [normed, y_part], [whole, whole], scale, embedding, half, chip, True)
        chip_lists = jnp.where(c == 0, jnp.concatenate([lists, lists_part]), jnp.concatenate([lists_part, lists]))
        mask0 = (chip_lists.reshape(2, 2 * top, tok)[:, 0, :] > 0).astype(F32).reshape(1, chip)
        count = jnp.broadcast_to(jnp.sum(mask0), (1, 128))
        lse0, total = stats(m0, s0, count, tps, xs, 0)
        total = total[0, 0]

        def shift(lse, mask):
            weight = mask / total
            return weight, jnp.where(mask > 0, lse.reshape(1, -1) - jnp.log(weight), BIG)

        w0, c0 = shift(lse0, mask0)
        *tab0, cnt0, loc0, pw0 = expand(scal, chip_lists, w0, nblk, lambda g, s: (g // (tok // 128), g % (tok // 128)),
                                        chip // 128)
        cnt0 = jnp.max(cnt0.reshape(nblk, -1), axis=1)
        du, g0, tz = du_call(scal, cnt0, z0, c0, embedding, (*tab0, loc0, pw0), half)
        du_sum = lax.psum_scatter(du, ('core', 'tp'), scatter_dimension=0, tiled=True)

        y_specs = [pl.BlockSpec((chip, dim), functools.partial(lambda j, i, s: (lax.rem(s[2] + j, xs), 0), j))
                   for j in range(1, xs)]
        z1, m1, s1 = forward(scal, [y_all] * (xs - 1), y_specs, scale, embedding, half, (xs - 1) * chip, False)
        lse1, _ = stats(m1, s1, count, tps, xs, 1)
        signs = (lists_all.reshape(xs, 2, 2 * top, tok)[:, :, 0, :] > 0).astype(F32).reshape(xs, chip)
        order = lax.rem(x + jnp.arange(1, xs), xs)
        mask1 = signs[order].reshape(1, -1)
        w1, c1 = shift(lse1, mask1)
        tg = tok // 128

        def rest_map(g, s):
            return (lax.rem(s[2] + 1 + g // (2 * tg), xs) * 2 + lax.rem(g // tg, 2), lax.rem(g, tg))

        *tab1, cnt1, loc1, pw1 = expand(scal, lists_all, w1, nblk, rest_map, (xs - 1) * chip // 128)
        cnt1 = jnp.max(cnt1.reshape(nblk, -1), axis=1)

        d_normed = du_sum * scale
        d_rest = d_normed - my_normed * jnp.mean(d_normed * my_normed, axis=1, keepdims=True)
        d_all = lax.all_gather(d_rest, 'tp', axis=0, tiled=True)
        grad_hidden = (inv_rms * d_all).astype(BF16)
        tail = jnp.concatenate([jnp.sum(du_sum * my_normed, axis=0), jnp.broadcast_to(jnp.sum(tz), (128,))])
        tails = lax.all_gather(tail[None, :], everyone, axis=0, tiled=True)
        sums = jnp.sum(tails, axis=0)
        grad_norm = sums[:dim]
        log_sum = jnp.sum(w0.reshape(-1) * lse0.reshape(-1)) + jnp.sum(w1.reshape(-1) * lse1.reshape(-1))
        loss_mean = log_sum - sums[dim]

        tables = (*tab1, loc1, pw1)
        nb = half // VB
        n0 = nb // 2
        out, send0 = de_call(scal, cnt1, y_all, xs, scale, z1, c1, g0, tables, half, vocab, 0, n0, None)
        recv0 = lax.ppermute(send0, 'core', swap)
        out, send1 = de_call(scal, cnt1, y_all, xs, scale, z1, c1, g0, tables, half, vocab, n0, nb - n0, out)
        recv1 = lax.ppermute(send1, 'core', swap)
        out = place(scal, recv0, out, half, 0)
        out = place(scal, recv1, out, half, n0 * VB)
        return loss_mean, grad_hidden, out, grad_norm

    tokens = ('x', 'core')
    return jax.shard_map(
        local_head,
        mesh=grid,
        in_specs=(P(tokens, None), P('tp', None), P(None), P(tokens, None), P(tokens, None), P(tokens)),
        out_specs=(P(), P(tokens, None), P('tp', tokens), P(None)),
        check_vma=False,
    )
```

time: 3820 us -> 375 us (0.10); the launches traced: 3760 us -> 372 us
  local copies, waits for them, and re-layouts: 2330 us -> 9.86 us
  blocking collectives: 596 us -> 0 us
  other arithmetic: 382 us -> 21.9 us
  waiting for transfers between devices: 380 us -> 141 us
  Pallas kernels: 0 us -> 177 us
  matrix products: 60.3 us -> 0 us
    gather x3 -> x1, local copies, waits for them, and re-layouts: 2310 us -> 0.56 us  [local_head(): mask1 = signs[order].reshape(1, -1)]
    psum x3 -> x0, blocking collectives: 560 us -> none  [the longest x1 517 us: local_head(): lax.psum(jnp.stack([jnp.sum(shifted, axis=1), teach_part], axis=1), 'tp')]
    unnamed x7 -> x4, other arithmetic: 363 us -> 0.06 us
    pallas_call x0 -> x12, Pallas kernels: none -> 177 us  [the longest x2 61.2 us: forward(): pl.pallas_call(functools.partial(fwd_kernel, own), out_shape=(jax.ShapeDt...]
    reduce_scatter x1, waiting for transfers between devices: 235 us -> 77.8 us  [local_head(): lax.psum_scatter(du, ('core', 'tp'), scatter_dimension=0, tiled=True)]
    psum x1 -> x0, waiting for transfers between devices: 145 us -> none  [local_head(): lax.psum(jnp.dot(dlogit_bf, embedding, preferred_element_type=jnp.float32...]
    all_gather x0 -> x4, waiting for transfers between devices: none -> 61.9 us  [the longest x1 46.4 us: local_head(): y_all = lax.all_gather(my_normed, everyone, axis=0, tiled=True)]
    dot_general x3 -> x0, matrix products: 60.3 us -> none  [the longest x1 24.9 us: local_head(): lax.dot_general(dlogit_bf, normed_bf, (((0,), (0,)), ((), ())), preferred...]
  transfers between devices with their start and end apart: 2 -> 9, of which waited for: 2 -> 4; matrix products, arithmetic and copies ran while one was open for 1% -> 6% of each run, Pallas kernels for 0% -> 30%
where the time goes in v1:
time: 375 us; the launch traced here: 372 us
  Pallas kernels  177 us (47%)
  waiting for transfers between devices  141 us (38%)
  other arithmetic  21.9 us (6%)
  between operations  19.6 us (5%)
  local copies, waits for them, and re-layouts  9.86 us (3%)
    reduce_scatter x1, waiting for transfers between devices, local_head(): lax.psum_scatter(du, ('core', 'tp'), scatter_dimension=0, tiled=True)  77.8 us
    pallas_call x2, Pallas kernels, forward(): pl.pallas_call(functools.partial(fwd_kernel, own), out_shape=(jax.ShapeDt...  61.2 us
    all_gather x1, waiting for transfers between devices, local_head(): y_all = lax.all_gather(my_normed, everyone, axis=0, tiled=True)  46.4 us
    pallas_call x2, Pallas kernels, de_call(): pl.pallas_call(functools.partial(de_kernel, b0, xs, prev is not None), ou...  32 us
    pallas_call x2, Pallas kernels, stats(): pl.pallas_call(functools.partial(stats_kernel, tps, xs, groups), out_shap...  31.4 us
    pallas_call x2, Pallas kernels, expand(): pl.pallas_call(functools.partial(expand_kernel, nblk), out_shape=(fulli,...  21.7 us
    pallas_call x1, Pallas kernels, du_call(): pl.pallas_call(du_kernel, out_shape=(jax.ShapeDtypeStruct((width, dim), F...  19.7 us
    all_gather x1, waiting for transfers between devices, local_head(): d_all = lax.all_gather(d_rest, 'tp', axis=0, tiled=True)  15.4 us
  transfers between devices with their start and end apart: 9, of which 4 were waited for; matrix products, arithmetic and copies ran while one was open for 6% of the time, Pallas kernels for 30%

profile of v1, /device:TPU:1, one launch (start us, length us, event | category | flops | bytes accessed | tf_op | source)
XLA Modules:
  0.0 371.7 jit_solution(17212022327070851252)
XLA Ops:
  8.0 0.0 reduce-scatter.2.cloned.1.call-start
  8.0 1.5 fusion
  9.6 1.4 convert_multiply_fusion.refs_0_
  11.0 1.5 collective-permute-start.1
  12.5 4.2 %sort_lists.1 = f32[512,256]{1,0:T(8,128)} custom-call(s32[256,256]{1,0:T(8,128)} %ids_ref.1, f32[256,256]{1,0:T(8,128)} %pt_ref.1, f32[1,256]{1,0:T(1,128)} %bitcast.59), custom_call_target="tpu_custom_call" | custom-call | flops 4000000000 | bytes 1048576 | tf_op jit(solution)/shard_map/sort_lists/pallas_call | solution.py:81
  16.7 0.4 collective-permute-start
  17.1 0.6 pad_add_fusion.sc_ref
  17.7 0.6 broadcast_add_fusion
  18.3 0.7 collective-permute-done
  19.0 1.7 maximum_select_fusion.list_ref
  20.8 0.7 convert_reduce_fusion
  21.5 21.5 %shard_map.93 = (f32[4096,512]{1,0:T(8,128)}, f32[8,512]{1,0:T(8,128)}, f32[8,512]{1,0:T(8,128)}) custom-call(s32[4]{0:T(128)} %pad_add_fusion.sc_ref, f32[256,2048]{1,0:T(8,128)} %copy-done, f32[256,2048]{1,0:T(8,128)} %collective-permute-done.1.refs_1_, f32[1,2048]{1,0:T(1,128)} %bitcast.42, bf16[8016,2048]{1,0:T(8,128)(2,1)} %e_ref.1), custom_call_target="tpu_custom_call" | custom-call | flops 8589934592 | bytes 29360128 | tf_op jit(solution)/shard_map/pallas_call | solution.py:214
  43.0 1.2 broadcast_in_dim.26.add_ref
  44.2 15.6 %shard_map.94 = (f32[4,128]{1,0:T(4,128)}, f32[1,128]{1,0:T(1,128)}) custom-call(f32[8,512]{1,0:T(8,128)} %get-tuple-element.30.m_ref, f32[8,512]{1,0:T(8,128)} %get-tuple-element.31.s_ref, f32[1,128]{1,0:T(1,128)} %broadcast_in_dim.26.add_ref), custom_call_target="tpu_custom_call" | custom-call | flops 2000000000 | bytes 65536 | tf_op jit(solution)/shard_map/pallas_call | solution.py:309
  60.5 0.6 copy.18
  61.1 6.6 %shard_map.97 = (s32[256,512]{1,0:T(8,128)}, f32[256,512]{1,0:T(8,128)}, s32[256,512]{1,0:T(8,128)}, s32[256,512]{1,0:T(8,128)}, f32[256,512]{1,0:T(8,128)}) custom-call(s32[4]{0:T(128)} %pad_add_fusion.sc_ref, f32[1024,256]{1,0:T(8,128)} %copy-done.3, f32[1,512]{1,0:T(1,128)} %bitcast.53), custom_call_target="tpu_custom_call" | custom-call | flops 1600000000 | bytes 3670016 | tf_op jit(solution)/shard_map/pallas_call | solution.py:157
  67.7 1.2 reduce_max.23
  68.9 0.1 reduce_max.24
  68.9 0.6 reduce_max.25.cnt_ref
  69.6 0.6 subtract_select_fusion.c_ref
  70.2 19.7 %grad_u.1 = (f32[512,2048]{1,0:T(8,128)}, bf16[4096,512]{1,0:T(8,128)(2,1)}, f32[8,512]{1,0:T(8,128)}) custom-call(s32[4]{0:T(128)} %pad_add_fusion.sc_ref, s32[32]{0:T(128)} %reduce_max.25.cnt_ref, f32[4096,512]{1,0:T(8,128)} %get-tuple-element.38.z_ref, f32[1,512]{1,0:T(1,128)} %subtract_select_fusion.c_ref, bf16[8016,2048]{1,0:T(8,128)(2,1)} %e_ref.1, ...), custom_call_target="tpu_custom_call" | custom-call | flops 8589934592 | bytes 33554432 | tf_op jit(solution)/shard_map/grad_u/pallas_call | solution.py:435
  89.9 0.0 reduce-scatter.2.cloned.1.call-update
  90.0 0.0 all-gather.7.cloned.1.call-start
  90.0 1.4 constant_dynamic-slice_fusion.1
  91.4 0.0 all-gather.7.cloned.1.call-update
  91.4 0.0 all-gather.9.cloned.1.call-start
  91.5 1.6 constant_dynamic-slice_fusion
  93.1 0.0 all-gather.9.cloned.1.call-update
  93.1 0.0 all-gather.13.cloned.1.call-start
  93.1 0.6 reduce_sum.77
  93.8 77.8 %reduce-scatter.2.cloned.1.call-done = f32[16,2048]{1,0:T(8,128)} async-done(((f32[512,2048]{1,0:T(8,128)}), f32[16,2048]{1,0:T(8,128)}) %reduce-scatter.2.cloned.1.call-update) | async-done | bytes 131088 | tf_op jit(solution)/shard_map/reduce_scatter | solution.py:641
  171.6 1.1 multiply_reduce_fusion
  172.7 0.7 concatenate.11
  173.3 0.6 reshape.223
  173.9 0.0 all-gather.13.cloned.1.call-update
  174.0 0.2 all-gather.11.cloned.1.call-start
  174.2 0.0 all-gather.7.cloned.1.call-done.list_ref
  174.3 0.9 fusion.1
  175.2 0.6 gather_fusion
  175.8 0.6 copy.20
  176.4 15.2 %shard_map.98 = (s32[256,1536]{1,0:T(8,128)}, f32[256,1536]{1,0:T(8,128)}, s32[256,1536]{1,0:T(8,128)}, s32[256,1536]{1,0:T(8,128)}, f32[256,1536]{1,0:T(8,128)}) custom-call(s32[4]{0:T(128)} %pad_add_fusion.sc_ref, f32[4096,256]{1,0:T(8,128)} %all-gather.7.cloned.1.call-done.list_ref, f32[1,1536]{1,0:T(1,128)} %bitcast.48), custom_call_target="tpu_custom_call" | custom-call | flops 4800000000 | bytes 11010048 | tf_op jit(solution)/shard_map/pallas_call | solution.py:157
  191.6 1.6 reduce_max.29
  193.1 0.1 reduce_max.36
  193.2 0.6 reduce_max.37.cnt_ref
  193.9 0.7 multiply_subtract_fusion
  194.6 46.4 %all-gather.9.cloned.1.call-done.refs_0_.refs_1_.refs_2_.refs_3_ = f32[2048,2048]{1,0:T(8,128)} async-done(((f32[16,2048]{1,0:T(8,128)}), f32[2048,2048]{1,0:T(8,128)}) %all-gather.9.cloned.1.call-update) | async-done | bytes 16777232 | tf_op jit(solution)/shard_map/all_gather | solution.py:617
  241.1 39.7 %shard_map.95 = (f32[4096,1536]{1,0:T(8,128)}, f32[8,1536]{1,0:T(8,128)}, f32[8,1536]{1,0:T(8,128)}) custom-call(s32[4]{0:T(128)} %pad_add_fusion.sc_ref, f32[2048,2048]{1,0:T(8,128)} %all-gather.9.cloned.1.call-done.refs_0_.refs_1_.refs_2_.refs_3_, f32[2048,2048]{1,0:T(8,128)} %all-gather.9.cloned.1.call-done.refs_0_.refs_1_.refs_2_.refs_3_, ...), custom_call_target="tpu_custom_call" | custom-call | flops 25769803776 | bytes 54525952 | tf_op jit(solution)/shard_map/pallas_call | solution.py:214
  280.8 15.8 %shard_map.96 = (f32[12,128]{1,0:T(8,128)}, f32[1,128]{1,0:T(1,128)}) custom-call(f32[8,1536]{1,0:T(8,128)} %get-tuple-element.34.m_ref, f32[8,1536]{1,0:T(8,128)} %get-tuple-element.35.s_ref, f32[1,128]{1,0:T(1,128)} %broadcast_in_dim.26.add_ref), custom_call_target="tpu_custom_call" | custom-call | flops 2000000000 | bytes 65536 | tf_op jit(solution)/shard_map/pallas_call | solution.py:309
  296.6 1.3 fusion.2.refs_6_
  297.9 16.0 %shard_map.99 = (f32[8016,256]{1,0:T(8,128)}, f32[2048,256]{1,0:T(8,128)}) custom-call(s32[4]{0:T(128)} %pad_add_fusion.sc_ref, s32[32]{0:T(128)} %reduce_max.37.cnt_ref, f32[2048,2048]{1,0:T(8,128)} %all-gather.9.cloned.1.call-done.refs_0_.refs_1_.refs_2_.refs_3_, f32[2048,2048]{1,0:T(8,128)} %all-gather.9.cloned.1.call-done.refs_0_.refs_1_.refs_2_.refs_3_, ...), custom_call_target="tpu_custom_call" | custom-call | flops 6442450944 | bytes 18874368 | tf_op jit(solution)/shard_map/pallas_call | solution.py:545
  313.9 0.4 collective-permute-start.3
  314.3 16.0 %shard_map.100 = (f32[8016,256]{1,0:T(8,128)}, f32[2048,256]{1,0:T(8,128)}) custom-call(s32[4]{0:T(128)} %pad_add_fusion.sc_ref, s32[32]{0:T(128)} %reduce_max.37.cnt_ref, f32[2048,2048]{1,0:T(8,128)} %all-gather.9.cloned.1.call-done.refs_0_.refs_1_.refs_2_.refs_3_, ...), custom_call_target="tpu_custom_call", output_to_operand_aliasing={{0}: (14, {})} | custom-call | flops 6442450944 | bytes 18874368 | tf_op jit(solution)/shard_map/pallas_call | solution.py:545
  330.4 0.3 collective-permute-start.2
  330.7 0.6 multiply_reduce_fusion.3
  331.3 0.0 all-gather.13.cloned.1.call-done
  331.4 1.9 reduce_sum.78
  333.3 0.5 slice.24
  333.8 0.6 slice.25
  334.4 15.4 %all-gather.11.cloned.1.call-done = f32[256,2048]{1,0:T(8,128)} async-done(((f32[16,2048]{1,0:T(8,128)}), f32[256,2048]{1,0:T(8,128)}) %all-gather.11.cloned.1.call-update) | async-done | bytes 2097168 | tf_op jit(solution)/shard_map/all_gather | solution.py:661
  349.8 2.7 multiply_convert_fusion
  352.6 0.6 multiply_reduce_fusion.2
  355.0 1.3 copy-done.2
  356.3 3.3 shard_map.101.prev_ref
  359.6 3.3 shard_map.102
  (44 shorter events, 0.3 us)
Async XLA Ops:
  8.0 163.6 %reduce-scatter.2.cloned.1.call-start = ((), (), s32[]{:S(2)}) async-start(), calls=%async_computation.3 | async-start | bytes 4325376 | tf_op jit(solution)/shard_map/reduce_scatter | solution.py:641
  11.0 5.7 %copy-start = (f32[256,2048]{1,0:T(8,128)}, f32[256,2048]{1,0:T(8,128)S(1)}, u32[]{:S(2)}) copy-start(f32[256,2048]{1,0:T(8,128)S(1)} %convert_multiply_fusion.refs_0_) | copy-start | bytes 6291460
  11.0 10.5 %collective-permute-start.1 = (f32[256,2048]{1,0:T(8,128)S(1)}, f32[256,2048]{1,0:T(8,128)}, u32[]{:S(2)}, u32[]{:S(2)}) collective-permute-start(f32[256,2048]{1,0:T(8,128)S(1)} %convert_multiply_fusion.refs_0_), channel_id=1, source_target_pairs={{0,1},{1,0},{2,3},{3,2},{4,5},{5,4},{6,7},{7,6},{8,9},{9,8},{10,11... | collective-permute-start | bytes 6291464 | tf_op jit(solution)/shard_map/ppermute | solution.py:618
  12.5 5.2 %copy-start.9 = (f32[2048]{0:T(1024)S(1)}, f32[2048]{0:T(1024)}, u32[]{:S(2)}) copy-start(f32[2048]{0:T(1024)} %param.8) | copy-start | bytes 24580
  16.7 2.3 collective-permute-start
  20.7 22.3 %copy-start.3 = (f32[1024,256]{1,0:T(8,128)}, f32[1024,256]{1,0:T(8,128)S(1)}, u32[]{:S(2)}) copy-start(f32[1024,256]{1,0:T(8,128)S(1)} %maximum_select_fusion.list_ref) | copy-start | bytes 3145732
  61.1 8.5 %copy-start.10 = (f32[4,128]{1,0:T(4,128)S(1)}, f32[4,128]{1,0:T(4,128)}, u32[]{:S(2)}) copy-start(f32[4,128]{1,0:T(4,128)} %get-tuple-element.33) | copy-start | bytes 6148
  61.1 8.5 %copy-start.11 = (f32[1,1,2,256]{3,1,2,0:T(1,128)S(1)}, f32[1,1,2,256]{3,1,2,0:T(1,128)}, u32[]{:S(2)}) copy-start(f32[1,1,2,256]{3,1,2,0:T(1,128)} %copy.18) | copy-start | bytes 6148
  89.9 3.2 copy-start.8
  89.9 81.6 %copy-start.5 = (f32[2048]{0:T(1024)S(1)}, f32[2048]{0:T(1024)}, u32[]{:S(2)}) copy-start(f32[2048]{0:T(1024)} %broadcast_add_fusion) | copy-start | bytes 24580
  89.9 85.8 %copy-start.12 = (f32[1,128]{1,0:T(1,128)S(1)}, f32[1,128]{1,0:T(1,128)}, u32[]{:S(2)}) copy-start(f32[1,128]{1,0:T(1,128)} %get-tuple-element.32) | copy-start | bytes 1540
  90.0 84.3 %all-gather.7.cloned.1.call-start = ((), (), s32[]{:S(2)}) async-start(), calls=%async_computation.1 | async-start | bytes 4227072 | tf_op jit(solution)/shard_map/all_gather | solution.py:622
  91.4 149.6 %all-gather.9.cloned.1.call-start = ((), (), s32[]{:S(2)}) async-start(), calls=%async_computation.2 | async-start | bytes 16908288 | tf_op jit(solution)/shard_map/all_gather | solution.py:617
  93.1 238.3 %all-gather.13.cloned.1.call-start = ((), (), s32[]{:S(2)}) async-start(), calls=%async_computation.5 | async-start | bytes 1122816 | tf_op jit(solution)/shard_map/all_gather | solution.py:664
  174.0 175.9 %all-gather.11.cloned.1.call-start = ((), (), s32[]{:S(2)}) async-start(), calls=%async_computation.4 | async-start | bytes 2228224 | tf_op jit(solution)/shard_map/all_gather | solution.py:661
  176.4 17.5 %copy-start.1 = (f32[16,2048]{1,0:T(8,128)S(1)}, f32[16,2048]{1,0:T(8,128)}, u32[]{:S(2)}) copy-start(f32[16,2048]{1,0:T(8,128)} %constant_dynamic-slice_fusion) | copy-start | bytes 393220
  176.4 17.5 %copy-start.4 = (f32[16,2048]{1,0:T(8,128)S(1)}, f32[16,2048]{1,0:T(8,128)}, u32[]{:S(2)}) copy-start(f32[16,2048]{1,0:T(8,128)} %reduce-scatter.2.cloned.1.call-done) | copy-start | bytes 393220
  280.8 15.8 %copy-start.7 = (f32[1,1,3,512]{3,1,2,0:T(1,128)S(1)}, f32[1,1,3,512]{3,1,2,0:T(1,128)}, u32[]{:S(2)}) copy-start(f32[1,1,3,512]{3,1,2,0:T(1,128)} %copy.20) | copy-start | bytes 18436
  313.9 41.1 %collective-permute-start.3 = (f32[2048,256]{1,0:T(8,128)}, f32[2048,256]{1,0:T(8,128)S(1)}, u32[]{:S(2)}, u32[]{:S(2)}) collective-permute-start(f32[2048,256]{1,0:T(8,128)} %get-tuple-element.54), channel_id=1, source_target_pairs={{0,1},{1,0},{2,3},{3,2},{4,5},{5,4},{6,7},{7,6},{8,9},{9,8},{10,11... | collective-permute-start | bytes 6291464 | tf_op jit(solution)/shard_map/ppermute | solution.py:674
  330.4 29.3 %collective-permute-start.2 = (f32[2048,256]{1,0:T(8,128)}, f32[2048,256]{1,0:T(8,128)}, u32[]{:S(2)}, u32[]{:S(2)}) collective-permute-start(f32[2048,256]{1,0:T(8,128)} %get-tuple-element.53), channel_id=1, source_target_pairs={{0,1},{1,0},{2,3},{3,2},{4,5},{5,4},{6,7},{7,6},{8,9},{9,8},{10,11... | collective-permute-start | bytes 6291464 | tf_op jit(solution)/shard_map/ppermute | solution.py:676
  331.3 21.2 %copy-start.6 = (f32[12,128]{1,0:T(8,128)S(1)}, f32[12,128]{1,0:T(8,128)}, u32[]{:S(2)}) copy-start(f32[12,128]{1,0:T(8,128)} %get-tuple-element.36) | copy-start | bytes 18436
  355.0 1.3 copy-start.2
Sparse Core Ops, SparseCore 0:
  90.1 81.4 reduce-scatter.1
Sparse Core Ops, SparseCore 1:
  93.6 66.3 all-gather.6
  163.6 77.5 all-gather.8
  243.7 63.3 all-gather.12
  309.3 40.5 all-gather.10

commit v2 on v0

v2 whole, which is shorter than its diff:
```python
import functools

import jax
import jax.numpy as jnp
import numpy as np
from jax import lax
from jax.experimental import pallas as pl
from jax.experimental.pallas import tpu as pltpu
from jax.sharding import Mesh
from jax.sharding import PartitionSpec as P


EPS_NORM = 1e-6
NEG = -1e30
BIG = 1e30
F32, BF16, I32 = jnp.float32, jnp.bfloat16, jnp.int32
LANES, SUB = 128, 8
SLOTS = 8
FAST = 2
TILE = 256
WIDE = 512
VMEM_LIMIT = 60 * 1024 * 1024
MESH = pl.DeviceIdType.MESH
VMEM = pl.BlockSpec(memory_space=pltpu.VMEM)
ANY = pl.BlockSpec(memory_space=pl.ANY)


def params(**kw):
    return pltpu.CompilerParams(vmem_limit_bytes=VMEM_LIMIT, **kw)


def cost(flops, nbytes, trans=0):
    return pl.CostEstimate(flops=int(flops), bytes_accessed=int(nbytes), transcendentals=int(trans))


def shape(rows, cols, dtype=F32):
    return jax.ShapeDtypeStruct((rows, cols), dtype)


def fixed(rows, cols):
    return pl.BlockSpec((rows, cols), lambda *a: (0, 0))


def by_row(rows, cols):
    return pl.BlockSpec((rows, cols), lambda i: (i, 0))


def sub8(a):
    return slice(SUB * a, SUB * a + SUB)


def iota(rows, cols, axis=0):
    return lax.broadcasted_iota(I32, (rows, cols), axis)


def at(start, size):
    return pl.ds(pl.multiple_of(start, size), size)


def core_rows(vocab, half):
    return jnp.where(lax.axis_index('core') == 0, half, vocab - half)


def sort_kernel(vocab, whole, ids_ref, pt_ref, mask_ref, out_ref):
    n = ids_ref.shape[1]
    sub = iota(SUB, LANES)
    nv = n // SUB
    base = lax.axis_index('tp') * vocab
    for g in range(ids_ref.shape[0] // LANES):
        cols = slice(g * LANES, (g + 1) * LANES)
        order = ids_ref[cols, :] - base
        key = (jnp.where(order < 0, order + whole, order) + 1).astype(F32).T
        prob = pt_ref[cols, :].T
        k = [key[sub8(a), :] for a in range(nv)]
        p = [prob[sub8(a), :] for a in range(nv)]
        size = 2
        while size <= n:
            j = size // 2
            while j:
                if j >= SUB:
                    for a in range(nv):
                        if (SUB * a) & j:
                            continue
                        b = a + j // SUB
                        up = ((SUB * a) & size) == 0
                        swap = k[a] > k[b] if up else k[a] < k[b]
                        lo, hi = jnp.minimum(k[a], k[b]), jnp.maximum(k[a], k[b])
                        k[a], k[b] = (lo, hi) if up else (hi, lo)
                        p[a], p[b] = jnp.where(swap, p[b], p[a]), jnp.where(swap, p[a], p[b])
                else:
                    low = (sub & j) == 0
                    for a in range(nv):
                        if size >= SUB:
                            want_min = low if ((SUB * a) & size) == 0 else (sub & j) != 0
                        else:
                            want_min = low == ((sub & size) == 0)
                        ka = jnp.where(low, pltpu.roll(k[a], SUB - j, 0), pltpu.roll(k[a], j, 0))
                        pa = jnp.where(low, pltpu.roll(p[a], SUB - j, 0), pltpu.roll(p[a], j, 0))
                        new = jnp.where(want_min, jnp.minimum(k[a], ka), jnp.maximum(k[a], ka))
                        p[a] = jnp.where(new == ka, pa, p[a])
                        k[a] = new
                j //= 2
            size *= 2
        sign = jnp.where(mask_ref[:, cols] > 0, 1.0, -1.0)
        for a in range(nv):
            out_ref[sub8(a), cols] = k[a] * sign
            out_ref[sub8(nv + a), cols] = p[a]


def sort_lists(ids, prob, mask, vocab, whole):
    tokens, top = ids.shape
    return pl.pallas_call(
        functools.partial(sort_kernel, vocab, whole),
        out_shape=shape(2 * top, tokens),
        in_specs=[VMEM] * 3,
        out_specs=VMEM,
        compiler_params=params(),
        cost_estimate=cost(4e9, tokens * top * 16),
        name='sort_lists',
    )(ids, prob, mask[None, :])


def roll_all(x, op):
    for sh in (4, 2, 1):
        x = op(x, pltpu.roll(x, sh, 0))
    return x


def expand_kernel(vocab, half, plan, *refs):
    lists, (w_ref, tabr_ref, tabp_ref, cnt_ref, loc_ref, pw_ref, src) = refs[:-7], refs[-7:]
    g = pl.program_id(0)
    core = lax.axis_index('core')
    rows = core_rows(vocab, half)
    top = src.shape[0] // 2
    nq = top // SUB
    nblk = half // LANES
    sub = iota(SUB, LANES)

    which = plan(g, core)
    for a, ref in enumerate(lists):
        @pl.when(which == a)
        def _():
            src[...] = ref[...]

    w = w_ref[...]
    over = jnp.zeros((SUB, LANES), I32)
    used = jnp.zeros((SUB, LANES), I32)
    first = jnp.full((SUB, LANES), nq, I32)
    prev = None
    for q in range(nq):
        order = jnp.abs(src[sub8(q), :]).astype(I32) - 1 - core * half
        ok = (order >= 0) & (order < rows)
        loc = jnp.where(ok, order, -1)
        loc_ref[sub8(q), :] = loc
        pw_ref[sub8(q), :] = src[sub8(nq + q), :] * w
        used = jnp.where(ok, q + 1, used)
        first = jnp.minimum(first, jnp.where(ok, q, nq))
        blk = loc >> 7
        if prev is not None:
            over = jnp.where((blk == prev) & ok, 1, over)
        prev = blk
    over = roll_all(over, jnp.maximum)
    lo, hi = jnp.min(first), jnp.max(used)

    @pl.when(g == 0)
    def _():
        cnt_ref[...] = jnp.zeros(cnt_ref.shape, I32)

    def body(bt, carry):
        b0 = bt * SUB

        def scan(q, acc):
            accc, accp = list(acc[0]), list(acc[1])
            here = at(q * SUB, SUB)
            loc = loc_ref[here, :]
            blk = (loc >> 7) - b0
            code = (sub + SUB * q) * LANES + (loc & (LANES - 1))
            p = pw_ref[here, :]
            for i in range(SUB):
                m = blk == i
                accc[i] = jnp.where(m, code, accc[i])
                accp[i] = jnp.where(m, p, accp[i])
            return tuple(accc), tuple(accp)

        empty = ((jnp.full((SUB, LANES), -1, I32),) * SUB, (jnp.zeros((SUB, LANES), F32),) * SUB)
        accc, accp = lax.fori_loop(lo, hi, scan, empty)
        most = jnp.zeros((SUB, LANES), I32)
        for i in range(SUB):
            code, p = accc[i], accp[i]
            head = roll_all(jnp.where(code >= 0, code, top * LANES), jnp.minimum)
            start = (head >> 7) & (SUB - 1)
            for sh in (1, 2, 4):
                move = (start & sh) != 0
                code = jnp.where(move, pltpu.roll(code, SUB - sh, 0), code)
                p = jnp.where(move, pltpu.roll(p, SUB - sh, 0), p)
            full = roll_all(jnp.where(code >= 0, sub + 1, 0), jnp.maximum)
            most = jnp.where(sub == i, full, most)
            row = at((b0 + i) * SUB, SUB)
            tabr_ref[row, :] = jnp.where(code >= 0, code & (LANES - 1), -1)
            tabp_ref[row, :] = p
        most = jnp.where(over > 0, SLOTS + 1, most)
        tile = at(b0, SUB)
        cnt_ref[tile, :] = jnp.maximum(cnt_ref[tile, :], most)
        return carry

    lax.fori_loop(0, nblk // SUB, body, 0)


def expand_call(lists, plan, lane_block, weight, vocab, half):
    top = lists[0].shape[0] // 2
    groups = weight.shape[1] // LANES
    nblk = half // LANES
    width = groups * LANES

    def spec(rows):
        return pl.BlockSpec((rows, LANES), lambda g: (0, g))

    tabr, tabp, cnt, loc, pw = pl.pallas_call(
        functools.partial(expand_kernel, vocab, half, plan),
        out_shape=(shape(nblk * SLOTS, width, I32), shape(nblk * SLOTS, width), shape(nblk, LANES, I32),
                   shape(top, width, I32), shape(top, width)),
        grid=(groups,),
        in_specs=[pl.BlockSpec((2 * top, LANES), lambda g: (0, lane_block(g)))] * len(lists) + [spec(1)],
        out_specs=(spec(nblk * SLOTS), spec(nblk * SLOTS), fixed(nblk, LANES), spec(top), spec(top)),
        scratch_shapes=[pltpu.VMEM((2 * top, LANES), F32)],
        compiler_params=params(),
        cost_estimate=cost(groups * 1e8, 4 * width * (4 * top + 2 * nblk * SLOTS)),
    )(*lists, weight)
    return (tabr, tabp, loc, pw), jnp.max(cnt, axis=1)


def tp_peer(j, tps):
    return {'tp': lax.rem(lax.axis_index('tp') + j, tps)}


def reduce_start(tps, du_ref, recv, ssem, rsem):
    rows = recv.shape[1]
    t = lax.axis_index('tp')
    barrier = pltpu.get_barrier_semaphore()

    def hello(j, carry):
        pl.semaphore_signal(barrier, inc=1, device_id=tp_peer(j, tps), device_id_type=MESH)
        return carry

    lax.fori_loop(1, tps, hello, 0)
    pl.semaphore_wait(barrier, tps - 1)
    pltpu.make_async_copy(du_ref.at[at(t * rows, rows), :], recv.at[0], rsem.at[0]).start()

    def start(j, carry):
        reduce_copy(j, tps, du_ref, recv, ssem, rsem).start()
        return carry

    lax.fori_loop(1, tps, start, 0)


def reduce_copy(j, tps, du_ref, recv, ssem, rsem):
    rows = recv.shape[1]
    peer = lax.rem(lax.axis_index('tp') + j, tps)
    return pltpu.make_async_remote_copy(
        src_ref=du_ref.at[at(peer * rows, rows), :], dst_ref=recv.at[j], send_sem=ssem.at[j], recv_sem=rsem.at[j],
        device_id={'tp': peer}, device_id_type=MESH)


def reduce_finish(tps, du_ref, y_ref, scale_ref, recv, ssem, rsem, rest_ref, dw_ref):
    rows = recv.shape[1]
    t = lax.axis_index('tp')
    pltpu.make_async_copy(du_ref.at[at(t * rows, rows), :], recv.at[0], rsem.at[0]).wait()

    def finish(j, carry):
        reduce_copy(j, tps, du_ref, recv, ssem, rsem).wait()
        return carry

    lax.fori_loop(1, tps, finish, 0)
    du = jnp.sum(recv[...], axis=0)
    y = y_ref[...]
    dy = du * scale_ref[...]
    rest_ref[...] = dy - y * jnp.mean(dy * y, axis=1, keepdims=True)
    dw_ref[...] = jnp.sum(du * y, axis=0, keepdims=True)


def fwd_kernel(vocab, half, bases, tps, *refs):
    ny = 2 * len(bases)
    y_refs, refs = refs[:ny], refs[ny:]
    scale_ref, e_ref = refs[:2]
    if tps:
        du_ref, ysl_ref, z_ref, m_ref, s_ref, u_ref, rest_ref, dw_ref, ut_ref, recv, ssem, rsem = refs[2:]
    else:
        z_ref, m_ref, s_ref, u_ref, ut_ref = refs[2:]
    i = pl.program_id(0)
    x, core = lax.axis_index('x'), lax.axis_index('core')
    rows = core_rows(vocab, half)
    cols = u_ref.shape[1] // 2

    @pl.when(i == 0)
    def _():
        if tps:
            reduce_start(tps, du_ref, recv, ssem, rsem)
        for a, y_ref in enumerate(y_refs):
            n = y_ref.shape[0]
            slot = core if a % 2 == 0 else 1 - core
            dest = at(bases[a // 2] + slot * n, n)
            ut_ref[:, dest] = (y_ref[...] * scale_ref[...]).astype(BF16).T
            for k in range(2):
                mine = at((2 * x + (core if k == 0 else 1 - core)) * cols, cols)
                u_ref[dest, k * cols:(k + 1) * cols] = (y_ref[:, mine] * scale_ref[:, mine]).astype(BF16)
        m_ref[...] = jnp.full(m_ref.shape, NEG, F32)
        s_ref[...] = jnp.zeros(s_ref.shape, F32)

    vb = e_ref.shape[0]
    left = rows - i * vb
    for r0 in range(0, vb, TILE):
        rs = slice(r0, r0 + TILE)
        keep = iota(TILE, WIDE) < left - r0
        for c0 in range(0, ut_ref.shape[1], WIDE):
            cs = slice(c0, c0 + WIDE)
            z = jnp.dot(e_ref[rs, :], ut_ref[:, cs], preferred_element_type=F32)
            z = jnp.where(keep, z, NEG)
            z_ref[rs, cs] = z
            z3 = z.reshape(TILE // SUB, SUB, WIDE)
            old = m_ref[:, cs]
            new = jnp.maximum(old, jnp.max(z3, axis=0))
            m_ref[:, cs] = new
            s_ref[:, cs] = s_ref[:, cs] * jnp.exp(old - new) + jnp.sum(jnp.exp(z3 - new[None]), axis=0)

    if tps:
        @pl.when(i == pl.num_programs(0) - 1)
        def _():
            reduce_finish(tps, du_ref, ysl_ref, scale_ref, recv, ssem, rsem, rest_ref, dw_ref)


def forward(ys, scale, emb, half, vb, du=None, ysl=None, tps=0):
    vocab, dim = emb.shape
    nb = half // vb
    bases, width = [], 0
    for y in ys[::2]:
        bases.append(width)
        width += 2 * y.shape[0]
    ccols = dim // 4
    in_specs = [fixed(*y.shape) for y in ys]
    in_specs += [fixed(1, dim), pl.BlockSpec((vb, dim), lambda i: (lax.axis_index('core') * nb + i, 0))]
    args = [*ys, scale, emb]
    out_shape = [shape(half, width), shape(SUB, width), shape(SUB, width), shape(width, ccols, BF16)]
    out_specs = [by_row(vb, width), fixed(SUB, width), fixed(SUB, width), fixed(width, ccols)]
    scratch = [pltpu.VMEM((dim, width), BF16)]
    more = {}
    if tps:
        part = ysl.shape[0]
        in_specs += [ANY, fixed(part, dim)]
        args += [du, ysl]
        out_shape += [shape(part, dim), shape(1, dim)]
        out_specs += [fixed(part, dim), fixed(1, dim)]
        scratch += [pltpu.VMEM((tps, part, dim), F32), pltpu.SemaphoreType.DMA((tps,)), pltpu.SemaphoreType.DMA((tps,))]
        more = dict(collective_id=3, has_side_effects=True)
    return pl.pallas_call(
        functools.partial(fwd_kernel, vocab, half, tuple(bases), tps),
        out_shape=out_shape,
        grid=(nb,),
        in_specs=in_specs,
        out_specs=out_specs,
        scratch_shapes=scratch,
        compiler_params=params(dimension_semantics=('arbitrary',), **more),
        cost_estimate=cost(2.0 * half * width * dim, half * dim * 2 + half * width * 4 + width * dim * 4, half * width),
    )(*args)


def pieces(x):
    return [x[:, g * LANES:(g + 1) * LANES] for g in range(x.shape[1] // LANES)]


def put_rows(ref, base, x):
    for g, piece in enumerate(pieces(x)):
        ref[base + g:base + g + 1, :] = piece


def stats_kernel(tps, xs, order, own, *refs):
    nlist = 2 * len(order)
    lists, refs = refs[:nlist], refs[nlist:]
    nstat = 2 if own else 4
    stat, refs = refs[:nstat], refs[nstat:]
    nadd = 0 if own else 3
    adds, refs = refs[:nadd], refs[nadd:]
    c_ref, w_ref, loss_ref, sums_ref, send, recv, xsend, xrecv, tsend, trecv, ssem, rsem, xssem, xrsem, tssem, trsem = refs
    t, x, core = lax.axis_index('tp'), lax.axis_index('x'), lax.axis_index('core')
    me = t * 2 + core
    peers = tps * 2
    near = xs * 2
    here = x * 2 + core
    gr = send.shape[0] // 2

    base = 0
    send[...] = jnp.zeros(send.shape, F32)
    for m_ref, s_ref in zip(stat[::2], stat[1::2]):
        m = jnp.max(m_ref[...], axis=0, keepdims=True)
        s = jnp.sum(s_ref[...] * jnp.exp(m_ref[...] - m), axis=0, keepdims=True)
        put_rows(send, base, m)
        put_rows(send, gr + base, s)
        base += m.shape[1] // LANES
    masks = []
    for (chip, lanes) in order_list(order):
        a, b = (ref[0:1, lanes] for ref in lists[2 * chip:2 * chip + 2])
        masks += [jnp.where(core == 0, a, b), jnp.where(core == 0, b, a)]
    mask = (jnp.concatenate(masks, axis=1) > 0).astype(F32)
    xsend[...] = jnp.zeros(xsend.shape, F32)
    if own:
        put_rows(xsend, 0, mask)
    else:
        put_rows(xsend, 0, adds[0][...])
        tz = jnp.sum(adds[1][...], axis=0, keepdims=True)
        xsend[xsend.shape[0] - SUB:xsend.shape[0] - SUB + 1, :] = functools.reduce(jnp.add, pieces(tz))

    barrier = pltpu.get_barrier_semaphore()

    def peer(j):
        r = lax.rem(me + j, peers)
        return {'tp': r // 2, 'core': lax.rem(r, 2)}

    def xpeer(j):
        r = lax.rem(here + j, near)
        return {'x': r // 2, 'core': lax.rem(r, 2)}

    def signal(to):
        def run(j, carry):
            pl.semaphore_signal(barrier, inc=1, device_id=to(j), device_id_type=MESH)
            return carry

        return run

    lax.fori_loop(1, peers, signal(peer), 0)
    lax.fori_loop(1, near, signal(xpeer), 0)
    pl.semaphore_wait(barrier, peers + near - 2)

    def copies(src, dst, s, r, to):
        def make(j):
            return pltpu.make_async_remote_copy(
                src_ref=src, dst_ref=dst.at[j], send_sem=s.at[j], recv_sem=r.at[j], device_id=to(j), device_id_type=MESH)

        def start(j, carry):
            make(j).start()
            return carry

        def wait(j, carry):
            make(j).wait()
            return carry

        return start, wait

    start, wait = copies(send, recv, ssem, rsem, peer)
    xstart, xwait = copies(xsend, xrecv, xssem, xrsem, xpeer)
    lax.fori_loop(1, near, xstart, 0)
    lax.fori_loop(1, peers, start, 0)
    lax.fori_loop(1, near, xwait, 0)
    total = xsend[...] + jnp.sum(xrecv[1:], axis=0)
    if not own:
        tsend[...] = total
        tstart, twait = copies(tsend, trecv, tssem, trsem, functools.partial(tp_peer, tps=tps))
        lax.fori_loop(1, tps, tstart, 0)
    lax.fori_loop(1, peers, wait, 0)
    mine, theirs = send[0:gr, :], recv[1:, 0:gr, :]
    best = jnp.maximum(mine, jnp.max(theirs, axis=0))
    acc = send[gr:, :] * jnp.exp(mine - best) + jnp.sum(recv[1:, gr:, :] * jnp.exp(theirs - best[None]), axis=0)
    lse = best + jnp.log(acc)
    lse = jnp.concatenate([lse[g:g + 1, :] for g in range(mask.shape[1] // LANES)], axis=1)
    if own:
        count = jnp.broadcast_to(jnp.sum(total, keepdims=True) / 2, (1, LANES))
        sums_ref[...] = count
    else:
        count = adds[2][...]
    w = mask / count[:, 0:1]
    w_ref[...] = w
    c_ref[...] = jnp.where(mask > 0, lse - jnp.log(w), BIG)
    loss_ref[...] = functools.reduce(jnp.add, pieces(w * lse))
    if not own:
        lax.fori_loop(1, tps, twait, 0)
        sums_ref[...] = tsend[...] + jnp.sum(trecv[1:], axis=0)


def order_list(order):
    return [(chip, lanes) for chip, cuts in enumerate(order) for lanes in cuts]


def stats(lists, order, stat, adds, tps, xs, cid):
    own = not adds
    width = sum(m.shape[1] for m in stat[::2])
    tok = lists[0].shape[1]
    gr = -(-width // (LANES * SUB)) * SUB
    xr = SUB if own else adds[0].shape[1] // LANES + SUB
    dma = pltpu.SemaphoreType.DMA
    return pl.pallas_call(
        functools.partial(stats_kernel, tps, xs, order, own),
        out_shape=(shape(1, width), shape(1, width), shape(1, LANES), shape(1 if own else xr, LANES)),
        grid=(1,),
        in_specs=[fixed(SUB, tok)] * len(lists) + [fixed(*a.shape) for a in (*stat, *adds)],
        out_specs=(fixed(1, width), fixed(1, width), fixed(1, LANES), fixed(1 if own else xr, LANES)),
        scratch_shapes=[
            pltpu.VMEM((2 * gr, LANES), F32),
            pltpu.VMEM((2 * tps, 2 * gr, LANES), F32),
            pltpu.VMEM((xr, LANES), F32),
            pltpu.VMEM((2 * xs, xr, LANES), F32),
            pltpu.VMEM((xr, LANES), F32),
            pltpu.VMEM((tps, xr, LANES), F32),
            dma((2 * tps,)), dma((2 * tps,)), dma((2 * xs,)), dma((2 * xs,)), dma((tps,)), dma((tps,)),
        ],
        compiler_params=params(collective_id=cid, has_side_effects=True),
        cost_estimate=cost(2e9, 1 << 16),
    )(*lists, *stat, *adds)


def fill_teacher(cnt_ref, first, nrb, tabr_ref, tabp_ref, loc_hbm, pw_hbm, tm, loc_s, pw_s, sem):
    width = tm.shape[1]
    rows = iota(LANES, LANES)
    zero = jnp.zeros((LANES, LANES), F32)

    def pick(row, val, t):
        for s in range(SUB):
            t = jnp.where(rows == row[s:s + 1, :], val[s:s + 1, :], t)
        return t

    for rb in range(nrb):
        n = cnt_ref[first + rb]
        rs = slice(rb * LANES, (rb + 1) * LANES)

        def tile(g, carry):
            lanes = at(g * LANES, LANES)

            @pl.when(n <= SLOTS)
            def _():
                tm[rs, lanes] = pick(tabr_ref[sub8(rb), lanes], tabp_ref[sub8(rb), lanes], zero)

            @pl.when(n > SLOTS)
            def _():
                a = pltpu.make_async_copy(loc_hbm.at[:, lanes], loc_s, sem.at[0])
                b = pltpu.make_async_copy(pw_hbm.at[:, lanes], pw_s, sem.at[1])
                a.start()
                b.start()
                a.wait()
                b.wait()
                base = (first + rb) * LANES

                def entries(k, t):
                    here = at(k * SUB, SUB)
                    return pick(loc_s[here, :] - base, pw_s[here, :], t)

                tm[rs, lanes] = lax.fori_loop(0, loc_s.shape[0] // SUB, entries, zero)

            return carry

        lax.fori_loop(0, width // LANES, tile, 0)


def teacher_fast(tabr_ref, tabp_ref, rb, cs):
    rows = iota(LANES, TILE)
    t = jnp.zeros((LANES, TILE), F32)
    for s in range(SUB * rb, SUB * rb + FAST):
        t = jnp.where(rows == tabr_ref[s:s + 1, cs], tabp_ref[s:s + 1, cs], t)
    return t


def most_slots(cnt_ref, first, nrb):
    n = cnt_ref[first]
    for rb in range(1, nrb):
        n = jnp.maximum(n, cnt_ref[first + rb])
    return n


def fill_scratch(vb, width, top):
    return [pltpu.VMEM((vb, width), F32), pltpu.VMEM((top, LANES), I32), pltpu.VMEM((top, LANES), F32),
            pltpu.SemaphoreType.DMA((2,))]


def g_kernel(cnt_ref, z_ref, c_ref, tabr_ref, tabp_ref, loc_hbm, pw_hbm, g_ref, gt_ref, tz_ref, *fill):
    i = pl.program_id(0)
    vb, width = z_ref.shape
    nrb = vb // LANES

    @pl.when(i == 0)
    def _():
        tz_ref[...] = jnp.zeros(tz_ref.shape, F32)

    slots = most_slots(cnt_ref, i * nrb, nrb)

    def make(teacher):
        for c0 in range(0, width, TILE):
            cs = slice(c0, c0 + TILE)
            tz = jnp.zeros((SUB, TILE), F32)
            for rb in range(nrb):
                rs = slice(rb * LANES, (rb + 1) * LANES)
                z = z_ref[rs, cs]
                t = teacher(rb, rs, cs)
                g = (jnp.exp(z - c_ref[:, cs]) - t).astype(BF16)
                g_ref[rs, cs] = g
                gt_ref[cs, rs] = g.T
                tz = tz + jnp.sum((t * z).reshape(LANES // SUB, SUB, TILE), axis=0)
            tz_ref[:, cs] += tz

    @pl.when(slots <= FAST)
    def _():
        make(lambda rb, rs, cs: teacher_fast(tabr_ref, tabp_ref, rb, cs))

    @pl.when(slots > FAST)
    def _():
        fill_teacher(cnt_ref, i * nrb, nrb, tabr_ref, tabp_ref, loc_hbm, pw_hbm, *fill)
        make(lambda rb, rs, cs: fill[0][rs, cs])


def g_own(cnt, z, c, tables):
    half, width = z.shape
    vb = WIDE
    trows = vb // LANES * SLOTS

    def row(i, n):
        return (i, 0)

    return pl.pallas_call(
        g_kernel,
        out_shape=(shape(half, width, BF16), shape(width, half, BF16), shape(SUB, width)),
        grid_spec=pltpu.PrefetchScalarGridSpec(
            num_scalar_prefetch=1,
            grid=(half // vb,),
            in_specs=[pl.BlockSpec((vb, width), row), fixed(1, width), pl.BlockSpec((trows, width), row),
                      pl.BlockSpec((trows, width), row), ANY, ANY],
            out_specs=(pl.BlockSpec((vb, width), row), pl.BlockSpec((width, vb), lambda i, n: (0, i)), fixed(SUB, width)),
            scratch_shapes=fill_scratch(vb, width, tables[2].shape[0]),
        ),
        compiler_params=params(dimension_semantics=('arbitrary',)),
        cost_estimate=cost(4e9, half * width * 8, half * width),
        name='g_own',
    )(cnt, z, c, *tables)


def du_kernel(vocab, half, gt_ref, e_ref, out_ref, mine, send, recv, ssem, rsem):
    i = pl.program_id(0)
    core = lax.axis_index('core')
    rows = core_rows(vocab, half)
    tok = out_ref.shape[0]
    tiles = pl.num_programs(0) - 2
    cut = (vocab - half) // TILE * TILE

    @pl.when(i == 0)
    def _():
        barrier = pltpu.get_barrier_semaphore()
        pl.semaphore_signal(barrier, inc=1, device_id={'core': 1 - core}, device_id_type=MESH)
        pl.semaphore_wait(barrier, 1)

    def copy(k):
        return pltpu.make_async_remote_copy(
            src_ref=send.at[k], dst_ref=recv.at[k], send_sem=ssem.at[k], recv_sem=rsem.at[k],
            device_id={'core': 1 - core}, device_id_type=MESH)

    @pl.when((i >= 1) & (i <= tiles))
    def _():
        copy(i - 1).start()

    @pl.when(i < tiles)
    def _():
        tail = e_ref[cut:, :]
        tail = jnp.where(iota(*tail.shape) < rows - cut, tail, jnp.zeros((), BF16))

        def part(which):
            g = gt_ref[at(which * tok, tok), :]
            return (jnp.dot(g[:, :cut], e_ref[:cut, :], preferred_element_type=F32)
                    + jnp.dot(g[:, cut:], tail, preferred_element_type=F32))

        send[i] = part(1 - core)
        mine[i] = part(core)

    @pl.when(i >= 2)
    def _():
        copy(i - 2).wait()
        out_ref[...] = mine[i - 2] + recv[i - 2]


def du_call(gt, emb, half):
    vocab, dim = emb.shape
    tok = gt.shape[0] // 2
    tiles = dim // WIDE
    buf = pltpu.VMEM((tiles, tok, WIDE), F32)
    dma = pltpu.SemaphoreType.DMA((tiles,))
    return pl.pallas_call(
        functools.partial(du_kernel, vocab, half),
        out_shape=shape(tok, dim),
        grid=(tiles + 2,),
        in_specs=[fixed(*gt.shape),
                  pl.BlockSpec((half, WIDE), lambda i: (lax.axis_index('core'), jnp.minimum(i, tiles - 1)))],
        out_specs=pl.BlockSpec((tok, WIDE), lambda i: (0, jnp.maximum(i - 2, 0))),
        scratch_shapes=[buf, buf, buf, dma, dma],
        compiler_params=params(dimension_semantics=('arbitrary',), collective_id=2, has_side_effects=True),
        cost_estimate=cost(4.0 * half * tok * dim, half * dim * 2),
        name='grad_u',
    )(gt, emb)


def de_kernel(b0, refs_y, cnt_ref, *refs):
    u_refs, refs = refs[:refs_y], refs[refs_y:]
    zn_ref, zf_ref, gown_ref, c_ref, tabr_ref, tabp_ref, loc_hbm, pw_hbm = refs[:8]
    out_ref, part_ref, u_ref, g_ref, *fill = refs[-8:]
    i = pl.program_id(0)
    vb, mine = gown_ref.shape
    cols = out_ref.shape[1]
    nrb = vb // LANES
    first = (b0 + jnp.minimum(i, pl.num_programs(0) - 2)) * nrb

    @pl.when(i == 0)
    def _():
        base = 0
        for ref in u_refs:
            u_ref[base:base + ref.shape[0], :] = ref[...]
            base += ref.shape[0]

    def make(p, teacher):
        g_ref[p, :, 0:mine] = gown_ref[...]
        c0 = 0
        for z_ref in (zn_ref, zf_ref):
            for l0 in range(0, z_ref.shape[1], TILE):
                cs = slice(c0, c0 + TILE)
                for rb in range(nrb):
                    rs = slice(rb * LANES, (rb + 1) * LANES)
                    g = jnp.exp(z_ref[rs, l0:l0 + TILE] - c_ref[:, cs]) - teacher(rb, rs, cs)
                    g_ref[p, rs, mine + c0:mine + c0 + TILE] = g.astype(BF16)
                c0 += TILE

    for p in range(2):
        @pl.when(lax.rem(i, 2) == p)
        def _():
            make(p, lambda rb, rs, cs: teacher_fast(tabr_ref, tabp_ref, rb, cs))
            acc = jnp.dot(g_ref[1 - p], u_ref[...], preferred_element_type=F32)
            out_ref[...] = acc[:, :cols]
            part_ref[...] = acc[:, cols:]

    @pl.when(most_slots(cnt_ref, first, nrb) > FAST)
    def _():
        fill_teacher(cnt_ref, first, nrb, tabr_ref, tabp_ref, loc_hbm, pw_hbm, *fill)
        for p in range(2):
            @pl.when(lax.rem(i, 2) == p)
            def _():
                make(p, lambda rb, rs, cs: fill[0][rs, cs])


def de_call(cnt, us, zn, zf, gown, c, tables, vocab, b0, nb, prev):
    half, mine = gown.shape
    ccols = us[0].shape[1]
    cols = ccols // 2
    tot = half // TILE
    width = zn.shape[1] + zf.shape[1]
    trows = TILE // LANES * SLOTS

    def rows(cols_, height=TILE):
        return pl.BlockSpec((height, cols_), lambda i, n: (b0 + jnp.minimum(i, nb - 1), 0))

    in_specs = [fixed(*u.shape) for u in us]
    in_specs += [rows(zn.shape[1]), rows(zf.shape[1]), rows(mine), fixed(1, width), rows(width, trows), rows(width, trows),
                 ANY, ANY]
    args = [*us, zn, zf, gown, c, *tables]
    aliases = {}
    if prev is not None:
        aliases = {1 + len(args): 0}
        args.append(prev)
        in_specs.append(ANY)
    return pl.pallas_call(
        functools.partial(de_kernel, b0, len(us)),
        out_shape=(shape(vocab, cols), shape(nb * TILE, cols)),
        grid_spec=pltpu.PrefetchScalarGridSpec(
            num_scalar_prefetch=1,
            grid=(nb + 1,),
            in_specs=in_specs,
            out_specs=(
                pl.BlockSpec((TILE, cols), lambda i, n: (lax.axis_index('core') * tot + b0 + jnp.maximum(i - 1, 0), 0)),
                pl.BlockSpec((TILE, cols), lambda i, n: (jnp.maximum(i - 1, 0), 0)),
            ),
            scratch_shapes=[pltpu.VMEM((width + mine, ccols), BF16), pltpu.VMEM((2, TILE, width + mine), BF16),
                            *fill_scratch(TILE, width, tables[2].shape[0])],
        ),
        input_output_aliases=aliases,
        compiler_params=params(dimension_semantics=('arbitrary',)),
        cost_estimate=cost(3.0 * nb * TILE * (width + mine) * ccols, nb * TILE * (width * 4 + mine * 2 + ccols * 4),
                           nb * TILE * width),
    )(cnt, *args)


def place_kernel(recv_ref, prev_ref, out_ref):
    out_ref[...] = recv_ref[...]


def place(recv, out, half, row0):
    cols = out.shape[1]
    step = 2 * WIDE
    return pl.pallas_call(
        place_kernel,
        out_shape=shape(*out.shape),
        grid=(recv.shape[0] // step,),
        in_specs=[by_row(step, cols), ANY],
        out_specs=pl.BlockSpec(
            (step, cols), lambda i: ((1 - lax.axis_index('core')) * (half // step) + row0 // step + i, 0)),
        input_output_aliases={1: 0},
        compiler_params=params(),
        cost_estimate=cost(1e8, recv.size * 8),
    )(recv, out)


def dh_kernel(tps, *refs):
    parts, (inv_ref, out_ref) = refs[:tps], refs[tps:]
    t = lax.axis_index('tp')
    for j, ref in enumerate(parts):
        rows = ref.shape[0]
        here = at(lax.rem(t - j + tps, tps) * rows, rows)
        out_ref[here, :] = (inv_ref[here, :] * ref[...]).astype(BF16)


def dh_call(parts, inv):
    tps = len(parts)
    part, dim = parts[0].shape
    return pl.pallas_call(
        functools.partial(dh_kernel, tps),
        out_shape=shape(part * tps, dim, BF16),
        in_specs=[VMEM] * (tps + 1),
        out_specs=VMEM,
        compiler_params=params(),
        cost_estimate=cost(1e8, part * tps * dim * 6),
        name='grad_h',
    )(*parts, inv)


def solution(mesh):
    tps = mesh.shape['tp']
    xs = mesh.shape['dp'] // 2
    grid = Mesh(np.asarray(mesh.devices).reshape(tps, xs, 2), ('tp', 'x', 'core'))

    def shift(x, axis, by):
        n = grid.shape[axis]
        return lax.ppermute(x, axis, [(i, (i + by) % n) for i in range(n)])

    def both(x):
        return [x, shift(x, 'core', 1)]

    def local_head(hidden, embedding, norm_weight, teach_ids, teach_prob, tok_mask):
        vocab, dim = embedding.shape
        tok = hidden.shape[0]
        half = -(-vocab // (2 * WIDE)) * WIDE
        part = tok // tps
        cut = tok // 2
        scale = (1.0 + norm_weight)[None, :]

        h_f32 = hidden.astype(F32)
        inv_rms = lax.rsqrt(jnp.mean(h_f32 * h_f32, axis=1, keepdims=True) + EPS_NORM)
        normed = lax.optimization_barrier(h_f32 * inv_rms)
        left = shift(normed, 'x', 1)
        right = shift(normed, 'x', -1)
        y_own = both(normed)
        lists = sort_lists(teach_ids, teach_prob, tok_mask, vocab, vocab * tps)
        l_own = both(lists)

        z0, m0, s0, u0 = forward(y_own, scale, embedding, half, 2 * WIDE)
        full = slice(0, tok)
        lo, hi = slice(0, cut), slice(cut, tok)
        c0, w0, loss0, count = stats(l_own, ((full,),), (m0, s0), (), tps, xs, 0)
        tg = tok // LANES
        tab0, cnt0 = expand_call(l_own, lambda g, c: lax.rem(g // tg + c, 2), lambda g: lax.rem(g, tg),
                                 w0, vocab, half)
        g0, gt0, tz = g_own(cnt0, z0, c0, tab0)
        du = du_call(gt0, embedding, half)

        far0 = shift(left[:cut], 'x', 1)
        far1 = shift(right[cut:], 'x', -1)
        l_left = shift(lists, 'x', 1)
        l_right = shift(lists, 'x', -1)
        l_far = shift(l_left, 'x', 1)
        y_near = both(left) + both(right)
        y_far = both(far0) + both(far1)
        l_rest = both(l_left) + both(l_right) + both(l_far)
        my_normed = lax.dynamic_slice(normed, (lax.axis_index('tp') * part, 0), (part, dim))
        z1, m1, s1, u1, d_rest, dw = forward(y_near, scale, embedding, half, WIDE, du, my_normed, tps)
        d_parts = [d_rest] + [shift(d_rest, 'tp', j) for j in range(1, tps)]
        z2, m2, s2, u2 = forward(y_far, scale, embedding, half, 2 * WIDE)
        c1, w1, loss1, sums = stats(l_rest, ((full,), (full,), (lo, hi)), (m1, s1, m2, s2), (dw, tz, count),
                                    tps, xs, 1)

        def plan(g, c):
            far = g // (2 * tg) == 2
            swap = jnp.where(far, lax.rem(g, 2), lax.rem(g // tg, 2))
            return g // (2 * tg) * 2 + lax.rem(swap + c, 2)

        def lane_block(g):
            return jnp.where(g // (2 * tg) == 2, lax.rem(g // 2, tg), lax.rem(g, tg))

        tab1, cnt1 = expand_call(l_rest, plan, lane_block, w1, vocab, half)

        grad_norm = sums[:dim // LANES].reshape(dim)
        loss_mean = jnp.sum(loss0) + jnp.sum(loss1) - jnp.sum(sums[dim // LANES])

        us = [u0, u1, u2]
        nb = half // TILE
        n0 = nb // 2
        out, send0 = de_call(cnt1, us, z1, z2, g0, c1, tab1, vocab, 0, n0, None)
        recv0 = shift(send0, 'core', 1)
        out, send1 = de_call(cnt1, us, z1, z2, g0, c1, tab1, vocab, n0, nb - n0, out)
        recv1 = shift(send1, 'core', 1)
        grad_hidden = dh_call(d_parts, inv_rms)
        out = place(recv0, out, half, 0)
        out = place(recv1, out, half, n0 * TILE)
        return loss_mean, grad_hidden, out, grad_norm

    tokens = ('x', 'core')
    return jax.shard_map(
        local_head,
        mesh=grid,
        in_specs=(P(tokens, None), P('tp', None), P(None), P(tokens, None), P(tokens, None), P(tokens)),
        out_specs=(P(), P(tokens, None), P('tp', tokens), P(None)),
        check_vma=False,
    )
```

time: 3820 us -> 349 us (0.09); the launches traced: 3760 us -> 345 us
  local copies, waits for them, and re-layouts: 2330 us -> 9.38 us
  blocking collectives: 596 us -> 0 us
  other arithmetic: 382 us -> 9.29 us
  waiting for transfers between devices: 380 us -> 66.6 us
  Pallas kernels: 0 us -> 219 us
  matrix products: 60.3 us -> 0 us
    gather x3 -> x0, local copies, waits for them, and re-layouts: 2310 us -> none  [local_head(): picked = jnp.take_along_axis(logits, safe_ids, axis=1)]
    psum x3 -> x0, blocking collectives: 560 us -> none  [the longest x1 517 us: local_head(): lax.psum(jnp.stack([jnp.sum(shifted, axis=1), teach_part], axis=1), 'tp')]
    unnamed x7 -> x0, other arithmetic: 363 us -> none
    reduce_scatter x1 -> x0, waiting for transfers between devices: 235 us -> none  [local_head(): lax.psum_scatter(embed_part, 'dp', scatter_dimension=1, tiled=True)]
    pallas_call x0 -> x15, Pallas kernels: none -> 219 us  [the longest x3 76.5 us: forward(): pl.pallas_call(functools.partial(fwd_kernel, vocab, half, tuple(bases), t...]
    psum x1 -> x0, waiting for transfers between devices: 145 us -> none  [local_head(): lax.psum(jnp.dot(dlogit_bf, embedding, preferred_element_type=jnp.float32...]
    ppermute x0 -> x33, waiting for transfers between devices: none -> 66.6 us  [shift(): return lax.ppermute(x, axis, [(i, (i + by) % n) for i in range(n)])]
    dot_general x3 -> x0, matrix products: 60.3 us -> none  [the longest x1 24.9 us: local_head(): lax.dot_general(dlogit_bf, normed_bf, (((0,), (0,)), ((), ())), preferred...]
  transfers between devices with their start and end apart: 2 -> 33, of which waited for: 2 -> 11; matrix products, arithmetic and copies ran while one was open for 1% -> 3% of each run, Pallas kernels for 0% -> 48%
where the time goes in v2:
time: 349 us; the launch traced here: 345 us
  Pallas kernels  219 us (63%)
  waiting for transfers between devices  66.6 us (19%)
  starting transfers between devices  36.2 us (10%)
  local copies, waits for them, and re-layouts  9.38 us (3%)
  other arithmetic  9.29 us (3%)
  between operations  4.09 us (1%)
    pallas_call x3, Pallas kernels, forward(): pl.pallas_call(functools.partial(fwd_kernel, vocab, half, tuple(bases), t...  76.5 us
    ppermute x33, waiting for transfers between devices, shift(): return lax.ppermute(x, axis, [(i, (i + by) % n) for i in range(n)])  66.6 us
    pallas_call x2, Pallas kernels, stats(): pl.pallas_call(functools.partial(stats_kernel, tps, xs, order, own), out_...  44.4 us
    pallas_call x2, Pallas kernels, de_call(): pl.pallas_call(functools.partial(de_kernel, b0, len(us)), out_shape=(shap...  37.3 us
    ppermute x33, starting transfers between devices, shift(): return lax.ppermute(x, axis, [(i, (i + by) % n) for i in range(n)])  36.2 us
    pallas_call x2, Pallas kernels, expand_call(): pl.pallas_call(functools.partial(expand_kernel, vocab, half, plan), out_s...  20.8 us
    pallas_call x1, Pallas kernels, du_call(): pl.pallas_call(functools.partial(du_kernel, vocab, half), out_shape=shape...  16.9 us
    pallas_call x1, Pallas kernels, g_own(): pl.pallas_call(g_kernel, out_shape=(shape(half, width, BF16), shape(width...  11.6 us
  transfers between devices with their start and end apart: 33, of which 11 were waited for; matrix products, arithmetic and copies ran while one was open for 3% of the time, Pallas kernels for 48%

profile of v2, /device:TPU:1, one launch (start us, length us, event | category | flops | bytes accessed | tf_op | source)
XLA Modules:
  0.0 344.9 jit_solution(12280552919394681698)
XLA Ops:
  0.6 1.5 fusion
  2.2 1.4 convert_multiply_fusion.refs_0_
  3.6 1.5 collective-permute-start.1
  5.1 2.6 collective-permute-start.10
  7.7 4.0 %sort_lists.1.refs_0_ = f32[512,256]{1,0:T(8,128)} custom-call(s32[256,256]{1,0:T(8,128)} %ids_ref.1, f32[256,256]{1,0:T(8,128)} %pt_ref.1, f32[1,256]{1,0:T(1,128)} %bitcast.9), custom_call_target="tpu_custom_call" | custom-call | flops 4000000000 | bytes 1048576 | tf_op jit(solution)/shard_map/sort_lists/pallas_call | solution.py:112
  11.7 0.4 collective-permute-start
  12.0 0.5 collective-permute-start.2
  12.5 0.6 broadcast_add_fusion
  13.1 0.7 constant_dynamic-slice_fusion.refs_7_
  13.8 2.5 collective-permute-start.4
  16.3 36.3 %collective-permute-done.10.refs_2_ = f32[256,2048]{1,0:T(8,128)} collective-permute-done((f32[256,2048]{1,0:T(8,128)S(1)}, f32[256,2048]{1,0:T(8,128)}, u32[]{:S(2)}, u32[]{:S(2)}) %collective-permute-start.10) | collective-permute-done | bytes 2097184 | tf_op jit(solution)/shard_map/ppermute | solution.py:829
  52.6 1.5 collective-permute-start.11
  54.0 1.8 collective-permute-done.8.refs_0_
  55.8 2.0 collective-permute-start.9
  57.8 16.5 %shard_map.93 = (f32[4096,512]{1,0:T(8,128)}, f32[8,512]{1,0:T(8,128)}, f32[8,512]{1,0:T(8,128)}, bf16[512,512]{1,0:T(8,128)(2,1)}) custom-call(f32[256,2048]{1,0:T(8,128)} %copy-done, f32[256,2048]{1,0:T(8,128)} %collective-permute-done.1.refs_1_, f32[1,2048]{1,0:T(1,128)} %bitcast.5, bf16[8016,2048]{1,0:T(8,128)(2,1)} %refs_5_.3), custom_call_target="tpu_custom_call" | custom-call | flops 8589934592 | bytes 29360128 | tf_op jit(solution)/shard_map/pallas_call | solution.py:354
  74.3 1.3 slice.16
  75.7 0.7 copy-done.22
  76.4 28.0 %shard_map.94 = (f32[1,512]{1,0:T(1,128)}, f32[1,512]{1,0:T(1,128)}, f32[1,128]{1,0:T(1,128)}, f32[1,128]{1,0:T(1,128)}) custom-call(f32[512,256]{1,0:T(8,128)} %sort_lists.1.refs_0_, f32[512,256]{1,0:T(8,128)} %copy-done.22, f32[8,512]{1,0:T(8,128)} %get-tuple-element.43.refs_2_, f32[8,512]{1,0:T(8,128)} %get-tuple-element.44.refs_3_), custom_call_target="tpu_custom_call" | custom-call | flops 2000000000 | bytes 65536 | tf_op jit(solution)/shard_map/pallas_call | solution.py:488
  104.4 5.4 %shard_map.95 = (s32[256,512]{1,0:T(8,128)}, f32[256,512]{1,0:T(8,128)}, s32[32,128]{1,0:T(8,128)}, s32[256,512]{1,0:T(8,128)}, f32[256,512]{1,0:T(8,128)}) custom-call(f32[512,256]{1,0:T(8,128)} %sort_lists.1.refs_0_, f32[512,256]{1,0:T(8,128)} %copy-done.22, f32[1,512]{1,0:T(1,128)} %get-tuple-element.46.refs_2_), custom_call_target="tpu_custom_call" | custom-call | flops 400000000 | bytes 3145728 | tf_op jit(solution)/shard_map/pallas_call | solution.py:218
  109.8 1.3 reduce_max.18.cnt_ref
  111.2 2.3 slice.17
  113.5 11.6 %g_own.1 = (bf16[4096,512]{1,0:T(8,128)(2,1)}, bf16[512,4096]{1,0:T(8,128)(2,1)}, f32[8,512]{1,0:T(8,128)}) custom-call(s32[32]{0:T(128)} %reduce_max.18.cnt_ref, f32[4096,512]{1,0:T(8,128)} %get-tuple-element.48.z_ref, f32[1,512]{1,0:T(1,128)} %get-tuple-element.49.c_ref, s32[256,512]{1,0:T(8,128)} %get-tuple-element.50.tabr_ref, ...), custom_call_target="tpu_custom_call" | custom-call | flops 4000000000 | bytes 16777216 | tf_op jit(solution)/shard_map/g_own/pallas_call | solution.py:613
  125.0 1.7 collective-permute-start.6
  126.8 16.9 %grad_u.1.refs_6_ = f32[256,2048]{1,0:T(8,128)} custom-call(bf16[512,4096]{1,0:T(8,128)(2,1)} %get-tuple-element.54.gt_ref, bf16[8016,2048]{1,0:T(8,128)(2,1)} %refs_5_.3), custom_call_target="tpu_custom_call" | custom-call | flops 8589934592 | bytes 16777216 | tf_op jit(solution)/shard_map/grad_u/pallas_call | solution.py:678
  143.6 0.5 collective-permute-start.3
  144.1 0.1 collective-permute-start.5
  144.2 0.4 collective-permute-start.7
  144.8 0.4 collective-permute-start.15
  145.1 43.6 %shard_map.96 = (f32[4096,1024]{1,0:T(8,128)}, f32[8,1024]{1,0:T(8,128)}, f32[8,1024]{1,0:T(8,128)}, bf16[1024,512]{1,0:T(8,128)(2,1)}, f32[16,2048]{1,0:T(8,128)}, /*index=5*/f32[1,2048]{1,0:T(1,128)}) custom-call(f32[256,2048]{1,0:T(8,128)} %collective-permute-done.8.refs_0_, f32[256,2048]{1,0:T(8,128)} %collective-permute-done.9.refs_1_, ...), custom_call_target="tpu_custom_call" | custom-call | flops 17179869184 | bytes 41943040 | tf_op jit(solution)/shard_map/pallas_call | solution.py:354
  188.8 0.9 copy-done.4
  189.7 16.4 %shard_map.97 = (f32[4096,512]{1,0:T(8,128)}, f32[8,512]{1,0:T(8,128)}, f32[8,512]{1,0:T(8,128)}, bf16[512,512]{1,0:T(8,128)(2,1)}) custom-call(f32[128,2048]{1,0:T(8,128)} %copy-done.2, f32[128,2048]{1,0:T(8,128)} %copy-done.4, f32[128,2048]{1,0:T(8,128)} %copy-done.3, f32[128,2048]{1,0:T(8,128)} %collective-permute-done.15.refs_3_, f32[1,2048]{1,0:T(1,128)} %bitcast.7, ...), custom_call_target="tpu_custom_call" | custom-call | flops 8589934592 | bytes 29360128 | tf_op jit(solution)/shard_map/pallas_call | solution.py:354
  206.2 16.4 %shard_map.98 = (f32[1,1536]{1,0:T(1,128)}, f32[1,1536]{1,0:T(1,128)}, f32[1,128]{1,0:T(1,128)}, f32[24,128]{1,0:T(8,128)}) custom-call(f32[512,256]{1,0:T(8,128)} %collective-permute-done.2.refs_0_, f32[512,256]{1,0:T(8,128)} %collective-permute-done.3.refs_1_, f32[512,256]{1,0:T(8,128)} %collective-permute-done.4.refs_2_, ...), custom_call_target="tpu_custom_call" | custom-call | flops 2000000000 | bytes 65536 | tf_op jit(solution)/shard_map/pallas_call | solution.py:488
  222.6 15.4 %shard_map.99 = (s32[256,1536]{1,0:T(8,128)}, f32[256,1536]{1,0:T(8,128)}, s32[32,128]{1,0:T(8,128)}, s32[256,1536]{1,0:T(8,128)}, f32[256,1536]{1,0:T(8,128)}) custom-call(f32[512,256]{1,0:T(8,128)} %collective-permute-done.2.refs_0_, f32[512,256]{1,0:T(8,128)} %collective-permute-done.3.refs_1_, f32[512,256]{1,0:T(8,128)} %collective-permute-done.4.refs_2_, ...), custom_call_target="tpu_custom_call" | custom-call | flops 1200000000 | bytes 9437184 | tf_op jit(solution)/shard_map/pallas_call | solution.py:218
  238.0 1.3 reduce_max.19.cnt_ref
  239.3 18.6 %shard_map.100 = (f32[8016,256]{1,0:T(8,128)}, f32[2048,256]{1,0:T(8,128)}) custom-call(s32[32]{0:T(128)} %reduce_max.19.cnt_ref, bf16[512,512]{1,0:T(8,128)(2,1)} %get-tuple-element.67.refs_0_, bf16[1024,512]{1,0:T(8,128)(2,1)} %get-tuple-element.68.refs_1_, bf16[512,512]{1,0:T(8,128)(2,1)} %get-tuple-element.69.refs_2_, ...), custom_call_target="tpu_custom_call" | custom-call | flops 6442450944 | bytes 18874368 | tf_op jit(solution)/shard_map/pallas_call | solution.py:758
  257.9 2.0 collective-permute-start.32
  260.0 18.7 %shard_map.101 = (f32[8016,256]{1,0:T(8,128)}, f32[2048,256]{1,0:T(8,128)}) custom-call(s32[32]{0:T(128)} %reduce_max.19.cnt_ref, bf16[512,512]{1,0:T(8,128)(2,1)} %get-tuple-element.67.refs_0_, bf16[1024,512]{1,0:T(8,128)(2,1)} %get-tuple-element.68.refs_1_, bf16[512,512]{1,0:T(8,128)(2,1)} %get-tuple-element.69.refs_2_, ...), custom_call_target="tpu_custom_call", output_to_operand_aliasing={{0}: (12, {})} | custom-call | flops 6442450944 | bytes 18874368 | tf_op jit(solution)/shard_map/pallas_call | solution.py:758
  278.7 0.2 collective-permute-start.31
  279.0 1.2 collective-permute-start.17
  280.2 1.4 collective-permute-start.18
  281.6 9.6 %collective-permute-done.16.refs_1_ = f32[16,2048]{1,0:T(8,128)S(1)} collective-permute-done((f32[16,2048]{1,0:T(8,128)S(1)}, f32[16,2048]{1,0:T(8,128)S(1)}, u32[]{:S(2)}, u32[]{:S(2)}) %collective-permute-start.16) | collective-permute-done | bytes 131104 | tf_op jit(solution)/shard_map/ppermute | solution.py:829
  291.3 0.2 collective-permute-done.18.refs_3_
  291.5 9.5 %collective-permute-done.19.refs_4_ = f32[16,2048]{1,0:T(8,128)S(1)} collective-permute-done((f32[16,2048]{1,0:T(8,128)S(1)}, f32[16,2048]{1,0:T(8,128)S(1)}, u32[]{:S(2)}, u32[]{:S(2)}) %collective-permute-start.19) | collective-permute-done | bytes 131104 | tf_op jit(solution)/shard_map/ppermute | solution.py:829
  301.0 1.5 collective-permute-done.20.refs_5_
  302.5 2.4 collective-permute-start.24
  304.9 2.3 collective-permute-done.22.refs_7_
  307.3 1.3 collective-permute-done.23.refs_8_
  308.6 2.6 collective-permute-start.26
  311.2 8.1 %collective-permute-start.27 = (f32[16,2048]{1,0:T(8,128)S(1)}, f32[16,2048]{1,0:T(8,128)}, u32[]{:S(2)}, u32[]{:S(2)}) collective-permute-start(f32[16,2048]{1,0:T(8,128)S(1)} %copy-done.5), channel_id=1, source_target_pairs={{0,96},{8,104},{16,112},{24,120},{32,0},{40,8},{48,16},{56,24},{64... | collective-permute-start | bytes 393224 | tf_op jit(solution)/shard_map/ppermute | solution.py:829
  319.3 0.8 copy.13.refs_16_
  320.1 1.2 reduce_sum.37
  321.3 1.3 reduce_sum.38
  323.9 0.6 slice_reduce_fusion
  325.1 1.4 collective-permute-start.28
  326.6 2.5 collective-permute-start.30
  329.0 0.6 slice_bitcast_fusion
  329.6 1.1 collective-permute-done.28.refs_13_
  330.7 1.3 collective-permute-done.29.refs_14_
  332.0 1.7 collective-permute-done.30.refs_15_
  333.8 0.6 copy-done.18
  334.4 2.8 grad_h.1
  337.2 1.3 copy-done.1
  338.5 2.6 shard_map.102.prev_ref
  341.2 2.6 shard_map.103
  (77 shorter events, 0.5 us)
Async XLA Ops:
  3.6 9.5 %copy-start = (f32[256,2048]{1,0:T(8,128)}, f32[256,2048]{1,0:T(8,128)S(1)}, u32[]{:S(2)}) copy-start(f32[256,2048]{1,0:T(8,128)S(1)} %convert_multiply_fusion.refs_0_) | copy-start | bytes 6291460
  3.6 10.2 %collective-permute-start.1 = (f32[256,2048]{1,0:T(8,128)S(1)}, f32[256,2048]{1,0:T(8,128)}, u32[]{:S(2)}, u32[]{:S(2)}) collective-permute-start(f32[256,2048]{1,0:T(8,128)S(1)} %convert_multiply_fusion.refs_0_), channel_id=1, source_target_pairs={{0,1},{1,0},{2,3},{3,2},{4,5},{5,4},{6,7},{7,6},{8,9},{9,8},{10,11... | collective-permute-start | bytes 6291464 | tf_op jit(solution)/shard_map/ppermute | solution.py:829
  5.1 47.5 %collective-permute-start.10 = (f32[256,2048]{1,0:T(8,128)S(1)}, f32[256,2048]{1,0:T(8,128)}, u32[]{:S(2)}, u32[]{:S(2)}) collective-permute-start(f32[256,2048]{1,0:T(8,128)S(1)} %convert_multiply_fusion.refs_0_), channel_id=1, source_target_pairs={{0,6},{2,0},{4,2},{6,4},{1,7},{3,1},{5,3},{7,5},{8,14},{10,8},{12,... | collective-permute-start | bytes 6291464 | tf_op jit(solution)/shard_map/ppermute | solution.py:829
  7.7 48.1 %collective-permute-start.8 = (f32[256,2048]{1,0:T(8,128)S(1)}, f32[256,2048]{1,0:T(8,128)}, u32[]{:S(2)}, u32[]{:S(2)}) collective-permute-start(f32[256,2048]{1,0:T(8,128)S(1)} %convert_multiply_fusion.refs_0_), channel_id=1, source_target_pairs={{0,2},{2,4},{4,6},{6,0},{1,3},{3,5},{5,7},{7,1},{8,10},{10,12},{12... | collective-permute-start | bytes 6291464 | tf_op jit(solution)/shard_map/ppermute | solution.py:829
  7.7 4.9 %copy-start.19 = (f32[2048]{0:T(1024)S(1)}, f32[2048]{0:T(1024)}, u32[]{:S(2)}) copy-start(f32[2048]{0:T(1024)} %param.8) | copy-start | bytes 24580
  11.7 64.0 %collective-permute-start = (f32[512,256]{1,0:T(8,128)}, f32[512,256]{1,0:T(8,128)S(1)}, u32[]{:S(2)}, u32[]{:S(2)}) collective-permute-start(f32[512,256]{1,0:T(8,128)} %sort_lists.1.refs_0_), channel_id=1, source_target_pairs={{0,1},{1,0},{2,3},{3,2},{4,5},{5,4},{6,7},{7,6},{8,9},{9,8},{10,11... | collective-permute-start | bytes 1572872 | tf_op jit(solution)/shard_map/ppermute | solution.py:829
  12.0 101.4 %collective-permute-start.2 = (f32[512,256]{1,0:T(8,128)}, f32[512,256]{1,0:T(8,128)}, u32[]{:S(2)}, u32[]{:S(2)}) collective-permute-start(f32[512,256]{1,0:T(8,128)} %sort_lists.1.refs_0_), channel_id=1, source_target_pairs={{0,2},{2,4},{4,6},{6,0},{1,3},{3,5},{5,7},{7,1},{8,10},{10,12},{12... | collective-permute-start | bytes 1572872 | tf_op jit(solution)/shard_map/ppermute | solution.py:829
  13.8 111.2 %collective-permute-start.4 = (f32[512,256]{1,0:T(8,128)}, f32[512,256]{1,0:T(8,128)}, u32[]{:S(2)}, u32[]{:S(2)}) collective-permute-start(f32[512,256]{1,0:T(8,128)} %sort_lists.1.refs_0_), channel_id=1, source_target_pairs={{0,6},{2,0},{4,2},{6,4},{1,7},{3,1},{5,3},{7,5},{8,14},{10,8},{12,... | collective-permute-start | bytes 1572872 | tf_op jit(solution)/shard_map/ppermute | solution.py:829
  52.6 92.1 %collective-permute-start.11 = (f32[256,2048]{1,0:T(8,128)}, f32[256,2048]{1,0:T(8,128)}, u32[]{:S(2)}, u32[]{:S(2)}) collective-permute-start(f32[256,2048]{1,0:T(8,128)} %collective-permute-done.10.refs_2_), channel_id=1, source_target_pairs={{0,1},{1,0},{2,3},{3,2},{4,5},{5,4},{6,7},{7,6},{8,9},{9,8},{10,11... | collective-permute-start | bytes 6291464 | tf_op jit(solution)/shard_map/ppermute | solution.py:829
  55.8 89.0 %collective-permute-start.9 = (f32[256,2048]{1,0:T(8,128)}, f32[256,2048]{1,0:T(8,128)}, u32[]{:S(2)}, u32[]{:S(2)}) collective-permute-start(f32[256,2048]{1,0:T(8,128)} %collective-permute-done.8.refs_0_), channel_id=1, source_target_pairs={{0,1},{1,0},{2,3},{3,2},{4,5},{5,4},{6,7},{7,6},{8,9},{9,8},{10,11... | collective-permute-start | bytes 6291464 | tf_op jit(solution)/shard_map/ppermute | solution.py:829
  75.6 0.8 copy-start.22
  75.7 68.4 %collective-permute-start.12 = (f32[128,2048]{1,0:T(8,128)S(1)}, f32[128,2048]{1,0:T(8,128)S(1)}, u32[]{:S(2)}, u32[]{:S(2)}) collective-permute-start(f32[128,2048]{1,0:T(8,128)S(1)} %slice.16), channel_id=1, source_target_pairs={{0,2},{2,4},{4,6},{6,0},{1,3},{3,5},{5,7},{7,1},{8,10},{10,12},{12... | collective-permute-start | bytes 3145736 | tf_op jit(solution)/shard_map/ppermute | solution.py:829
  113.5 30.8 %collective-permute-start.14 = (f32[128,2048]{1,0:T(8,128)}, f32[128,2048]{1,0:T(8,128)S(1)}, u32[]{:S(2)}, u32[]{:S(2)}) collective-permute-start(f32[128,2048]{1,0:T(8,128)} %slice.17), channel_id=1, source_target_pairs={{0,6},{2,0},{4,2},{6,4},{1,7},{3,1},{5,3},{7,5},{8,14},{10,8},{12,... | collective-permute-start | bytes 3145736 | tf_op jit(solution)/shard_map/ppermute | solution.py:829
  125.0 18.6 %collective-permute-start.6 = (f32[512,256]{1,0:T(8,128)}, f32[512,256]{1,0:T(8,128)S(1)}, u32[]{:S(2)}, u32[]{:S(2)}) collective-permute-start(f32[512,256]{1,0:T(8,128)} %collective-permute-done.2.refs_0_), channel_id=1, source_target_pairs={{0,2},{2,4},{4,6},{6,0},{1,3},{3,5},{5,7},{7,1},{8,10},{10,12},{12... | collective-permute-start | bytes 1572872 | tf_op jit(solution)/shard_map/ppermute | solution.py:829
  143.6 45.1 %copy-start.21 = (f32[512,256]{1,0:T(8,128)}, f32[512,256]{1,0:T(8,128)S(1)}, u32[]{:S(2)}) copy-start(f32[512,256]{1,0:T(8,128)S(1)} %collective-permute-done.6.refs_4_) | copy-start | bytes 1572868
  143.6 62.5 %collective-permute-start.3 = (f32[512,256]{1,0:T(8,128)}, f32[512,256]{1,0:T(8,128)}, u32[]{:S(2)}, u32[]{:S(2)}) collective-permute-start(f32[512,256]{1,0:T(8,128)} %collective-permute-done.2.refs_0_), channel_id=1, source_target_pairs={{0,1},{1,0},{2,3},{3,2},{4,5},{5,4},{6,7},{7,6},{8,9},{9,8},{10,11... | collective-permute-start | bytes 1572872 | tf_op jit(solution)/shard_map/ppermute | solution.py:829
  144.1 44.7 %copy-start.2 = (f32[128,2048]{1,0:T(8,128)}, f32[128,2048]{1,0:T(8,128)S(1)}, u32[]{:S(2)}) copy-start(f32[128,2048]{1,0:T(8,128)S(1)} %collective-permute-done.12.refs_0_) | copy-start | bytes 3145732
  144.1 62.1 %collective-permute-start.5 = (f32[512,256]{1,0:T(8,128)}, f32[512,256]{1,0:T(8,128)}, u32[]{:S(2)}, u32[]{:S(2)}) collective-permute-start(f32[512,256]{1,0:T(8,128)} %collective-permute-done.4.refs_2_), channel_id=1, source_target_pairs={{0,1},{1,0},{2,3},{3,2},{4,5},{5,4},{6,7},{7,6},{8,9},{9,8},{10,11... | collective-permute-start | bytes 1572872 | tf_op jit(solution)/shard_map/ppermute | solution.py:829
  144.2 44.5 %copy-start.3 = (f32[128,2048]{1,0:T(8,128)}, f32[128,2048]{1,0:T(8,128)S(1)}, u32[]{:S(2)}) copy-start(f32[128,2048]{1,0:T(8,128)S(1)} %collective-permute-done.14.refs_2_) | copy-start | bytes 3145732
  144.2 61.9 %collective-permute-start.7 = (f32[512,256]{1,0:T(8,128)S(1)}, f32[512,256]{1,0:T(8,128)}, u32[]{:S(2)}, u32[]{:S(2)}) collective-permute-start(f32[512,256]{1,0:T(8,128)S(1)} %collective-permute-done.6.refs_4_), channel_id=1, source_target_pairs={{0,1},{1,0},{2,3},{3,2},{4,5},{5,4},{6,7},{7,6},{8,9},{9,8},{10,11... | collective-permute-start | bytes 1572872 | tf_op jit(solution)/shard_map/ppermute | solution.py:829
  144.6 44.2 %collective-permute-start.13 = (f32[128,2048]{1,0:T(8,128)S(1)}, f32[128,2048]{1,0:T(8,128)S(1)}, u32[]{:S(2)}, u32[]{:S(2)}) collective-permute-start(f32[128,2048]{1,0:T(8,128)S(1)} %collective-permute-done.12.refs_0_), channel_id=1, source_target_pairs={{0,1},{1,0},{2,3},{3,2},{4,5},{5,4},{6,7},{7,6},{8,9},{9,8},{10,11... | collective-permute-start | bytes 3145736 | tf_op jit(solution)/shard_map/ppermute | solution.py:829
  144.8 44.0 %collective-permute-start.15 = (f32[128,2048]{1,0:T(8,128)S(1)}, f32[128,2048]{1,0:T(8,128)}, u32[]{:S(2)}, u32[]{:S(2)}) collective-permute-start(f32[128,2048]{1,0:T(8,128)S(1)} %collective-permute-done.14.refs_2_), channel_id=1, source_target_pairs={{0,1},{1,0},{2,3},{3,2},{4,5},{5,4},{6,7},{7,6},{8,9},{9,8},{10,11... | collective-permute-start | bytes 3145736 | tf_op jit(solution)/shard_map/ppermute | solution.py:829
  188.8 1.0 copy-start.4
  257.9 79.3 %collective-permute-start.32 = (f32[2048,256]{1,0:T(8,128)}, f32[2048,256]{1,0:T(8,128)S(1)}, u32[]{:S(2)}, u32[]{:S(2)}) collective-permute-start(f32[2048,256]{1,0:T(8,128)} %get-tuple-element.80), channel_id=1, source_target_pairs={{0,1},{1,0},{2,3},{3,2},{4,5},{5,4},{6,7},{7,6},{8,9},{9,8},{10,11... | collective-permute-start | bytes 6291464 | tf_op jit(solution)/shard_map/ppermute | solution.py:829
  260.0 18.9 %copy-start.5 = (f32[16,2048]{1,0:T(8,128)S(1)}, f32[16,2048]{1,0:T(8,128)}, u32[]{:S(2)}) copy-start(f32[16,2048]{1,0:T(8,128)} %get-tuple-element.64.refs_0_) | copy-start | bytes 393220
  260.0 63.9 %copy-start.20 = (f32[24,128]{1,0:T(8,128)S(1)}, f32[24,128]{1,0:T(8,128)}, u32[]{:S(2)}) copy-start(f32[24,128]{1,0:T(8,128)} %get-tuple-element.63) | copy-start | bytes 36868
  278.7 62.5 %collective-permute-start.31 = (f32[2048,256]{1,0:T(8,128)}, f32[2048,256]{1,0:T(8,128)}, u32[]{:S(2)}, u32[]{:S(2)}) collective-permute-start(f32[2048,256]{1,0:T(8,128)} %get-tuple-element.79), channel_id=1, source_target_pairs={{0,1},{1,0},{2,3},{3,2},{4,5},{5,4},{6,7},{7,6},{8,9},{9,8},{10,11... | collective-permute-start | bytes 6291464 | tf_op jit(solution)/shard_map/ppermute | solution.py:829
  278.9 12.3 %collective-permute-start.16 = (f32[16,2048]{1,0:T(8,128)S(1)}, f32[16,2048]{1,0:T(8,128)S(1)}, u32[]{:S(2)}, u32[]{:S(2)}) collective-permute-start(f32[16,2048]{1,0:T(8,128)S(1)} %copy-done.5), channel_id=1, source_target_pairs={{0,8},{8,16},{16,24},{24,32},{32,40},{40,48},{48,56},{56,64},{64,7... | collective-permute-start | bytes 393224 | tf_op jit(solution)/shard_map/ppermute | solution.py:829
  279.0 12.2 %collective-permute-start.17 = (f32[16,2048]{1,0:T(8,128)S(1)}, f32[16,2048]{1,0:T(8,128)S(1)}, u32[]{:S(2)}, u32[]{:S(2)}) collective-permute-start(f32[16,2048]{1,0:T(8,128)S(1)} %copy-done.5), channel_id=1, source_target_pairs={{0,16},{8,24},{16,32},{24,40},{32,48},{40,56},{48,64},{56,72},{64,... | collective-permute-start | bytes 393224 | tf_op jit(solution)/shard_map/ppermute | solution.py:829
  280.2 11.3 %collective-permute-start.18 = (f32[16,2048]{1,0:T(8,128)S(1)}, f32[16,2048]{1,0:T(8,128)S(1)}, u32[]{:S(2)}, u32[]{:S(2)}) collective-permute-start(f32[16,2048]{1,0:T(8,128)S(1)} %copy-done.5), channel_id=1, source_target_pairs={{0,24},{8,32},{16,40},{24,48},{32,56},{40,64},{48,72},{56,80},{64,... | collective-permute-start | bytes 393224 | tf_op jit(solution)/shard_map/ppermute | solution.py:829
  291.2 42.5 %copy-start.6 = (f32[16,2048]{1,0:T(8,128)}, f32[16,2048]{1,0:T(8,128)S(1)}, u32[]{:S(2)}) copy-start(f32[16,2048]{1,0:T(8,128)S(1)} %collective-permute-done.16.refs_1_) | copy-start | bytes 393220
  291.2 9.8 %collective-permute-start.19 = (f32[16,2048]{1,0:T(8,128)S(1)}, f32[16,2048]{1,0:T(8,128)S(1)}, u32[]{:S(2)}, u32[]{:S(2)}) collective-permute-start(f32[16,2048]{1,0:T(8,128)S(1)} %copy-done.5), channel_id=1, source_target_pairs={{0,32},{8,40},{16,48},{24,56},{32,64},{40,72},{48,80},{56,88},{64,... | collective-permute-start | bytes 393224 | tf_op jit(solution)/shard_map/ppermute | solution.py:829
  291.2 42.5 %copy-start.7 = (f32[16,2048]{1,0:T(8,128)}, f32[16,2048]{1,0:T(8,128)S(1)}, u32[]{:S(2)}) copy-start(f32[16,2048]{1,0:T(8,128)S(1)} %collective-permute-done.17.refs_2_) | copy-start | bytes 393220
  291.2 11.3 %collective-permute-start.20 = (f32[16,2048]{1,0:T(8,128)S(1)}, f32[16,2048]{1,0:T(8,128)S(1)}, u32[]{:S(2)}, u32[]{:S(2)}) collective-permute-start(f32[16,2048]{1,0:T(8,128)S(1)} %copy-done.5), channel_id=1, source_target_pairs={{0,40},{8,48},{16,56},{24,64},{32,72},{40,80},{48,88},{56,96},{64,... | collective-permute-start | bytes 393224 | tf_op jit(solution)/shard_map/ppermute | solution.py:829
  291.5 42.2 %copy-start.8 = (f32[16,2048]{1,0:T(8,128)}, f32[16,2048]{1,0:T(8,128)S(1)}, u32[]{:S(2)}) copy-start(f32[16,2048]{1,0:T(8,128)S(1)} %collective-permute-done.18.refs_3_) | copy-start | bytes 393220
  291.5 11.0 %collective-permute-start.21 = (f32[16,2048]{1,0:T(8,128)S(1)}, f32[16,2048]{1,0:T(8,128)S(1)}, u32[]{:S(2)}, u32[]{:S(2)}) collective-permute-start(f32[16,2048]{1,0:T(8,128)S(1)} %copy-done.5), channel_id=1, source_target_pairs={{0,48},{8,56},{16,64},{24,72},{32,80},{40,88},{48,96},{56,104},{64... | collective-permute-start | bytes 393224 | tf_op jit(solution)/shard_map/ppermute | solution.py:829
  301.0 32.7 %copy-start.9 = (f32[16,2048]{1,0:T(8,128)}, f32[16,2048]{1,0:T(8,128)S(1)}, u32[]{:S(2)}) copy-start(f32[16,2048]{1,0:T(8,128)S(1)} %collective-permute-done.19.refs_4_) | copy-start | bytes 393220
  301.0 6.3 %collective-permute-start.22 = (f32[16,2048]{1,0:T(8,128)S(1)}, f32[16,2048]{1,0:T(8,128)S(1)}, u32[]{:S(2)}, u32[]{:S(2)}) collective-permute-start(f32[16,2048]{1,0:T(8,128)S(1)} %copy-done.5), channel_id=1, source_target_pairs={{0,56},{8,64},{16,72},{24,80},{32,88},{40,96},{48,104},{56,112},{6... | collective-permute-start | bytes 393224 | tf_op jit(solution)/shard_map/ppermute | solution.py:829
  302.5 31.2 %copy-start.10 = (f32[16,2048]{1,0:T(8,128)}, f32[16,2048]{1,0:T(8,128)S(1)}, u32[]{:S(2)}) copy-start(f32[16,2048]{1,0:T(8,128)S(1)} %collective-permute-done.20.refs_5_) | copy-start | bytes 393220
  302.5 6.1 %collective-permute-start.23 = (f32[16,2048]{1,0:T(8,128)S(1)}, f32[16,2048]{1,0:T(8,128)S(1)}, u32[]{:S(2)}, u32[]{:S(2)}) collective-permute-start(f32[16,2048]{1,0:T(8,128)S(1)} %copy-done.5), channel_id=1, source_target_pairs={{0,64},{8,72},{16,80},{24,88},{32,96},{40,104},{48,112},{56,120},{... | collective-permute-start | bytes 393224 | tf_op jit(solution)/shard_map/ppermute | solution.py:829
  302.5 31.1 %copy-start.11 = (f32[16,2048]{1,0:T(8,128)}, f32[16,2048]{1,0:T(8,128)S(1)}, u32[]{:S(2)}) copy-start(f32[16,2048]{1,0:T(8,128)S(1)} %collective-permute-done.21.refs_6_) | copy-start | bytes 393220
  302.5 8.7 %collective-permute-start.24 = (f32[16,2048]{1,0:T(8,128)S(1)}, f32[16,2048]{1,0:T(8,128)S(1)}, u32[]{:S(2)}, u32[]{:S(2)}) collective-permute-start(f32[16,2048]{1,0:T(8,128)S(1)} %copy-done.5), channel_id=1, source_target_pairs={{0,72},{8,80},{16,88},{24,96},{32,104},{40,112},{48,120},{56,0},{6... | collective-permute-start | bytes 393224 | tf_op jit(solution)/shard_map/ppermute | solution.py:829
  307.3 26.4 %copy-start.12 = (f32[16,2048]{1,0:T(8,128)}, f32[16,2048]{1,0:T(8,128)S(1)}, u32[]{:S(2)}) copy-start(f32[16,2048]{1,0:T(8,128)S(1)} %collective-permute-done.22.refs_7_) | copy-start | bytes 393220
  307.3 17.9 %collective-permute-start.25 = (f32[16,2048]{1,0:T(8,128)S(1)}, f32[16,2048]{1,0:T(8,128)S(1)}, u32[]{:S(2)}, u32[]{:S(2)}) collective-permute-start(f32[16,2048]{1,0:T(8,128)S(1)} %copy-done.5), channel_id=1, source_target_pairs={{0,80},{8,88},{16,96},{24,104},{32,112},{40,120},{48,0},{56,8},{64... | collective-permute-start | bytes 393224 | tf_op jit(solution)/shard_map/ppermute | solution.py:829
  308.6 25.1 %copy-start.13 = (f32[16,2048]{1,0:T(8,128)}, f32[16,2048]{1,0:T(8,128)S(1)}, u32[]{:S(2)}) copy-start(f32[16,2048]{1,0:T(8,128)S(1)} %collective-permute-done.23.refs_8_) | copy-start | bytes 393220
  308.6 17.9 %collective-permute-start.26 = (f32[16,2048]{1,0:T(8,128)S(1)}, f32[16,2048]{1,0:T(8,128)}, u32[]{:S(2)}, u32[]{:S(2)}) collective-permute-start(f32[16,2048]{1,0:T(8,128)S(1)} %copy-done.5), channel_id=1, source_target_pairs={{0,88},{8,96},{16,104},{24,112},{32,120},{40,0},{48,8},{56,16},{64... | collective-permute-start | bytes 393224 | tf_op jit(solution)/shard_map/ppermute | solution.py:829
  311.2 22.5 %copy-start.14 = (f32[16,2048]{1,0:T(8,128)}, f32[16,2048]{1,0:T(8,128)S(1)}, u32[]{:S(2)}) copy-start(f32[16,2048]{1,0:T(8,128)S(1)} %collective-permute-done.24.refs_9_) | copy-start | bytes 393220
  311.2 15.3 %collective-permute-start.27 = (f32[16,2048]{1,0:T(8,128)S(1)}, f32[16,2048]{1,0:T(8,128)}, u32[]{:S(2)}, u32[]{:S(2)}) collective-permute-start(f32[16,2048]{1,0:T(8,128)S(1)} %copy-done.5), channel_id=1, source_target_pairs={{0,96},{8,104},{16,112},{24,120},{32,0},{40,8},{48,16},{56,24},{64... | collective-permute-start | bytes 393224 | tf_op jit(solution)/shard_map/ppermute | solution.py:829
  325.1 8.6 %copy-start.15 = (f32[16,2048]{1,0:T(8,128)}, f32[16,2048]{1,0:T(8,128)S(1)}, u32[]{:S(2)}) copy-start(f32[16,2048]{1,0:T(8,128)S(1)} %collective-permute-done.25.refs_10_) | copy-start | bytes 393220
  325.1 5.6 %collective-permute-start.28 = (f32[16,2048]{1,0:T(8,128)S(1)}, f32[16,2048]{1,0:T(8,128)S(1)}, u32[]{:S(2)}, u32[]{:S(2)}) collective-permute-start(f32[16,2048]{1,0:T(8,128)S(1)} %copy-done.5), channel_id=1, source_target_pairs={{0,104},{8,112},{16,120},{24,0},{32,8},{40,16},{48,24},{56,32},{64... | collective-permute-start | bytes 393224 | tf_op jit(solution)/shard_map/ppermute | solution.py:829
  326.5 5.4 %collective-permute-start.29 = (f32[16,2048]{1,0:T(8,128)S(1)}, f32[16,2048]{1,0:T(8,128)S(1)}, u32[]{:S(2)}, u32[]{:S(2)}) collective-permute-start(f32[16,2048]{1,0:T(8,128)S(1)} %copy-done.5), channel_id=1, source_target_pairs={{0,112},{8,120},{16,0},{24,8},{32,16},{40,24},{48,32},{56,40},{64,... | collective-permute-start | bytes 393224 | tf_op jit(solution)/shard_map/ppermute | solution.py:829
  326.6 7.1 %collective-permute-start.30 = (f32[16,2048]{1,0:T(8,128)S(1)}, f32[16,2048]{1,0:T(8,128)S(1)}, u32[]{:S(2)}, u32[]{:S(2)}) collective-permute-start(f32[16,2048]{1,0:T(8,128)S(1)} %copy-done.5), channel_id=1, source_target_pairs={{0,120},{8,0},{16,8},{24,16},{32,24},{40,32},{48,40},{56,48},{64,5... | collective-permute-start | bytes 393224 | tf_op jit(solution)/shard_map/ppermute | solution.py:829
  330.7 3.0 copy-start.16
  332.0 1.8 copy-start.17
  333.8 0.7 copy-start.18
  337.2 1.3 copy-start.1

commit v3 on v2

v3 whole, which is shorter than its diff:
```python
import functools

import jax
import jax.numpy as jnp
import numpy as np
from jax import lax
from jax.experimental import pallas as pl
from jax.experimental.pallas import tpu as pltpu
from jax.sharding import Mesh
from jax.sharding import PartitionSpec as P


EPS_NORM = 1e-6
BIG = 1e30
NEG = -BIG
SMALL, LARGE = 1e8, 4e9
F32, BF16, I32 = jnp.float32, jnp.bfloat16, jnp.int32
LANES, SUB = 128, 8
ORDERED = ('arbitrary',)
SLOTS = 8
FAST = 2
TILE = 256
WIDE = 512
VMEM_LIMIT = 60 * 1024 * 1024
MESH = pl.DeviceIdType.MESH
VMEM = pl.BlockSpec(memory_space=pltpu.VMEM)
ANY = pl.BlockSpec(memory_space=pl.ANY)


def params(**kw):
    return pltpu.CompilerParams(vmem_limit_bytes=VMEM_LIMIT, **kw)


def cost(flops, nbytes, trans=0):
    return pl.CostEstimate(flops=int(flops), bytes_accessed=int(nbytes), transcendentals=int(trans))


def shape(rows, cols, dtype=F32):
    return jax.ShapeDtypeStruct((rows, cols), dtype)


def fixed(rows, cols):
    return pl.BlockSpec((rows, cols), lambda *a: (0, 0))


def one_row(cols):
    return fixed(1, cols)


def by_row(rows, cols):
    return pl.BlockSpec((rows, cols), lambda i: (i, 0))


def sub8(a):
    return slice(SUB * a, SUB * a + SUB)


def iota(rows, cols, axis=0):
    return lax.broadcasted_iota(I32, (rows, cols), axis)


def at(start, size):
    return pl.ds(pl.multiple_of(start, size), size)


def step_id():
    return pl.program_id(0)


def last_step():
    return pl.num_programs(0) - 1


def row_of(x):
    return (1, x.size)


def line(cols):
    return shape(1, cols)


def core_rows(vocab, half):
    return jnp.where(lax.axis_index('core') == 0, half, vocab - half)


class Links:
    def __init__(self, ssem, rsem):
        self.ssem, self.rsem, self.used = ssem, rsem, 0

    def copy(self, src, dst, to):
        k = self.used
        self.used += 1
        return pltpu.make_async_remote_copy(
            src_ref=src, dst_ref=dst, send_sem=self.ssem.at[k], recv_sem=self.rsem.at[k], device_id=to, device_id_type=MESH)


def start(copies):
    for c in copies:
        c.start()


def wait(copies):
    for c in copies:
        c.wait()


def hello(peers):
    for to in peers:
        pl.semaphore_signal(pltpu.get_barrier_semaphore(), inc=1, device_id=to, device_id_type=MESH)


def meet(peers):
    pl.semaphore_wait(pltpu.get_barrier_semaphore(), len(peers))


def dmas(n):
    return [pltpu.SemaphoreType.DMA((n,))] * 2


def comm(cid, **kw):
    return params(collective_id=cid, has_side_effects=True, **kw)


def other_core():
    return {'core': 1 - lax.axis_index('core')}


def along(axis, j, n):
    return {axis: lax.rem(lax.axis_index(axis) + j, n)}


def chip_peers(xs):
    here = lax.axis_index('x') * 2 + lax.axis_index('core')
    spots = [lax.rem(here + j, 2 * xs) for j in range(1, 2 * xs)]
    return [{'x': r // 2, 'core': lax.rem(r, 2)} for r in spots]


def pieces(x):
    return [x[:, g * LANES:(g + 1) * LANES] for g in range(x.shape[1] // LANES)]


def put_rows(ref, base, x):
    for g, piece in enumerate(pieces(x)):
        ref[base + g:base + g + 1, :] = piece


def norm_kernel(xs, h_ref, mask_ref, y_ref, inv_ref, count_ref, send, recv, ssem, rsem):
    peers = chip_peers(xs)
    hello(peers)
    send[...] = jnp.zeros(send.shape, F32)
    put_rows(send, 0, mask_ref[...])
    for r0 in range(0, h_ref.shape[0], LANES):
        rs = slice(r0, r0 + LANES)
        h = h_ref[rs, :].astype(F32)
        inv = lax.rsqrt(jnp.mean(h * h, axis=1, keepdims=True) + EPS_NORM)
        inv_ref[rs, :] = inv
        y_ref[rs, :] = h * inv
    meet(peers)
    links = Links(ssem, rsem)
    copies = [links.copy(send, recv.at[k], to) for k, to in enumerate(peers)]
    start(copies)
    wait(copies)
    total = send[...] + jnp.sum(recv[...], axis=0)
    count_ref[...] = jnp.broadcast_to(jnp.sum(total, keepdims=True), count_ref.shape)


def norm(hidden, mask, xs):
    tok, dim = hidden.shape
    n = 2 * xs - 1
    return pl.pallas_call(
        functools.partial(norm_kernel, xs),
        out_shape=(shape(tok, dim), shape(tok, 1), line(LANES)),
        in_specs=[VMEM] * 2,
        out_specs=(VMEM,) * 3,
        scratch_shapes=[pltpu.VMEM((SUB, LANES), F32), pltpu.VMEM((n, SUB, LANES), F32), *dmas(n)],
        compiler_params=comm(4),
        cost_estimate=cost(1e9, tok * dim * 6),
        name='norm',
    )(hidden, mask)


def sort_kernel(vocab, whole, ids_ref, pt_ref, mask_ref, y_hbm, out_ref, ypart_hbm, lpart_hbm, ssem, rsem):
    links = Links(ssem, rsem)
    to = other_core()
    y_copy, l_copy = links.copy(y_hbm, ypart_hbm, to), links.copy(out_ref, lpart_hbm, to)
    hello([to])
    meet([to])
    y_copy.start()
    n = ids_ref.shape[1]
    sub = iota(SUB, LANES)
    nv = n // SUB
    base = lax.axis_index('tp') * vocab
    for g in range(ids_ref.shape[0] // LANES):
        cols = slice(g * LANES, (g + 1) * LANES)
        order = ids_ref[cols, :] - base
        key = (jnp.where(order < 0, order + whole, order) + 1).astype(F32).T
        prob = pt_ref[cols, :].T
        k = [key[sub8(a), :] for a in range(nv)]
        p = [prob[sub8(a), :] for a in range(nv)]
        size = 2
        while size <= n:
            j = size // 2
            while j:
                if j >= SUB:
                    for a in range(nv):
                        if (SUB * a) & j:
                            continue
                        b = a + j // SUB
                        up = ((SUB * a) & size) == 0
                        swap = k[a] > k[b] if up else k[a] < k[b]
                        lo, hi = jnp.minimum(k[a], k[b]), jnp.maximum(k[a], k[b])
                        k[a], k[b] = (lo, hi) if up else (hi, lo)
                        p[a], p[b] = jnp.where(swap, p[b], p[a]), jnp.where(swap, p[a], p[b])
                else:
                    low = (sub & j) == 0
                    for a in range(nv):
                        if size >= SUB:
                            want_min = low if ((SUB * a) & size) == 0 else (sub & j) != 0
                        else:
                            want_min = low == ((sub & size) == 0)
                        ka = jnp.where(low, pltpu.roll(k[a], SUB - j, 0), pltpu.roll(k[a], j, 0))
                        pa = jnp.where(low, pltpu.roll(p[a], SUB - j, 0), pltpu.roll(p[a], j, 0))
                        new = jnp.where(want_min, jnp.minimum(k[a], ka), jnp.maximum(k[a], ka))
                        p[a] = jnp.where(new == ka, pa, p[a])
                        k[a] = new
                j //= 2
            size *= 2
        sign = jnp.where(mask_ref[:, cols] > 0, 1.0, -1.0)
        for a in range(nv):
            out_ref[sub8(a), cols] = k[a] * sign
            out_ref[sub8(nv + a), cols] = p[a]
    y_copy.wait()
    l_copy.start()
    l_copy.wait()


def sort_lists(ids, prob, mask, y, vocab, whole):
    tokens, top = ids.shape
    lists = shape(2 * top, tokens)
    return pl.pallas_call(
        functools.partial(sort_kernel, vocab, whole),
        out_shape=(lists, shape(*y.shape), lists),
        in_specs=[VMEM] * 3 + [ANY],
        out_specs=(VMEM, ANY, ANY),
        scratch_shapes=dmas(2),
        compiler_params=comm(5),
        cost_estimate=cost(LARGE, tokens * top * 16),
        name='sort_lists',
    )(ids, prob, mask, y)


def roll_all(x, op):
    for sh in (4, 2, 1):
        x = op(x, pltpu.roll(x, sh, 0))
    return x


def local_order(block, core, half):
    return jnp.abs(block).astype(I32) - 1 - core * half


def expand_kernel(vocab, half, plan, lane_block, *refs):
    lists, (w_ref, tabr_ref, tabp_ref, cnt_ref, src, loc_s, pw_s, sem) = refs[:-8], refs[-8:]
    g = step_id()
    groups = (last_step() + 1)
    core = lax.axis_index('core')
    rows = core_rows(vocab, half)
    top = src.shape[1] // 2
    nq = top // SUB
    nblk = half // LANES
    sub = iota(SUB, LANES)
    blank = jnp.zeros((SUB, LANES), I32)

    def fetch(k):
        which = plan(k, core)
        for a, ref in enumerate(lists):
            @pl.when(which == a)
            def _():
                pltpu.make_async_copy(ref.at[:, at(lane_block(k) * LANES, LANES)], src.at[k], sem.at[k]).start()

    @pl.when(g == 0)
    def _():
        cnt_ref[...] = jnp.zeros(cnt_ref.shape, I32)
        for k in range(src.shape[0]):
            fetch(k)

    pltpu.make_async_copy(lists[0].at[:, 0:LANES], src.at[g], sem.at[g]).wait()
    w = w_ref[...]
    over = blank
    used = blank
    first = jnp.full((SUB, LANES), nq, I32)
    prev = None
    for q in range(nq):
        order = local_order(src[g, sub8(q), :], core, half)
        ok = (order >= 0) & (order < rows)
        loc = jnp.where(ok, order, -1)
        loc_s[sub8(q), :] = loc
        pw_s[sub8(q), :] = src[g, sub8(nq + q), :] * w
        used = jnp.where(ok, q + 1, used)
        first = jnp.minimum(first, jnp.where(ok, q, nq))
        blk = loc >> 7
        if prev is not None:
            over = jnp.where((blk == prev) & ok, 1, over)
        prev = blk
    over = roll_all(over, jnp.maximum)
    lo, hi = jnp.min(first), jnp.max(used)

    def body(bt, carry):
        b0 = bt * SUB

        def scan(q, acc):
            accc, accp = list(acc[0]), list(acc[1])
            here = at(q * SUB, SUB)
            loc = loc_s[here, :]
            blk = (loc >> 7) - b0
            code = (sub + SUB * q) * LANES + (loc & (LANES - 1))
            p = pw_s[here, :]
            for i in range(SUB):
                m = blk == i
                accc[i] = jnp.where(m, code, accc[i])
                accp[i] = jnp.where(m, p, accp[i])
            return tuple(accc), tuple(accp)

        empty = (((blank - 1),) * SUB, (jnp.zeros((SUB, LANES), F32),) * SUB)
        accc, accp = lax.fori_loop(lo, hi, scan, empty)
        most = blank
        for i in range(SUB):
            code, p = accc[i], accp[i]
            head = roll_all(jnp.where(code >= 0, code, top * LANES), jnp.minimum)
            start_ = (head >> 7) & (SUB - 1)
            for sh in (1, 2, 4):
                move = (start_ & sh) != 0
                code = jnp.where(move, pltpu.roll(code, SUB - sh, 0), code)
                p = jnp.where(move, pltpu.roll(p, SUB - sh, 0), p)
            full = roll_all(jnp.where(code >= 0, sub + 1, 0), jnp.maximum)
            most = jnp.where(sub == i, full, most)
            row = at((b0 + i) * SUB, SUB)
            tabr_ref[row, :] = jnp.where(code >= 0, code & (LANES - 1), -1)
            tabp_ref[row, :] = p
        most = jnp.where(over > 0, SLOTS + 1, most)
        tile = at(b0, SUB)
        cnt_ref[tile, :] = jnp.maximum(cnt_ref[tile, :], most)
        return carry

    lax.fori_loop(0, nblk // SUB, body, 0)

    @pl.when(g == groups - 1)
    def _():
        most = jnp.max(cnt_ref[...].astype(F32), axis=1, keepdims=True)
        cnt_ref[...] = jnp.broadcast_to(most, cnt_ref.shape).astype(I32)


def expand(lists, plan, lane_block, weight, vocab, half):
    top = lists[0].shape[0] // 2
    groups = weight.shape[1] // LANES
    nblk = half // LANES
    width = groups * LANES

    def spec(rows):
        return pl.BlockSpec((rows, LANES), lambda g: (0, g))

    tabr, tabp, cnt = pl.pallas_call(
        functools.partial(expand_kernel, vocab, half, plan, lane_block),
        out_shape=(shape(nblk * SLOTS, width, I32), shape(nblk * SLOTS, width), shape(nblk, LANES, I32)),
        grid=(groups,),
        in_specs=[ANY] * len(lists) + [spec(1)],
        out_specs=(spec(nblk * SLOTS), spec(nblk * SLOTS), fixed(nblk, LANES)),
        scratch_shapes=[pltpu.VMEM((groups, 2 * top, LANES), F32), pltpu.VMEM((top, LANES), I32),
                        pltpu.VMEM((top, LANES), F32), pltpu.SemaphoreType.DMA((groups,))],
        compiler_params=params(dimension_semantics=ORDERED),
        cost_estimate=cost(groups * SMALL, 4 * width * (2 * top + 2 * nblk * SLOTS)),
    )(*lists, weight)
    return (tabr, tabp), cnt


def put_tokens(y_ref, dest, scale_ref, ut_ref, u_ref):
    here = at(dest, y_ref.shape[0])
    cols = u_ref.shape[1] // 2
    ut_ref[:, here] = (y_ref[...] * scale_ref[...]).astype(BF16).T
    core = lax.axis_index('core')
    for k, c in enumerate((core, 1 - core)):
        mine = at((2 * lax.axis_index('x') + c) * cols, cols)
        u_ref[here, k * cols:(k + 1) * cols] = (y_ref[:, mine] * scale_ref[:, mine]).astype(BF16)


def tiles(vocab, half, e_ref, ut_ref, z_ref, m_ref, s_ref):
    vb = e_ref.shape[0]
    i = step_id()
    left = core_rows(vocab, half) - i * vb

    @pl.when(i == 0)
    def _():
        m_ref[...] = jnp.full(m_ref.shape, NEG, F32)
        s_ref[...] = jnp.zeros(s_ref.shape, F32)

    for r0 in range(0, vb, TILE):
        rs = slice(r0, r0 + TILE)
        keep = iota(TILE, WIDE) < left - r0
        for c0 in range(0, ut_ref.shape[1], WIDE):
            cs = slice(c0, c0 + WIDE)
            z = jnp.dot(e_ref[rs, :], ut_ref[:, cs], preferred_element_type=F32)
            z = jnp.where(keep, z, NEG)
            z_ref[rs, cs] = z
            z3 = z.reshape(TILE // SUB, SUB, WIDE)
            old = m_ref[:, cs]
            new = jnp.maximum(old, jnp.max(z3, axis=0))
            m_ref[:, cs] = new
            s_ref[:, cs] = s_ref[:, cs] * jnp.exp(old - new) + jnp.sum(jnp.exp(z3 - new[None]), axis=0)


def own_kernel(vocab, half, y_ref, ypart_ref, scale_ref, e_ref, z_ref, m_ref, s_ref, u_ref, ut_ref):
    @pl.when(step_id() == 0)
    def _():
        tok = y_ref.shape[0]
        core = lax.axis_index('core')
        put_tokens(y_ref, core * tok, scale_ref, ut_ref, u_ref)
        put_tokens(ypart_ref, (1 - core) * tok, scale_ref, ut_ref, u_ref)

    tiles(vocab, half, e_ref, ut_ref, z_ref, m_ref, s_ref)


class Square:
    def __init__(self, n):
        t = lax.axis_index('tp')
        self.z, self.y, self.n = t // n, lax.rem(t, n), n
        self.zs = [lax.rem(self.z + j, n) for j in range(1, n)]
        self.ys = [lax.rem(self.y + j, n) for j in range(1, n)]
        self.along_z = [{'tp': z * n + self.y} for z in self.zs]
        self.along_y = [{'tp': self.z * n + y} for y in self.ys]
        self.peers = self.along_z + self.along_y


def x_peers(xs):
    return [along('x', 1, xs), along('x', xs - 1, xs)]


def gather_tokens(srcs, own, part, lsem, links):
    here = [pltpu.make_async_copy(src, own.at[k], lsem.at[k]) for k, src in enumerate(srcs)]
    there = [links.copy(src, part.at[k], other_core()) for k, src in enumerate(srcs)]
    return here, there


def place_tokens(here, there, own, part, scale_ref, ut_ref, u_ref):
    n = own.shape[1]
    core = lax.axis_index('core')
    wait(here)
    for k in range(own.shape[0]):
        put_tokens(own.at[k], (2 * k + core) * n, scale_ref, ut_ref, u_ref)
    wait(there)
    for k in range(own.shape[0]):
        put_tokens(part.at[k], (2 * k + 1 - core) * n, scale_ref, ut_ref, u_ref)


def near_kernel(xs, n, vocab, half, left, right, du, ysl_ref, scale_ref, e_ref,
                z_ref, m_ref, s_ref, u_ref, far0, far1, rest_ref, dw_ref,
                ut_ref, own, part, a1, b1, sa, sb, a2, b2, lsem, ssem, rsem):
    i = step_id()
    sq = Square(n)
    links = Links(ssem, rsem)
    cut = far0.shape[0]
    h = du.shape[3] // 2
    ahead, behind = x_peers(xs)
    here, there = gather_tokens((left, right), own, part, lsem, links)
    far = [links.copy(left.at[:cut, :], far0, ahead), links.copy(right.at[cut:2 * cut, :], far1, behind)]
    first, second = [], []
    for j, (z, y, to_z, to_y) in enumerate(zip(sq.zs, sq.ys, sq.along_z, sq.along_y)):
        k = j + 1
        first.append(links.copy(du.at[:, y, :, :h], a1.at[k], to_y))
        first.append(links.copy(du.at[z, :, :, h:2 * h], b1.at[k], to_z))
        second.append(links.copy(sa.at[z], a2.at[j], to_z))
        second.append(links.copy(sb.at[y], b2.at[j], to_y))
    mine = [pltpu.make_async_copy(du.at[:, sq.y, :, :h], a1.at[0], lsem.at[2]),
            pltpu.make_async_copy(du.at[sq.z, :, :, h:2 * h], b1.at[0], lsem.at[3])]
    peers = [other_core(), ahead, behind, *sq.peers]

    @pl.when(i == 0)
    def _():
        start(here)
        start(mine)
        hello(peers)
        meet(peers)
        start(there)
        start(first)
        start(far)
        place_tokens(here, there, own, part, scale_ref, ut_ref, u_ref)

    tiles(vocab, half, e_ref, ut_ref, z_ref, m_ref, s_ref)

    @pl.when(i == (last_step() + 1) - 3)
    def _():
        wait(mine)
        wait(first)
        sa[...] = jnp.sum(a1[...], axis=0)
        sb[...] = jnp.sum(b1[...], axis=0)

    @pl.when(i == (last_step() + 1) - 2)
    def _():
        start(second)

    @pl.when(i == last_step())
    def _():
        wait(second)
        parts = ((sa[sq.z] + jnp.sum(a2[...], axis=0), slice(h)), (sb[sq.y] + jnp.sum(b2[...], axis=0), slice(h, 2 * h)))
        dot = 0.0
        for du_sum, cs in parts:
            y = ysl_ref[:, cs]
            dot = dot + jnp.sum(du_sum * scale_ref[:, cs] * y, axis=1, keepdims=True)
            dw_ref[:, cs] = jnp.sum(du_sum * y, axis=0, keepdims=True)
        mean = dot / (2 * h)
        for du_sum, cs in parts:
            rest_ref[:, cs] = du_sum * scale_ref[:, cs] - ysl_ref[:, cs] * mean
        wait(far)


def far_kernel(xs, n, vocab, half, far0, far1, lists, rest_ref, scale_ref, e_ref,
               z_ref, m_ref, s_ref, u_ref, dh, l_left, p_left, l_right, p_right, l_far, p_far,
               ut_ref, own, part, lsem, ssem, rsem):
    i = step_id()
    sq = Square(n)
    links = Links(ssem, rsem)
    h = rest_ref.shape[1] // 2
    rows = lists.shape[0] // 2
    ahead, behind = x_peers(xs)
    core = other_core()
    here, there = gather_tokens((far0, far1), own, part, lsem, links)
    lists1 = [links.copy(lists, l_left, ahead), links.copy(lists, l_right, behind)]
    lists2 = [links.copy(l_left.at[:rows, :], l_far.at[:rows, :], ahead),
              links.copy(l_right.at[rows:2 * rows, :], l_far.at[rows:2 * rows, :], behind),
              links.copy(l_left, p_left, core), links.copy(l_right, p_right, core)]
    lists3 = [links.copy(l_far, p_far, core)]
    first, second = [], []
    a, b = slice(h), slice(h, 2 * h)
    z, y = sq.z, sq.y
    for to_z, to_y in zip(sq.along_z, sq.along_y):
        first.append(links.copy(rest_ref.at[:, a], dh.at[z, y, :, a], to_z))
        first.append(links.copy(rest_ref.at[:, b], dh.at[z, y, :, b], to_y))
        second.append(links.copy(dh.at[:, y, :, a], dh.at[:, y, :, a], to_y))
        second.append(links.copy(dh.at[z, :, :, b], dh.at[z, :, :, b], to_z))
    mine = [pltpu.make_async_copy(rest_ref, dh.at[z, y], lsem.at[2])]
    peers = [core, ahead, behind, *sq.peers]

    @pl.when(i == 0)
    def _():
        start(here)
        start(mine)
        hello(peers)
        meet(peers)
        start(there)
        start(first)
        start(lists1)
        place_tokens(here, there, own, part, scale_ref, ut_ref, u_ref)

    tiles(vocab, half, e_ref, ut_ref, z_ref, m_ref, s_ref)

    @pl.when(i == 2)
    def _():
        wait(mine)
        wait(first)
        start(second)

    @pl.when(i == last_step())
    def _():
        wait(lists1)
        start(lists2)
        wait(lists2)
        start(lists3)
        wait(second)
        wait(lists3)


def forward(kernel, ins, in_specs, scale, emb, half, vb, width, outs=(), scratch=(), cid=None):
    vocab, dim = emb.shape
    nb = half // vb
    ccols = dim // 4
    return pl.pallas_call(
        functools.partial(kernel, vocab, half),
        out_shape=[shape(half, width), shape(SUB, width), shape(SUB, width), shape(width, ccols, BF16)] + [o for o, _ in outs],
        grid=(nb,),
        in_specs=in_specs + [one_row(dim), pl.BlockSpec((vb, dim), lambda i: (lax.axis_index('core') * nb + i, 0))],
        out_specs=[by_row(vb, width), fixed(SUB, width), fixed(SUB, width), fixed(width, ccols)] + [o for _, o in outs],
        scratch_shapes=[pltpu.VMEM((dim, width), BF16), *scratch],
        compiler_params=(params if cid is None else functools.partial(comm, cid))(dimension_semantics=ORDERED),
        cost_estimate=cost(2.0 * half * width * dim, half * dim * 2 + half * width * 4 + width * dim * 4, half * width),
    )(*ins, scale, emb)


def tokens_scratch(n, dim):
    return [pltpu.VMEM((2, n, dim), F32)] * 2


def stats_kernel(tps, xs, order, own, *refs):
    nlist = 2 * len(order)
    lists, refs = refs[:nlist], refs[nlist:]
    nstat = 2 if own else 4
    stat, refs = refs[:nstat], refs[nstat:]
    count_ref, refs = refs[0], refs[1:]
    if own:
        c_ref, w_ref, loss_ref, send, recv, ssem, rsem = refs
    else:
        dw_ref, tz_ref, loss0_ref, c_ref, w_ref, loss_ref, dwsum_ref, send, recv, xsend, xrecv, tsend, trecv, ssem, rsem = refs
    core = lax.axis_index('core')
    me = lax.axis_index('tp') * 2 + core
    spots = [lax.rem(me + j, 2 * tps) for j in range(1, 2 * tps)]
    peers = [{'tp': r // 2, 'core': lax.rem(r, 2)} for r in spots]
    near = [] if own else chip_peers(xs)
    gr = send.shape[0] // 2
    hello(peers + near)

    base = 0
    send[...] = jnp.zeros(send.shape, F32)
    for m_ref, s_ref in zip(stat[::2], stat[1::2]):
        m = jnp.max(m_ref[...], axis=0, keepdims=True)
        s = jnp.sum(s_ref[...] * jnp.exp(m_ref[...] - m), axis=0, keepdims=True)
        put_rows(send, base, m)
        put_rows(send, gr + base, s)
        base += m.shape[1] // LANES
    masks = []
    for chip, cuts in enumerate(order):
        for lanes in cuts:
            a, b = (ref[0:1, lanes] for ref in lists[2 * chip:2 * chip + 2])
            masks += [jnp.where(core == 0, a, b), jnp.where(core == 0, b, a)]
    mask = (jnp.concatenate(masks, axis=1) > 0).astype(F32)
    w = mask / count_ref[:, 0:1]
    w_ref[...] = w

    links = Links(ssem, rsem)
    copies = [links.copy(send, recv.at[k], to) for k, to in enumerate(peers)]
    if not own:
        xsend[...] = jnp.zeros(xsend.shape, F32)
        put_rows(xsend, 0, dw_ref[...])
        tz = functools.reduce(jnp.add, pieces(jnp.sum(tz_ref[...], axis=0, keepdims=True)))
        last = xsend.shape[0] - SUB
        xsend[last:last + 1, :] = tz
        xcopies = [links.copy(xsend, xrecv.at[k], to) for k, to in enumerate(near)]
        tcopies = [links.copy(tsend, trecv.at[j - 1], along('tp', j, tps)) for j in range(1, tps)]
    meet(peers + near)
    start(copies)
    if not own:
        start(xcopies)
        wait(xcopies)
        tsend[...] = xsend[...] + jnp.sum(xrecv[...], axis=0)
    wait(copies)
    if not own:
        start(tcopies)
    mine, theirs = send[:gr, :], recv[:, :gr, :]
    best = jnp.maximum(mine, jnp.max(theirs, axis=0))
    acc = send[gr:, :] * jnp.exp(mine - best) + jnp.sum(recv[:, gr:, :] * jnp.exp(theirs - best[None]), axis=0)
    lse = best + jnp.log(acc)
    lse = jnp.concatenate([lse[g:g + 1, :] for g in range(mask.shape[1] // LANES)], axis=1)
    c_ref[...] = jnp.where(mask > 0, lse - jnp.log(w), BIG)
    loss = functools.reduce(jnp.add, pieces(w * lse))
    if own:
        loss_ref[...] = loss
    else:
        wait(tcopies)
        total = tsend[...] + jnp.sum(trecv[...], axis=0)
        dwsum_ref[...] = jnp.concatenate([total[g:g + 1, :] for g in range(last)], axis=1)
        loss_ref[...] = jnp.sum(loss + loss0_ref[...] - total[last:last + 1, :], axis=1, keepdims=True)


def stats(lists, order, stat, count, tps, xs, cid, adds=()):
    own = not adds
    width = sum(m.shape[1] for m in stat[::2])
    tok = lists[0].shape[1]
    gr = -(-width // (LANES * SUB)) * SUB
    n = 2 * tps - 1
    outs = [line(width), line(width), line(LANES if own else 1)]
    scratch = [pltpu.VMEM((2 * gr, LANES), F32), pltpu.VMEM((n, 2 * gr, LANES), F32)]
    if not own:
        outs.append(shape(*adds[0].shape))
        xr = adds[0].shape[1] // LANES + SUB
        near = 2 * xs - 1
        scratch += [pltpu.VMEM((xr, LANES), F32), pltpu.VMEM((near, xr, LANES), F32),
                    pltpu.VMEM((xr, LANES), F32), pltpu.VMEM((tps - 1, xr, LANES), F32)]
        n += near + tps - 1
    return pl.pallas_call(
        functools.partial(stats_kernel, tps, xs, order, own),
        out_shape=outs,
        grid=(1,),
        in_specs=[fixed(SUB, tok)] * len(lists) + [fixed(*a.shape) for a in (*stat, count, *adds)],
        out_specs=[fixed(*o.shape) for o in outs],
        scratch_shapes=scratch + dmas(n),
        compiler_params=comm(cid),
        cost_estimate=cost(2e9, 1 << 16),
    )(*lists, *stat, count, *adds)


def fill_teacher(cnt_ref, first, nrb, tabr_ref, tabp_ref, w_ref, lists, plan, lane_block, half, tm, src, sem):
    width = tm.shape[1]
    core = lax.axis_index('core')
    rows = iota(LANES, LANES)
    zero = jnp.zeros((LANES, LANES), F32)
    top = src.shape[0] // 2

    def pick(row, val, t):
        for s in range(SUB):
            t = jnp.where(rows == row[s:s + 1, :], val[s:s + 1, :], t)
        return t

    for rb in range(nrb):
        n = cnt_ref[first + rb, 0]
        rs = slice(rb * LANES, (rb + 1) * LANES)

        def tile(g, carry):
            lanes = at(g * LANES, LANES)

            @pl.when(n <= SLOTS)
            def _():
                tm[rs, lanes] = pick(tabr_ref[sub8(rb), lanes], tabp_ref[sub8(rb), lanes], zero)

            @pl.when(n > SLOTS)
            def _():
                which = plan(g, core)
                for a, ref in enumerate(lists):
                    @pl.when(which == a)
                    def _():
                        copy = pltpu.make_async_copy(ref.at[:, at(lane_block(g) * LANES, LANES)], src, sem.at[0])
                        copy.start()
                        copy.wait()
                w = w_ref[:, lanes]

                def entries(k, t):
                    order = local_order(src[at(k * SUB, SUB), :], core, half) - (first + rb) * LANES
                    return pick(order, src[at(top + k * SUB, SUB), :] * w, t)

                tm[rs, lanes] = lax.fori_loop(0, top // SUB, entries, zero)

            return carry

        lax.fori_loop(0, width // LANES, tile, 0)


def g_tile(z_ref, z0, c_ref, cs, rb, tabr_ref, tabp_ref, tm, put):
    c = c_ref[:, cs]
    step = 2 * SUB
    rows = iota(step, TILE)
    slots = range(SUB * rb, SUB * rb + FAST)
    ids = [jnp.broadcast_to(tabr_ref[s:s + 1, cs], (step, TILE)) for s in slots]
    vals = [tabp_ref[s:s + 1, cs] for s in slots]
    for r0 in range(0, LANES, step):
        rs = slice(rb * LANES + r0, rb * LANES + r0 + step)
        z = z_ref[rs, z0:z0 + TILE]
        if tm is None:
            t = jnp.zeros((step, TILE), F32)
            for row, val in zip(ids, vals):
                t = jnp.where(rows + r0 == row, val, t)
        else:
            t = tm[rs, cs]
        put(rs, (jnp.exp(z - c) - t).astype(BF16), t, z)


def most_slots(cnt_ref, first, nrb):
    n = cnt_ref[first, 0]
    for rb in range(1, nrb):
        n = jnp.maximum(n, cnt_ref[first + rb, 0])
    return n


def fill_scratch(vb, width, lists):
    return [pltpu.VMEM((vb, width), F32), pltpu.VMEM((lists[0].shape[0], LANES), F32), pltpu.SemaphoreType.DMA((1,))]


def g_kernel(half, plan, lane_block, cnt_ref, z_ref, c_ref, tabr_ref, tabp_ref, w_ref, *refs):
    lists, (g_ref, gt_ref, tz_ref, tm, src, sem) = refs[:-6], refs[-6:]
    i = step_id()
    vb, width = z_ref.shape
    nrb = vb // LANES

    @pl.when(i == 0)
    def _():
        tz_ref[...] = jnp.zeros(tz_ref.shape, F32)

    slots = most_slots(cnt_ref, i * nrb, nrb)

    def make(full):
        for c0 in range(0, width, TILE):
            cs = slice(c0, c0 + TILE)
            acc = [jnp.zeros((SUB, TILE), F32)]

            def put(rs, g, t, z):
                g_ref[rs, cs] = g
                tz = t * z
                acc[0] = acc[0] + tz[:SUB] + tz[SUB:]

            for rb in range(nrb):
                g_tile(z_ref, c0, c_ref, cs, rb, tabr_ref, tabp_ref, full, put)
                rs = slice(rb * LANES, (rb + 1) * LANES)
                gt_ref[cs, rs] = g_ref[rs, cs].T
            tz_ref[:, cs] += acc[0]

    @pl.when(slots <= FAST)
    def _():
        make(None)

    @pl.when(slots > FAST)
    def _():
        fill_teacher(cnt_ref, i * nrb, nrb, tabr_ref, tabp_ref, w_ref, lists, plan, lane_block, half, tm, src, sem)
        make(tm)


def g_own(cnt, z, c, tables, w, lists, plan, lane_block):
    half, width = z.shape
    vb = WIDE
    trows = vb // LANES * SLOTS

    def row(i, n):
        return (i, 0)

    return pl.pallas_call(
        functools.partial(g_kernel, half, plan, lane_block),
        out_shape=(shape(half, width, BF16), shape(width, half, BF16), shape(SUB, width)),
        grid_spec=pltpu.PrefetchScalarGridSpec(
            num_scalar_prefetch=1,
            grid=(half // vb,),
            in_specs=[pl.BlockSpec((vb, width), row), one_row(width), pl.BlockSpec((trows, width), row),
                      pl.BlockSpec((trows, width), row), one_row(width)] + [ANY] * len(lists),
            out_specs=(pl.BlockSpec((vb, width), row), pl.BlockSpec((width, vb), lambda i, n: (0, i)), fixed(SUB, width)),
            scratch_shapes=fill_scratch(vb, width, lists),
        ),
        compiler_params=params(dimension_semantics=ORDERED),
        cost_estimate=cost(LARGE, half * width * 8, half * width),
        name='g_own',
    )(cnt, z, c, *tables, w, *lists)


def du_kernel(vocab, half, gt_ref, e_ref, out_ref, mine, send, recv, ssem, rsem):
    i = step_id()
    core = lax.axis_index('core')
    rows = core_rows(vocab, half)
    tok = out_ref.shape[0]
    tiles = (last_step() + 1) - 2
    cut = (vocab - half) // TILE * TILE

    @pl.when(i == 0)
    def _():
        hello([other_core()])
        meet([other_core()])

    def copy(k):
        return pltpu.make_async_remote_copy(
            src_ref=send.at[k], dst_ref=recv.at[k], send_sem=ssem.at[k], recv_sem=rsem.at[k],
            device_id=other_core(), device_id_type=MESH)

    @pl.when((i >= 1) & (i <= tiles))
    def _():
        copy(i - 1).start()

    @pl.when(i < tiles)
    def _():
        tail = e_ref[cut:, :]
        tail = jnp.where(iota(*tail.shape) < rows - cut, tail, jnp.zeros((), BF16))

        def part(which):
            g = gt_ref[at(which * tok, tok), :]
            return (jnp.dot(g[:, :cut], e_ref[:cut, :], preferred_element_type=F32)
                    + jnp.dot(g[:, cut:], tail, preferred_element_type=F32))

        send[i] = part(1 - core)
        mine[i] = part(core)

    @pl.when(i >= 2)
    def _():
        copy(i - 2).wait()
        out_ref[...] = mine[i - 2] + recv[i - 2]


def du_call(gt, emb, half):
    vocab, dim = emb.shape
    tok = gt.shape[0] // 2
    tiles = dim // WIDE
    buf = pltpu.VMEM((tiles, tok, WIDE), F32)
    dma = pltpu.SemaphoreType.DMA((tiles,))
    return pl.pallas_call(
        functools.partial(du_kernel, vocab, half),
        out_shape=shape(tok, dim),
        grid=(tiles + 2,),
        in_specs=[fixed(*gt.shape),
                  pl.BlockSpec((half, WIDE), lambda i: (lax.axis_index('core'), jnp.minimum(i, tiles - 1)))],
        out_specs=pl.BlockSpec((tok, WIDE), lambda i: (0, jnp.maximum(i - 2, 0))),
        scratch_shapes=[buf, buf, buf, dma, dma],
        compiler_params=comm(2, dimension_semantics=ORDERED),
        cost_estimate=cost(4.0 * half * tok * dim, half * dim * 2),
        name='grad_u',
    )(gt, emb)


def de_kernel(half, b0, nu, plan, lane_block, cnt_ref, *refs):
    u_refs, refs = refs[:nu], refs[nu:]
    zn_ref, zf_ref, gown_ref, c_ref, tabr_ref, tabp_ref, w_ref = refs[:7]
    lists = refs[7:13]
    out_ref, part_ref, u_ref, g_ref, tm, src, sem = refs[-7:]
    i = step_id()
    vb, mine = gown_ref.shape
    cols = out_ref.shape[1]
    nrb = vb // LANES
    first = (b0 + i) * nrb

    @pl.when(i == 0)
    def _():
        base = 0
        for ref in u_refs:
            u_ref[base:base + ref.shape[0], :] = ref[...]
            base += ref.shape[0]

    def make(full):
        acc = jnp.dot(gown_ref[...], u_ref[:mine, :], preferred_element_type=F32)
        c0 = 0
        for z_ref in (zn_ref, zf_ref):
            for z0 in range(0, z_ref.shape[1], TILE):
                cs = slice(c0, c0 + TILE)

                def put(rs, g, t, z):
                    g_ref[rs, cs] = g

                for rb in range(nrb):
                    g_tile(z_ref, z0, c_ref, cs, rb, tabr_ref, tabp_ref, full, put)
                acc = acc + jnp.dot(g_ref[:, cs], u_ref[mine + c0:mine + c0 + TILE, :], preferred_element_type=F32)
                c0 += TILE
        out_ref[...] = acc[:, :cols]
        part_ref[...] = acc[:, cols:]

    slots = most_slots(cnt_ref, first, nrb)

    @pl.when(slots <= FAST)
    def _():
        make(None)

    @pl.when(slots > FAST)
    def _():
        fill_teacher(cnt_ref, first, nrb, tabr_ref, tabp_ref, w_ref, lists, plan, lane_block, half, tm, src, sem)
        make(tm)


def de_call(cnt, us, zn, zf, gown, c, tables, w, lists, plan, lane_block, vocab, b0, nb, prev):
    half, mine = gown.shape
    ccols = us[0].shape[1]
    cols = ccols // 2
    tot = half // TILE
    width = zn.shape[1] + zf.shape[1]
    trows = TILE // LANES * SLOTS

    def rows(cols_, height=TILE):
        return pl.BlockSpec((height, cols_), lambda i, n: (b0 + i, 0))

    in_specs = [fixed(*u.shape) for u in us]
    in_specs += [rows(zn.shape[1]), rows(zf.shape[1]), rows(mine), one_row(width), rows(width, trows), rows(width, trows),
                 one_row(width)] + [ANY] * len(lists)
    args = [*us, zn, zf, gown, c, *tables, w, *lists]
    aliases = {}
    if prev is not None:
        aliases = {1 + len(args): 0}
        args.append(prev)
        in_specs.append(ANY)
    return pl.pallas_call(
        functools.partial(de_kernel, half, b0, len(us), plan, lane_block),
        out_shape=(shape(vocab, cols), shape(nb * TILE, cols)),
        grid_spec=pltpu.PrefetchScalarGridSpec(
            num_scalar_prefetch=1,
            grid=(nb,),
            in_specs=in_specs,
            out_specs=(
                pl.BlockSpec((TILE, cols), lambda i, n: (lax.axis_index('core') * tot + b0 + i, 0)),
                pl.BlockSpec((TILE, cols), lambda i, n: (i, 0)),
            ),
            scratch_shapes=[pltpu.VMEM((width + mine, ccols), BF16), pltpu.VMEM((TILE, width), BF16),
                            *fill_scratch(TILE, width, lists)],
        ),
        input_output_aliases=aliases,
        compiler_params=params(dimension_semantics=ORDERED),
        cost_estimate=cost(3.0 * nb * TILE * (width + mine) * ccols, nb * TILE * (width * 4 + mine * 2 + ccols * 4),
                           nb * TILE * width),
    )(cnt, *args)


def place_kernel(half_blocks, a_ref, b_ref, prev_ref, out_ref):
    i = step_id()
    for k, ref in enumerate((a_ref, b_ref)):
        @pl.when(i // half_blocks == k)
        def _():
            out_ref[...] = ref[...]


def place(recvs, out, half):
    cols = out.shape[1]
    step = 2 * WIDE
    n = recvs[0].shape[0] // step
    return pl.pallas_call(
        functools.partial(place_kernel, n),
        out_shape=shape(*out.shape),
        grid=(2 * n,),
        in_specs=[pl.BlockSpec((step, cols), lambda i: (jnp.minimum(i, n - 1), 0)),
                  pl.BlockSpec((step, cols), lambda i: (jnp.maximum(i - n, 0), 0)), ANY],
        out_specs=pl.BlockSpec((step, cols), lambda i: ((1 - lax.axis_index('core')) * (half // step) + i, 0)),
        input_output_aliases={2: 0},
        compiler_params=params(),
        cost_estimate=cost(SMALL, out.size * 4),
        name='place',
    )(*recvs, out)


def dh_kernel(d_ref, inv_ref, out_ref):
    out_ref[...] = (inv_ref[...] * d_ref[...]).astype(BF16)


def dh_call(d, inv):
    tok, dim = d.shape
    step = tok // 4
    return pl.pallas_call(
        dh_kernel,
        out_shape=shape(tok, dim, BF16),
        grid=(tok // step,),
        in_specs=[by_row(step, dim), by_row(step, 1)],
        out_specs=by_row(step, dim),
        compiler_params=params(),
        cost_estimate=cost(SMALL, tok * dim * 6),
        name='grad_h',
    )(d, inv)


def solution(mesh):
    tps = mesh.shape['tp']
    xs = mesh.shape['dp'] // 2
    n = round(tps ** 0.5)
    grid = Mesh(np.asarray(mesh.devices).reshape(tps, xs, 2), ('tp', 'x', 'core'))

    def shift(x, axis, by):
        size = grid.shape[axis]
        return lax.ppermute(x, axis, [(i, (i + by) % size) for i in range(size)])

    def local_head(hidden, embedding, norm_weight, teach_ids, teach_prob, tok_mask):
        vocab, dim = embedding.shape
        tok = hidden.shape[0]
        chip = 2 * tok
        half = -(-vocab // (2 * WIDE)) * WIDE
        part = tok // tps
        cut = tok // 2
        tg = tok // LANES
        scale = (1.0 + norm_weight).reshape(row_of(norm_weight))
        mask = tok_mask.reshape(row_of(tok_mask))

        normed, inv_rms, count = norm(hidden, mask, xs)
        left = shift(normed, 'x', 1)
        right = shift(normed, 'x', -1)
        lists, y_part, l_part = sort_lists(teach_ids, teach_prob, mask, normed, vocab, vocab * tps)

        z0, m0, s0, u0 = forward(own_kernel, [normed, y_part], [fixed(tok, dim)] * 2, scale, embedding, half, 2 * WIDE,
                                 chip)
        full = slice(tok)
        lo, hi = slice(cut), slice(cut, tok)
        c0, w0, loss0 = stats([lists, l_part], ((full,),), (m0, s0), count, tps, xs, 0)
        own_plan = (lambda g, c: lax.rem(g // tg + c, 2)), (lambda g: lax.rem(g, tg))
        tab0, cnt0 = expand([lists, l_part], *own_plan, w0, vocab, half)
        g0, gt0, tz = g_own(cnt0, z0, c0, tab0, w0, [lists, l_part], *own_plan)
        du = du_call(gt0, embedding, half)

        my_normed = lax.dynamic_slice(normed, (lax.axis_index('tp') * part, 0), (part, dim))
        square = pltpu.VMEM((n, n, part, dim // 2), F32)
        strip = pltpu.VMEM((n, part, dim // 2), F32)
        short = pltpu.VMEM((n - 1, part, dim // 2), F32)
        dma = pltpu.SemaphoreType.DMA
        z1, m1, s1, u1, far0, far1, d_rest, dw = forward(
            functools.partial(near_kernel, xs, n), [left, right, du.reshape(n, n, part, dim), my_normed],
            [ANY] * 3 + [fixed(part, dim)], scale, embedding, half, WIDE, 2 * chip,
            outs=[(shape(cut, dim), ANY)] * 2 + [(shape(part, dim), fixed(part, dim)), (line(dim), one_row(dim))],
            scratch=[*tokens_scratch(tok, dim), square, square, strip, strip, short, short, dma((4,)),
                     *dmas(4 + 4 * (n - 1))], cid=3)
        one = (shape(*lists.shape), ANY)
        z2, m2, s2, u2, dh, *l_rest = forward(
            functools.partial(far_kernel, xs, n), [far0, far1, lists, d_rest], [ANY] * 3 + [fixed(part, dim)],
            scale, embedding, half, WIDE, chip,
            outs=[(jax.ShapeDtypeStruct((n, n, part, dim), F32), ANY)] + [one] * 6,
            scratch=[*tokens_scratch(cut, dim), dma((3,)), *dmas(9 + 4 * (n - 1))], cid=6)
        c1, w1, loss, dw_sum = stats(l_rest, ((full,), (full,), (lo, hi)), (m1, s1, m2, s2), count, tps, xs, 1,
                                     (dw, tz, loss0))

        def plan(g, c):
            far = g // (2 * tg) == 2
            swap = jnp.where(far, lax.rem(g, 2), lax.rem(g // tg, 2))
            return g // (2 * tg) * 2 + lax.rem(swap + c, 2)

        def lane_block(g):
            return jnp.where(g // (2 * tg) == 2, lax.rem(g // 2, tg), lax.rem(g, tg))

        rest_plan = plan, lane_block
        tab1, cnt1 = expand(l_rest, *rest_plan, w1, vocab, half)

        nb = half // TILE
        n0 = nb // 2

        def grad_e(b0, count_, prev):
            return de_call(cnt1, [u0, u1, u2], z1, z2, g0, c1, tab1, w1, l_rest, *rest_plan, vocab, b0, count_, prev)

        out, send0 = grad_e(0, n0, None)
        recv0 = shift(send0, 'core', 1)
        out, send1 = grad_e(n0, nb - n0, out)
        recv1 = shift(send1, 'core', 1)
        grad_hidden = dh_call(dh.reshape(tok, dim), inv_rms)
        out = place([recv0, recv1], out, half)
        return loss.reshape(()), grad_hidden, out, dw_sum.reshape(dim)

    tokens = ('x', 'core')
    return jax.shard_map(
        local_head,
        mesh=grid,
        in_specs=(P(tokens, None), P('tp', None), P(None), P(tokens, None), P(tokens, None), P(tokens)),
        out_specs=(P(), P(tokens, None), P('tp', tokens), P(None)),
        check_vma=False,
    )
```

time: 349 us -> 239 us (0.68)
  waiting for transfers between devices: 66.6 us -> 3.31 us
  starting transfers between devices: 36.2 us -> 3.78 us
  other arithmetic: 9.29 us -> 0.6 us
  local copies, waits for them, and re-layouts: 9.38 us -> 3.48 us
  Pallas kernels: 219 us -> 224 us
    ppermute x33 -> x4, waiting for transfers between devices: 66.6 us -> 3.31 us  [shift(): return lax.ppermute(x, axis, [(i, (i + by) % size) for i in range(size)])]
    ppermute x33 -> x4, starting transfers between devices: 36.2 us -> 3.78 us  [shift(): return lax.ppermute(x, axis, [(i, (i + by) % size) for i in range(size)])]
    pallas_call x12, Pallas kernels: 158 us -> 175 us  [the longest x3 91.9 us: forward(): pl.pallas_call(functools.partial(kernel, vocab, half), out_shape=[shape(h...]
    pallas_call x2, Pallas kernels: 44.4 us -> 32.5 us  [stats(): pl.pallas_call(functools.partial(stats_kernel, tps, xs, order, own), out_...]
    reduce_sum x4 -> x0, other arithmetic: 4.56 us -> none  [the longest x3 3.05 us: local_head(): loss_mean = jnp.sum(loss0) + jnp.sum(loss1) - jnp.sum(sums[dim // LANES])]
    slice x2 -> x0, local copies, waits for them, and re-layouts: 3.6 us -> none  [the longest x1 2.3 us: local_head(): far1 = shift(right[cut:], 'x', -1)]
  transfers between devices with their start and end apart: 33 -> 4, of which waited for: 11 -> 2; matrix products, arithmetic and copies ran while one was open for 3% -> 1% of each run, Pallas kernels for 48% -> 32%
where the time goes in v3:
time: 239 us; the launch traced here: 238 us
  Pallas kernels  224 us (94%)
  starting transfers between devices  3.78 us (2%)
  local copies, waits for them, and re-layouts  3.48 us (1%)
  waiting for transfers between devices  3.31 us (1%)
  between operations  2.54 us (1%)
    pallas_call x3, Pallas kernels, forward(): pl.pallas_call(functools.partial(kernel, vocab, half), out_shape=[shape(h...  91.9 us
    pallas_call x2, Pallas kernels, stats(): pl.pallas_call(functools.partial(stats_kernel, tps, xs, order, own), out_...  32.5 us
    pallas_call x2, Pallas kernels, de_call(): pl.pallas_call(functools.partial(de_kernel, half, b0, len(us), plan, lane...  27 us
    pallas_call x2, Pallas kernels, expand(): pl.pallas_call(functools.partial(expand_kernel, vocab, half, plan, lane_b...  17.2 us
    pallas_call x1, Pallas kernels, du_call(): pl.pallas_call(functools.partial(du_kernel, vocab, half), out_shape=shape...  16.1 us
    pallas_call x1, Pallas kernels, g_own(): pl.pallas_call(functools.partial(g_kernel, half, plan, lane_block), out_s...  11.8 us
    pallas_call x1, Pallas kernels, norm(): pl.pallas_call(functools.partial(norm_kernel, xs), out_shape=(shape(tok,...  9.72 us
    pallas_call x1, Pallas kernels, sort_lists(): pl.pallas_call(functools.partial(sort_kernel, vocab, whole), out_shape=(l...  8.55 us
  transfers between devices with their start and end apart: 4, of which 2 were waited for; matrix products, arithmetic and copies ran while one was open for 1% of the time, Pallas kernels for 32%

profile of v3, /device:TPU:1, one launch (start us, length us, event | category | flops | bytes accessed | tf_op | source)
XLA Modules:
  0.0 237.6 jit_solution(12271462890777013965)
XLA Ops:
  0.6 0.0 copy-start.1
  0.6 9.7 %norm.1 = (f32[256,2048]{1,0:T(8,128)}, f32[256,1]{1,0:T(8,128)}, f32[1,128]{1,0:T(1,128)}) custom-call(bf16[256,2048]{1,0:T(8,128)(2,1)} %h_ref.1, f32[1,256]{1,0:T(1,128)} %bitcast.12), custom_call_target="tpu_custom_call" | custom-call | flops 1000000000 | bytes 3145728 | tf_op jit(solution)/shard_map/norm/pallas_call | solution.py:170
  10.4 1.8 collective-permute-start.1
  12.2 0.0 collective-permute-start
  12.2 0.0 copy-done.1
  12.2 0.6 broadcast_add_fusion
  12.8 8.6 %sort_lists.1 = (f32[512,256]{1,0:T(8,128)}, f32[256,2048]{1,0:T(8,128)}, f32[512,256]{1,0:T(8,128)}) custom-call(s32[256,256]{1,0:T(8,128)} %ids_ref.1, f32[256,256]{1,0:T(8,128)} %pt_ref.1, f32[1,256]{1,0:T(1,128)} %bitcast.13, f32[256,2048]{1,0:T(8,128)} %get-tuple-element.53.y_hbm.y_ref), custom_call_target="tpu_custom_call" | custom-call | flops 4000000000 | bytes 1048576 | tf_op jit(solution)/shard_map/sort_lists/pallas_call | solution.py:240
  21.4 16.7 %shard_map.93 = (f32[4096,512]{1,0:T(8,128)}, f32[8,512]{1,0:T(8,128)}, f32[8,512]{1,0:T(8,128)}, bf16[512,512]{1,0:T(8,128)(2,1)}) custom-call(f32[256,2048]{1,0:T(8,128)} %get-tuple-element.53.y_hbm.y_ref, f32[256,2048]{1,0:T(8,128)} %get-tuple-element.56.ypart_ref, f32[1,2048]{1,0:T(1,128)} %bitcast.8, bf16[8016,2048]{1,0:T(8,128)(2,1)} %e_ref.7), custom_call_target="tpu_custom_call" | custom-call | flops 8589934592 | bytes 29360128 | tf_op jit(solution)/shard_map/pallas_call | solution.py:575
  38.0 13.7 %shard_map.94 = (f32[1,512]{1,0:T(1,128)}, f32[1,512]{1,0:T(1,128)}, f32[1,128]{1,0:T(1,128)}) custom-call(f32[512,256]{1,0:T(8,128)} %get-tuple-element.54.refs_0_.lists, f32[512,256]{1,0:T(8,128)} %get-tuple-element.55.refs_1_, f32[8,512]{1,0:T(8,128)} %get-tuple-element.57.refs_2_, f32[8,512]{1,0:T(8,128)} %get-tuple-element.58.refs_3_, ...), custom_call_target="tpu_custom_call" | custom-call | flops 2000000000 | bytes 65536 | tf_op jit(solution)/shard_map/pallas_call | solution.py:676
  51.7 5.4 %shard_map.95 = (s32[256,512]{1,0:T(8,128)}, f32[256,512]{1,0:T(8,128)}, s32[32,128]{1,0:T(8,128)}) custom-call(f32[512,256]{1,0:T(8,128)} %get-tuple-element.54.refs_0_.lists, f32[512,256]{1,0:T(8,128)} %get-tuple-element.55.refs_1_, f32[1,512]{1,0:T(1,128)} %get-tuple-element.60.refs_2_.w_ref), custom_call_target="tpu_custom_call" | custom-call | flops 400000000 | bytes 2097152 | tf_op jit(solution)/shard_map/pallas_call | solution.py:362
  57.2 1.6 constant_dynamic-slice_fusion.ysl_ref
  58.7 11.8 %g_own.1 = (bf16[4096,512]{1,0:T(8,128)(2,1)}, bf16[512,4096]{1,0:T(8,128)(2,1)}, f32[8,512]{1,0:T(8,128)}) custom-call(s32[32,128]{1,0:T(8,128)} %get-tuple-element.61.cnt_ref, f32[4096,512]{1,0:T(8,128)} %get-tuple-element.62.z_ref, f32[1,512]{1,0:T(1,128)} %get-tuple-element.63.c_ref, s32[256,512]{1,0:T(8,128)} %get-tuple-element.64.tabr_ref, ...), custom_call_target="tpu_custom_call" | custom-call | flops 4000000000 | bytes 16777216 | tf_op jit(solution)/shard_map/g_own/pallas_call | solution.py:809
  70.6 16.1 %grad_u.1 = f32[256,2048]{1,0:T(8,128)} custom-call(bf16[512,4096]{1,0:T(8,128)(2,1)} %get-tuple-element.66.gt_ref, bf16[8016,2048]{1,0:T(8,128)(2,1)} %e_ref.7), custom_call_target="tpu_custom_call" | custom-call | flops 8589934592 | bytes 16777216 | tf_op jit(solution)/shard_map/grad_u/pallas_call | solution.py:873
  86.7 0.0 collective-permute-done.1.right
  86.7 0.0 copy-start.3
  86.7 0.0 collective-permute-done.left
  86.8 1.3 copy-done.3
  88.1 40.6 %shard_map.96 = (f32[4096,1024]{1,0:T(8,128)}, f32[8,1024]{1,0:T(8,128)}, f32[8,1024]{1,0:T(8,128)}, bf16[1024,512]{1,0:T(8,128)(2,1)}, f32[128,2048]{1,0:T(8,12...) custom-call(f32[256,2048]{1,0:T(8,128)} %collective-permute-done.left, f32[256,2048]{1,0:T(8,128)} %copy-done.3, ...), custom_call_target="tpu_custom_call" | custom-call | flops 17179869184 | bytes 41943040 | tf_op jit(solution)/shard_map/pallas_call | solution.py:575
  128.6 34.7 %shard_map.97 = (f32[4096,512]{1,0:T(8,128)}, f32[8,512]{1,0:T(8,128)}, f32[8,512]{1,0:T(8,128)}, bf16[512,512]{1,0:T(8,128)(2,1)}, f32[4,4,16,2048]{3,2,1,0:T(8...) custom-call(f32[128,2048]{1,0:T(8,128)} %get-tuple-element.67.far0, ...), custom_call_target="tpu_custom_call" | custom-call | flops 8589934592 | bytes 29360128 | tf_op jit(solution)/shard_map/pallas_call | solution.py:575
  163.4 18.8 %shard_map.98 = (f32[1,1536]{1,0:T(1,128)}, f32[1,1536]{1,0:T(1,128)}, f32[1,1]{1,0:T(1,128)}, f32[1,2048]{1,0:T(1,128)}) custom-call(f32[512,256]{1,0:T(8,128)} %get-tuple-element.70.refs_0_.refs_10_, f32[512,256]{1,0:T(8,128)} %get-tuple-element.71.refs_1_.refs_11_, f32[512,256]{1,0:T(8,128)} %get-tuple-element.72.refs_2_.refs_12_, ...), custom_call_target="tpu_custom_call" | custom-call | flops 2000000000 | bytes 65536 | tf_op jit(solution)/shard_map/pallas_call | solution.py:676
  182.2 11.8 %shard_map.99 = (s32[256,1536]{1,0:T(8,128)}, f32[256,1536]{1,0:T(8,128)}, s32[32,128]{1,0:T(8,128)}) custom-call(f32[512,256]{1,0:T(8,128)} %get-tuple-element.70.refs_0_.refs_10_, f32[512,256]{1,0:T(8,128)} %get-tuple-element.71.refs_1_.refs_11_, f32[512,256]{1,0:T(8,128)} %get-tuple-element.72.refs_2_.refs_12_, ...), custom_call_target="tpu_custom_call" | custom-call | flops 1200000000 | bytes 6291456 | tf_op jit(solution)/shard_map/pallas_call | solution.py:362
  194.0 13.5 %shard_map.100 = (f32[8016,256]{1,0:T(8,128)}, f32[2048,256]{1,0:T(8,128)}) custom-call(s32[32,128]{1,0:T(8,128)} %get-tuple-element.87.cnt_ref, bf16[512,512]{1,0:T(8,128)(2,1)} %get-tuple-element.88.refs_0_, bf16[1024,512]{1,0:T(8,128)(2,1)} %get-tuple-element.89.refs_1_, bf16[512,512]{1,0:T(8,128)(2,1)} %get-tuple-element.90.refs_2_, ...), custom_call_target="tpu_custom_call" | custom-call | flops 6442450944 | bytes 18874368 | tf_op jit(solution)/shard_map/pallas_call | solution.py:954
  207.5 13.5 %shard_map.101 = (f32[8016,256]{1,0:T(8,128)}, f32[2048,256]{1,0:T(8,128)}) custom-call(s32[32,128]{1,0:T(8,128)} %get-tuple-element.87.cnt_ref, bf16[512,512]{1,0:T(8,128)(2,1)} %get-tuple-element.88.refs_0_, bf16[1024,512]{1,0:T(8,128)(2,1)} %get-tuple-element.89.refs_1_, ...), custom_call_target="tpu_custom_call", output_to_operand_aliasing={{0}: (17, {})} | custom-call | flops 6442450944 | bytes 18874368 | tf_op jit(solution)/shard_map/pallas_call | solution.py:954
  221.0 1.9 collective-permute-start.3
  222.8 0.1 collective-permute-start.2
  222.9 3.7 %grad_h.1 = bf16[256,2048]{1,0:T(8,128)(2,1)} custom-call(f32[256,2048]{1,0:T(8,128)} %bitcast.7, f32[256,1]{1,0:T(8,128)} %get-tuple-element.85.inv_ref), custom_call_target="tpu_custom_call" | custom-call | flops 100000000 | bytes 3145728 | tf_op jit(solution)/shard_map/grad_h/pallas_call | solution.py:1008
  226.7 0.2 collective-permute-done.3.b_ref
  226.8 0.0 copy-start
  226.8 3.1 %collective-permute-done.2.a_ref = f32[2048,256]{1,0:T(8,128)} collective-permute-done((f32[2048,256]{1,0:T(8,128)}, f32[2048,256]{1,0:T(8,128)}, u32[]{:S(2)}, u32[]{:S(2)}) %collective-permute-start.2) | collective-permute-done | bytes 2097184 | tf_op jit(solution)/shard_map/ppermute | solution.py:1028
  230.0 0.0 copy-done
  230.0 0.0 copy-start.2
  230.0 5.3 %place.1 = f32[8016,256]{1,0:T(8,128)} custom-call(f32[2048,256]{1,0:T(8,128)} %collective-permute-done.2.a_ref, f32[2048,256]{1,0:T(8,128)} %copy-done, f32[8016,256]{1,0:T(8,128)} %get-tuple-element.100.prev_ref), custom_call_target="tpu_custom_call", output_to_operand_aliasing={{}: (2, {})} | custom-call | flops 100000000 | bytes 8208384 | tf_op jit(solution)/shard_map/place/pallas_call | solution.py:987
  235.9 0.0 copy-done.2
  235.9 0.6 copy.17
Async XLA Ops:
  0.6 11.6 %copy-start.1 = (f32[2048]{0:T(1024)S(1)}, f32[2048]{0:T(1024)}, u32[]{:S(2)}) copy-start(f32[2048]{0:T(1024)} %param.8) | copy-start | bytes 24580
  10.4 76.4 %collective-permute-start.1 = (f32[256,2048]{1,0:T(8,128)}, f32[256,2048]{1,0:T(8,128)S(1)}, u32[]{:S(2)}, u32[]{:S(2)}) collective-permute-start(f32[256,2048]{1,0:T(8,128)} %get-tuple-element.53.y_hbm.y_ref), channel_id=1, source_target_pairs={{0,6},{2,0},{4,2},{6,4},{1,7},{3,1},{5,3},{7,5},{8,14},{10,8},{12,... | collective-permute-start | bytes 6291464 | tf_op jit(solution)/shard_map/ppermute | solution.py:1028
  12.2 74.6 %collective-permute-start = (f32[256,2048]{1,0:T(8,128)}, f32[256,2048]{1,0:T(8,128)}, u32[]{:S(2)}, u32[]{:S(2)}) collective-permute-start(f32[256,2048]{1,0:T(8,128)} %get-tuple-element.53.y_hbm.y_ref), channel_id=1, source_target_pairs={{0,2},{2,4},{4,6},{6,0},{1,3},{3,5},{5,7},{7,1},{8,10},{10,12},{12... | collective-permute-start | bytes 6291464 | tf_op jit(solution)/shard_map/ppermute | solution.py:1028
  86.7 1.3 copy-start.3
  221.0 5.9 %collective-permute-start.3 = (f32[2048,256]{1,0:T(8,128)}, f32[2048,256]{1,0:T(8,128)S(1)}, u32[]{:S(2)}, u32[]{:S(2)}) collective-permute-start(f32[2048,256]{1,0:T(8,128)} %get-tuple-element.99), channel_id=1, source_target_pairs={{0,1},{1,0},{2,3},{3,2},{4,5},{5,4},{6,7},{7,6},{8,9},{9,8},{10,11... | collective-permute-start | bytes 6291464 | tf_op jit(solution)/shard_map/ppermute | solution.py:1028
  222.8 7.1 %collective-permute-start.2 = (f32[2048,256]{1,0:T(8,128)}, f32[2048,256]{1,0:T(8,128)}, u32[]{:S(2)}, u32[]{:S(2)}) collective-permute-start(f32[2048,256]{1,0:T(8,128)} %get-tuple-element.97), channel_id=1, source_target_pairs={{0,1},{1,0},{2,3},{3,2},{4,5},{5,4},{6,7},{7,6},{8,9},{9,8},{10,11... | collective-permute-start | bytes 6291464 | tf_op jit(solution)/shard_map/ppermute | solution.py:1028
  226.8 3.1 %copy-start = (f32[2048,256]{1,0:T(8,128)}, f32[2048,256]{1,0:T(8,128)S(1)}, u32[]{:S(2)}) copy-start(f32[2048,256]{1,0:T(8,128)S(1)} %collective-permute-done.3.b_ref) | copy-start | bytes 6291460
  230.0 5.9 %copy-start.2 = (f32[1,2048]{1,0:T(1,128)S(1)}, f32[1,2048]{1,0:T(1,128)}, u32[]{:S(2)}) copy-start(f32[1,2048]{1,0:T(1,128)} %get-tuple-element.101) | copy-start | bytes 24580

commit v4 on v3

--- a/solution.py
+++ b/solution.py
@@ -24,7 +24,7 @@
 VMEM_LIMIT = 60 * 1024 * 1024
 MESH = pl.DeviceIdType.MESH
 VMEM = pl.BlockSpec(memory_space=pltpu.VMEM)
-ANY = pl.BlockSpec(memory_space=pl.ANY)
+ANY = pl.BlockSpec(memory_space=pltpu.HBM)
 
 
 def params(**kw):
@@ -139,6 +139,18 @@
     return [x[:, g * LANES:(g + 1) * LANES] for g in range(x.shape[1] // LANES)]
 
 
+def to_row(x, rows):
+    return jnp.concatenate([x[g:g + 1, :] for g in range(rows)], axis=1)
+
+
+def total(ref):
+    return jnp.sum(ref[...], axis=0)
+
+
+def zeros(ref, dtype=F32):
+    return jnp.zeros(ref.shape, dtype)
+
+
 def put_rows(ref, base, x):
     for g, piece in enumerate(pieces(x)):
         ref[base + g:base + g + 1, :] = piece
@@ -147,21 +159,23 @@
 def norm_kernel(xs, h_ref, mask_ref, y_ref, inv_ref, count_ref, send, recv, ssem, rsem):
     peers = chip_peers(xs)
     hello(peers)
-    send[...] = jnp.zeros(send.shape, F32)
+    send[...] = zeros(send)
     put_rows(send, 0, mask_ref[...])
-    for r0 in range(0, h_ref.shape[0], LANES):
-        rs = slice(r0, r0 + LANES)
+    links = Links(ssem, rsem)
+    copies = [links.copy(send, recv.at[k], to) for k, to in enumerate(peers)]
+    half = h_ref.shape[0] // 2
+    for r0 in (0, half):
+        rs = slice(r0, r0 + half)
         h = h_ref[rs, :].astype(F32)
         inv = lax.rsqrt(jnp.mean(h * h, axis=1, keepdims=True) + EPS_NORM)
         inv_ref[rs, :] = inv
         y_ref[rs, :] = h * inv
-    meet(peers)
-    links = Links(ssem, rsem)
-    copies = [links.copy(send, recv.at[k], to) for k, to in enumerate(peers)]
-    start(copies)
+        if r0 == 0:
+            meet(peers)
+            start(copies)
     wait(copies)
-    total = send[...] + jnp.sum(recv[...], axis=0)
-    count_ref[...] = jnp.broadcast_to(jnp.sum(total, keepdims=True), count_ref.shape)
+    both = send[...] + total(recv)
+    count_ref[...] = jnp.broadcast_to(jnp.sum(both, keepdims=True), count_ref.shape)
 
 
 def norm(hidden, mask, xs):
@@ -179,10 +193,10 @@
     )(hidden, mask)
 
 
-def sort_kernel(vocab, whole, ids_ref, pt_ref, mask_ref, y_hbm, out_ref, ypart_hbm, lpart_hbm, ssem, rsem):
+def sort_kernel(vocab, whole, ids_ref, pt_ref, mask_ref, y_hbm, out_ref, ypart_hbm, ssem, rsem):
     links = Links(ssem, rsem)
     to = other_core()
-    y_copy, l_copy = links.copy(y_hbm, ypart_hbm, to), links.copy(out_ref, lpart_hbm, to)
+    y_copy = links.copy(y_hbm, ypart_hbm, to)
     hello([to])
     meet([to])
     y_copy.start()
@@ -230,8 +244,6 @@
             out_ref[sub8(a), cols] = k[a] * sign
             out_ref[sub8(nv + a), cols] = p[a]
     y_copy.wait()
-    l_copy.start()
-    l_copy.wait()
 
 
 def sort_lists(ids, prob, mask, y, vocab, whole):
@@ -239,11 +251,11 @@
     lists = shape(2 * top, tokens)
     return pl.pallas_call(
         functools.partial(sort_kernel, vocab, whole),
-        out_shape=(lists, shape(*y.shape), lists),
+        out_shape=(lists, shape(*y.shape)),
         in_specs=[VMEM] * 3 + [ANY],
-        out_specs=(VMEM, ANY, ANY),
-        scratch_shapes=dmas(2),
-        compiler_params=comm(5),
+        out_specs=(VMEM, ANY),
+        scratch_shapes=dmas(1),
+        compiler_params=comm(7),
         cost_estimate=cost(LARGE, tokens * top * 16),
         name='sort_lists',
     )(ids, prob, mask, y)
@@ -280,7 +292,7 @@
 
     @pl.when(g == 0)
     def _():
-        cnt_ref[...] = jnp.zeros(cnt_ref.shape, I32)
+        cnt_ref[...] = zeros(cnt_ref, I32)
         for k in range(src.shape[0]):
             fetch(k)
 
@@ -373,14 +385,27 @@
     return (tabr, tabp), cnt
 
 
-def put_tokens(y_ref, dest, scale_ref, ut_ref, u_ref):
+def put_tokens(y_ref, dest, w_ref, ut_ref, u_ref):
     here = at(dest, y_ref.shape[0])
     cols = u_ref.shape[1] // 2
-    ut_ref[:, here] = (y_ref[...] * scale_ref[...]).astype(BF16).T
+    ut_ref[:, here] = (y_ref[...] * (1 + w_ref[...])).astype(BF16).T
     core = lax.axis_index('core')
     for k, c in enumerate((core, 1 - core)):
         mine = at((2 * lax.axis_index('x') + c) * cols, cols)
-        u_ref[here, k * cols:(k + 1) * cols] = (y_ref[:, mine] * scale_ref[:, mine]).astype(BF16)
+        u_ref[here, k * cols:(k + 1) * cols] = (y_ref[:, mine] * (1 + w_ref[:, mine])).astype(BF16)
+
+
+class Tokens:
+    def __init__(self, srcs, buf, sem):
+        self.buf = buf
+        self.copies = [pltpu.make_async_copy(src, buf.at[k], sem.at[k]) for k, src in enumerate(srcs)]
+
+    def place(self, *refs):
+        core = lax.axis_index('core')
+        n = self.buf.shape[1]
+        for k, copy in enumerate(self.copies):
+            copy.wait()
+            put_tokens(self.buf.at[k], (k // 2 * 2 + (1 - core if k % 2 else core)) * n, *refs)
 
 
 def tiles(vocab, half, e_ref, ut_ref, z_ref, m_ref, s_ref):
@@ -391,7 +416,7 @@
     @pl.when(i == 0)
     def _():
         m_ref[...] = jnp.full(m_ref.shape, NEG, F32)
-        s_ref[...] = jnp.zeros(s_ref.shape, F32)
+        s_ref[...] = zeros(s_ref)
 
     for r0 in range(0, vb, TILE):
         rs = slice(r0, r0 + TILE)
@@ -408,15 +433,23 @@
             s_ref[:, cs] = s_ref[:, cs] * jnp.exp(old - new) + jnp.sum(jnp.exp(z3 - new[None]), axis=0)
 
 
-def own_kernel(vocab, half, y_ref, ypart_ref, scale_ref, e_ref, z_ref, m_ref, s_ref, u_ref, ut_ref):
+def own_kernel(vocab, half, y, ypart, lists, w_ref, e_ref, z_ref, m_ref, s_ref, u_ref, lpart, ut_ref, buf, lsem, ssem, rsem):
+    swap = [Links(ssem, rsem).copy(lists, lpart, other_core())]
+
     @pl.when(step_id() == 0)
     def _():
-        tok = y_ref.shape[0]
-        core = lax.axis_index('core')
-        put_tokens(y_ref, core * tok, scale_ref, ut_ref, u_ref)
-        put_tokens(ypart_ref, (1 - core) * tok, scale_ref, ut_ref, u_ref)
+        tokens = Tokens((y, ypart), buf, lsem)
+        start(tokens.copies)
+        hello([other_core()])
+        meet([other_core()])
+        start(swap)
+        tokens.place(w_ref, ut_ref, u_ref)
 
     tiles(vocab, half, e_ref, ut_ref, z_ref, m_ref, s_ref)
+
+    @pl.when(step_id() == last_step())
+    def _():
+        wait(swap)
 
 
 class Square:
@@ -434,121 +467,120 @@
     return [along('x', 1, xs), along('x', xs - 1, xs)]
 
 
-def gather_tokens(srcs, own, part, lsem, links):
-    here = [pltpu.make_async_copy(src, own.at[k], lsem.at[k]) for k, src in enumerate(srcs)]
-    there = [links.copy(src, part.at[k], other_core()) for k, src in enumerate(srcs)]
-    return here, there
-
-
-def place_tokens(here, there, own, part, scale_ref, ut_ref, u_ref):
-    n = own.shape[1]
-    core = lax.axis_index('core')
-    wait(here)
-    for k in range(own.shape[0]):
-        put_tokens(own.at[k], (2 * k + core) * n, scale_ref, ut_ref, u_ref)
-    wait(there)
-    for k in range(own.shape[0]):
-        put_tokens(part.at[k], (2 * k + 1 - core) * n, scale_ref, ut_ref, u_ref)
-
-
-def near_kernel(xs, n, vocab, half, left, right, du, ysl_ref, scale_ref, e_ref,
-                z_ref, m_ref, s_ref, u_ref, far0, far1, rest_ref, dw_ref,
-                ut_ref, own, part, a1, b1, sa, sb, a2, b2, lsem, ssem, rsem):
+def near_kernel(xs, n, vocab, half, left, p_left, right, p_right, du, y, l_left, l_right, w_ref, e_ref,
+                z_ref, m_ref, s_ref, u_ref, far0, p_far0, far1, p_far1, p_ll, p_lr, rest_ref, dw_ref,
+                ut_ref, buf, a1, b1, sa, sb, a2, b2, ysl, lsem, ssem, rsem):
     i = step_id()
     sq = Square(n)
     links = Links(ssem, rsem)
-    cut = far0.shape[0]
+    cut, part = far0.shape[0], ysl.shape[0]
     h = du.shape[3] // 2
     ahead, behind = x_peers(xs)
-    here, there = gather_tokens((left, right), own, part, lsem, links)
-    far = [links.copy(left.at[:cut, :], far0, ahead), links.copy(right.at[cut:2 * cut, :], far1, behind)]
+    core = other_core()
+    tokens = Tokens((left, p_left, right, p_right), buf, lsem)
+    far = [links.copy(left.at[:cut, :], far0, ahead), links.copy(right.at[cut:, :], far1, behind)]
+    swap1 = [links.copy(l_left, p_ll, core), links.copy(l_right, p_lr, core)]
+    swap2 = [links.copy(far0, p_far0, core), links.copy(far1, p_far1, core)]
     first, second = [], []
-    for j, (z, y, to_z, to_y) in enumerate(zip(sq.zs, sq.ys, sq.along_z, sq.along_y)):
+    for j, (z, yy, to_z, to_y) in enumerate(zip(sq.zs, sq.ys, sq.along_z, sq.along_y)):
         k = j + 1
-        first.append(links.copy(du.at[:, y, :, :h], a1.at[k], to_y))
-        first.append(links.copy(du.at[z, :, :, h:2 * h], b1.at[k], to_z))
+        first.append(links.copy(du.at[:, yy, :, :h], a1.at[k], to_y))
+        first.append(links.copy(du.at[z, :, :, h:], b1.at[k], to_z))
         second.append(links.copy(sa.at[z], a2.at[j], to_z))
-        second.append(links.copy(sb.at[y], b2.at[j], to_y))
-    mine = [pltpu.make_async_copy(du.at[:, sq.y, :, :h], a1.at[0], lsem.at[2]),
-            pltpu.make_async_copy(du.at[sq.z, :, :, h:2 * h], b1.at[0], lsem.at[3])]
-    peers = [other_core(), ahead, behind, *sq.peers]
+        second.append(links.copy(sb.at[yy], b2.at[j], to_y))
+    mine = [pltpu.make_async_copy(du.at[:, sq.y, :, :h], a1.at[0], lsem.at[4]),
+            pltpu.make_async_copy(du.at[sq.z, :, :, h:], b1.at[0], lsem.at[5]),
+            pltpu.make_async_copy(y.at[at(lax.axis_index('tp') * part, part), :], ysl, lsem.at[6])]
+    peers = [core, ahead, behind, *sq.peers]
 
     @pl.when(i == 0)
     def _():
-        start(here)
+        start(tokens.copies)
         start(mine)
         hello(peers)
         meet(peers)
-        start(there)
         start(first)
         start(far)
-        place_tokens(here, there, own, part, scale_ref, ut_ref, u_ref)
+        start(swap1)
+        tokens.place(w_ref, ut_ref, u_ref)
 
     tiles(vocab, half, e_ref, ut_ref, z_ref, m_ref, s_ref)
 
-    @pl.when(i == (last_step() + 1) - 3)
+    @pl.when(i == last_step() - 2)
     def _():
         wait(mine)
         wait(first)
-        sa[...] = jnp.sum(a1[...], axis=0)
-        sb[...] = jnp.sum(b1[...], axis=0)
-
-    @pl.when(i == (last_step() + 1) - 2)
+        sa[...] = total(a1)
+        sb[...] = total(b1)
+
+    @pl.when(i == last_step() - 1)
     def _():
         start(second)
 
     @pl.when(i == last_step())
     def _():
+        wait(far)
+        start(swap2)
         wait(second)
-        parts = ((sa[sq.z] + jnp.sum(a2[...], axis=0), slice(h)), (sb[sq.y] + jnp.sum(b2[...], axis=0), slice(h, 2 * h)))
+        parts = ((sa[sq.z] + total(a2), slice(h)), (sb[sq.y] + total(b2), slice(h, 2 * h)))
         dot = 0.0
         for du_sum, cs in parts:
-            y = ysl_ref[:, cs]
-            dot = dot + jnp.sum(du_sum * scale_ref[:, cs] * y, axis=1, keepdims=True)
-            dw_ref[:, cs] = jnp.sum(du_sum * y, axis=0, keepdims=True)
+            yv = ysl[:, cs]
+            dot = dot + jnp.sum(du_sum * (1 + w_ref[:, cs]) * yv, axis=1, keepdims=True)
+            dw_ref[:, cs] = jnp.sum(du_sum * yv, axis=0, keepdims=True)
         mean = dot / (2 * h)
         for du_sum, cs in parts:
-            rest_ref[:, cs] = du_sum * scale_ref[:, cs] - ysl_ref[:, cs] * mean
-        wait(far)
-
-
-def far_kernel(xs, n, vocab, half, far0, far1, lists, rest_ref, scale_ref, e_ref,
-               z_ref, m_ref, s_ref, u_ref, dh, l_left, p_left, l_right, p_right, l_far, p_far,
-               ut_ref, own, part, lsem, ssem, rsem):
+            rest_ref[:, cs] = du_sum * (1 + w_ref[:, cs]) - ysl[:, cs] * mean
+        wait(swap1)
+        wait(swap2)
+
+
+def far_kernel(xs, n, vocab, half, far0, p_far0, far1, p_far1, l_left, l_right, rest_ref, dw_ref, tz_ref, w_ref, e_ref,
+               z_ref, m_ref, s_ref, u_ref, dh, l_far, p_lf, dwsum_ref, tzsum_ref,
+               ut_ref, buf, xsend, xrecv, tsend, trecv, lsem, ssem, rsem):
     i = step_id()
     sq = Square(n)
     links = Links(ssem, rsem)
     h = rest_ref.shape[1] // 2
-    rows = lists.shape[0] // 2
+    rows = l_left.shape[0] // 2
     ahead, behind = x_peers(xs)
-    core = other_core()
-    here, there = gather_tokens((far0, far1), own, part, lsem, links)
-    lists1 = [links.copy(lists, l_left, ahead), links.copy(lists, l_right, behind)]
-    lists2 = [links.copy(l_left.at[:rows, :], l_far.at[:rows, :], ahead),
-              links.copy(l_right.at[rows:2 * rows, :], l_far.at[rows:2 * rows, :], behind),
-              links.copy(l_left, p_left, core), links.copy(l_right, p_right, core)]
-    lists3 = [links.copy(l_far, p_far, core)]
-    first, second = [], []
-    a, b = slice(h), slice(h, 2 * h)
+    tokens = Tokens((far0, p_far0, far1, p_far1), buf, lsem)
+    lists = [links.copy(l_left.at[:rows, :], l_far.at[:rows, :], ahead),
+             links.copy(l_right.at[rows:, :], l_far.at[rows:, :], behind)]
+    swap = [links.copy(l_far, p_lf, other_core())]
+    near = chip_peers(xs)
+    everyone = [along('tp', j, n * n) for j in range(1, n * n)]
+    xcopies = [links.copy(xsend, xrecv.at[k], to) for k, to in enumerate(near)]
+    tcopies = [links.copy(tsend, trecv.at[k], to) for k, to in enumerate(everyone)]
     z, y = sq.z, sq.y
+    first, second, third = [], [], []
     for to_z, to_y in zip(sq.along_z, sq.along_y):
-        first.append(links.copy(rest_ref.at[:, a], dh.at[z, y, :, a], to_z))
-        first.append(links.copy(rest_ref.at[:, b], dh.at[z, y, :, b], to_y))
-        second.append(links.copy(dh.at[:, y, :, a], dh.at[:, y, :, a], to_y))
-        second.append(links.copy(dh.at[z, :, :, b], dh.at[z, :, :, b], to_z))
-    mine = [pltpu.make_async_copy(rest_ref, dh.at[z, y], lsem.at[2])]
-    peers = [core, ahead, behind, *sq.peers]
+        first.append(links.copy(rest_ref.at[:, :h], dh.at[z, y, :, :h], to_z))
+        first.append(links.copy(rest_ref.at[:, h:], dh.at[z, y, :, h:], to_y))
+    m = n // 2
+    for to, back, low in ((0, -1, 0), (-1, 0, m)):
+        yb, zb = sq.ys[back], sq.zs[back]
+        second.append(links.copy(dh.at[:, y, :, :h], dh.at[:, y, :, :h], sq.along_y[to]))
+        second.append(links.copy(dh.at[z, :, :, h:], dh.at[z, :, :, h:], sq.along_z[to]))
+        third.append(links.copy(dh.at[low:low + m, yb, :, :h], dh.at[low:low + m, yb, :, :h], sq.along_y[to]))
+        third.append(links.copy(dh.at[zb, low:low + m, :, h:], dh.at[zb, low:low + m, :, h:], sq.along_z[to]))
+    mine = [pltpu.make_async_copy(rest_ref, dh.at[z, y], lsem.at[4])]
+    peers = near + everyone
 
     @pl.when(i == 0)
     def _():
-        start(here)
+        start(tokens.copies)
         start(mine)
         hello(peers)
+        xsend[...] = zeros(xsend)
+        put_rows(xsend, 0, dw_ref[...])
+        last = xsend.shape[0] - SUB
+        xsend[last:last + 1, :] = functools.reduce(jnp.add, pieces(jnp.sum(tz_ref[...], axis=0, keepdims=True)))
         meet(peers)
-        start(there)
         start(first)
-        start(lists1)
-        place_tokens(here, there, own, part, scale_ref, ut_ref, u_ref)
+        start(xcopies)
+        start(lists)
+        tokens.place(w_ref, ut_ref, u_ref)
 
     tiles(vocab, half, e_ref, ut_ref, z_ref, m_ref, s_ref)
 
@@ -557,21 +589,32 @@
         wait(mine)
         wait(first)
         start(second)
+        wait(xcopies)
+        tsend[...] = xsend[...] + total(xrecv)
+
+    @pl.when(i == 3)
+    def _():
+        start(tcopies)
 
     @pl.when(i == last_step())
     def _():
-        wait(lists1)
-        start(lists2)
-        wait(lists2)
-        start(lists3)
+        wait(lists)
+        start(swap)
         wait(second)
-        wait(lists3)
-
-
-def forward(kernel, ins, in_specs, scale, emb, half, vb, width, outs=(), scratch=(), cid=None):
+        start(third)
+        wait(tcopies)
+        both = tsend[...] + total(trecv)
+        last = both.shape[0] - SUB
+        dwsum_ref[...] = to_row(both, last)
+        tzsum_ref[...] = both[last:last + 1, :]
+        wait(swap)
+        wait(third)
+
+
+def forward(kernel, ins, in_specs, scale, emb, half, vb, width, u_cols, cid, outs, scratch):
     vocab, dim = emb.shape
     nb = half // vb
-    ccols = dim // 4
+    ccols = u_cols
     return pl.pallas_call(
         functools.partial(kernel, vocab, half),
         out_shape=[shape(half, width), shape(SUB, width), shape(SUB, width), shape(width, ccols, BF16)] + [o for o, _ in outs],
@@ -579,40 +622,34 @@
         in_specs=in_specs + [one_row(dim), pl.BlockSpec((vb, dim), lambda i: (lax.axis_index('core') * nb + i, 0))],
         out_specs=[by_row(vb, width), fixed(SUB, width), fixed(SUB, width), fixed(width, ccols)] + [o for _, o in outs],
         scratch_shapes=[pltpu.VMEM((dim, width), BF16), *scratch],
-        compiler_params=(params if cid is None else functools.partial(comm, cid))(dimension_semantics=ORDERED),
+        compiler_params=comm(cid, dimension_semantics=ORDERED),
         cost_estimate=cost(2.0 * half * width * dim, half * dim * 2 + half * width * 4 + width * dim * 4, half * width),
     )(*ins, scale, emb)
 
 
-def tokens_scratch(n, dim):
-    return [pltpu.VMEM((2, n, dim), F32)] * 2
-
-
-def stats_kernel(tps, xs, order, own, *refs):
+def merge(m, s, ms, ss):
+    best = jnp.maximum(m, jnp.max(ms, axis=0))
+    return best, s * jnp.exp(m - best) + jnp.sum(ss * jnp.exp(ms - best[None]), axis=0)
+
+
+def stats_kernel(tps, order, *refs):
     nlist = 2 * len(order)
     lists, refs = refs[:nlist], refs[nlist:]
-    nstat = 2 if own else 4
-    stat, refs = refs[:nstat], refs[nstat:]
-    count_ref, refs = refs[0], refs[1:]
-    if own:
-        c_ref, w_ref, loss_ref, send, recv, ssem, rsem = refs
-    else:
-        dw_ref, tz_ref, loss0_ref, c_ref, w_ref, loss_ref, dwsum_ref, send, recv, xsend, xrecv, tsend, trecv, ssem, rsem = refs
+    stat, refs = refs[:-12], refs[-12:]
+    count_ref, c_ref, w_ref, loss_ref, pair, pairr, send, recv, out, outr, ssem, rsem = refs
     core = lax.axis_index('core')
-    me = lax.axis_index('tp') * 2 + core
-    spots = [lax.rem(me + j, 2 * tps) for j in range(1, 2 * tps)]
-    peers = [{'tp': r // 2, 'core': lax.rem(r, 2)} for r in spots]
-    near = [] if own else chip_peers(xs)
-    gr = send.shape[0] // 2
-    hello(peers + near)
-
+    peers = [along('tp', j, tps) for j in range(1, tps)]
+    partner = other_core()
+    everyone = [partner, *peers]
+    hello(everyone)
+    gr = pair.shape[0] // 2
     base = 0
-    send[...] = jnp.zeros(send.shape, F32)
+    pair[...] = zeros(pair)
     for m_ref, s_ref in zip(stat[::2], stat[1::2]):
         m = jnp.max(m_ref[...], axis=0, keepdims=True)
         s = jnp.sum(s_ref[...] * jnp.exp(m_ref[...] - m), axis=0, keepdims=True)
-        put_rows(send, base, m)
-        put_rows(send, gr + base, s)
+        put_rows(pair, base, m)
+        put_rows(pair, gr + base, s)
         base += m.shape[1] // LANES
     masks = []
     for chip, cuts in enumerate(order):
@@ -624,65 +661,46 @@
     w_ref[...] = w
 
     links = Links(ssem, rsem)
+    both = [links.copy(pair, pairr, partner)]
     copies = [links.copy(send, recv.at[k], to) for k, to in enumerate(peers)]
-    if not own:
-        xsend[...] = jnp.zeros(xsend.shape, F32)
-        put_rows(xsend, 0, dw_ref[...])
-        tz = functools.reduce(jnp.add, pieces(jnp.sum(tz_ref[...], axis=0, keepdims=True)))
-        last = xsend.shape[0] - SUB
-        xsend[last:last + 1, :] = tz
-        xcopies = [links.copy(xsend, xrecv.at[k], to) for k, to in enumerate(near)]
-        tcopies = [links.copy(tsend, trecv.at[j - 1], along('tp', j, tps)) for j in range(1, tps)]
-    meet(peers + near)
+    back = [links.copy(out, outr, partner)]
+    meet(everyone)
+    start(both)
+    wait(both)
+    m, s = merge(pair[:gr, :], pair[gr:, :], pairr[:gr, :][None], pairr[gr:, :][None])
+    hg = base // 2
+    mine, mid = slice(hg), slice(SUB, SUB + hg)
+    send[...] = zeros(send)
+    for rows, x in ((mine, m), (mid, s)):
+        send[rows, :] = jnp.where(core == 0, x[:hg, :], x[hg:base, :])
     start(copies)
-    if not own:
-        start(xcopies)
-        wait(xcopies)
-        tsend[...] = xsend[...] + jnp.sum(xrecv[...], axis=0)
     wait(copies)
-    if not own:
-        start(tcopies)
-    mine, theirs = send[:gr, :], recv[:, :gr, :]
-    best = jnp.maximum(mine, jnp.max(theirs, axis=0))
-    acc = send[gr:, :] * jnp.exp(mine - best) + jnp.sum(recv[:, gr:, :] * jnp.exp(theirs - best[None]), axis=0)
-    lse = best + jnp.log(acc)
-    lse = jnp.concatenate([lse[g:g + 1, :] for g in range(mask.shape[1] // LANES)], axis=1)
+    m, s = merge(send[mine, :], send[mid, :], recv[:, mine, :], recv[:, mid, :])
+    out[...] = zeros(out)
+    out[mine, :] = m + jnp.log(s)
+    start(back)
+    wait(back)
+    a, b = out[mine, :], outr[mine, :]
+    lse = jnp.concatenate([jnp.where(core == 0, a, b), jnp.where(core == 0, b, a)], axis=0)
+    lse = to_row(lse, base)
     c_ref[...] = jnp.where(mask > 0, lse - jnp.log(w), BIG)
-    loss = functools.reduce(jnp.add, pieces(w * lse))
-    if own:
-        loss_ref[...] = loss
-    else:
-        wait(tcopies)
-        total = tsend[...] + jnp.sum(trecv[...], axis=0)
-        dwsum_ref[...] = jnp.concatenate([total[g:g + 1, :] for g in range(last)], axis=1)
-        loss_ref[...] = jnp.sum(loss + loss0_ref[...] - total[last:last + 1, :], axis=1, keepdims=True)
-
-
-def stats(lists, order, stat, count, tps, xs, cid, adds=()):
-    own = not adds
+    loss_ref[...] = functools.reduce(jnp.add, pieces(w * lse))
+
+
+def stats(lists, order, stat, count, tps, cid):
     width = sum(m.shape[1] for m in stat[::2])
-    tok = lists[0].shape[1]
     gr = -(-width // (LANES * SUB)) * SUB
-    n = 2 * tps - 1
-    outs = [line(width), line(width), line(LANES if own else 1)]
-    scratch = [pltpu.VMEM((2 * gr, LANES), F32), pltpu.VMEM((n, 2 * gr, LANES), F32)]
-    if not own:
-        outs.append(shape(*adds[0].shape))
-        xr = adds[0].shape[1] // LANES + SUB
-        near = 2 * xs - 1
-        scratch += [pltpu.VMEM((xr, LANES), F32), pltpu.VMEM((near, xr, LANES), F32),
-                    pltpu.VMEM((xr, LANES), F32), pltpu.VMEM((tps - 1, xr, LANES), F32)]
-        n += near + tps - 1
+    pair, some, line_ = (pltpu.VMEM((rows, LANES), F32) for rows in (2 * gr, 2 * SUB, SUB))
     return pl.pallas_call(
-        functools.partial(stats_kernel, tps, xs, order, own),
-        out_shape=outs,
+        functools.partial(stats_kernel, tps, order),
+        out_shape=[line(width), line(width), line(LANES)],
         grid=(1,),
-        in_specs=[fixed(SUB, tok)] * len(lists) + [fixed(*a.shape) for a in (*stat, count, *adds)],
-        out_specs=[fixed(*o.shape) for o in outs],
-        scratch_shapes=scratch + dmas(n),
+        in_specs=[fixed(SUB, lists[0].shape[1])] * len(lists) + [fixed(*a.shape) for a in (*stat, count)],
+        out_specs=[one_row(width), one_row(width), one_row(LANES)],
+        scratch_shapes=[pair, pair, some, pltpu.VMEM((tps - 1, 2 * SUB, LANES), F32), line_, line_, *dmas(tps + 1)],
         compiler_params=comm(cid),
-        cost_estimate=cost(2e9, 1 << 16),
-    )(*lists, *stat, count, *adds)
+        cost_estimate=cost(SMALL, 1 << 16),
+    )(*lists, *stat, count)
 
 
 def fill_teacher(cnt_ref, first, nrb, tabr_ref, tabp_ref, w_ref, lists, plan, lane_block, half, tm, src, sem):
@@ -728,6 +746,40 @@
             return carry
 
         lax.fori_loop(0, width // LANES, tile, 0)
+
+
+class Ring:
+    def __init__(self, srcs, b0, buf, sem):
+        self.srcs, self.b0, self.buf, self.sem = srcs, b0, buf, sem
+
+    def copies(self, k):
+        depth, rows = self.buf.shape[:2]
+        slot = lax.rem(k, depth)
+        c0 = 0
+        for a, src in enumerate(self.srcs):
+            c1 = c0 + src.shape[1]
+            yield pltpu.make_async_copy(src.at[at((self.b0 + k) * rows, rows), :], self.buf.at[slot, :, c0:c1],
+                                        self.sem.at[slot, a])
+            c0 = c1
+
+    def turn(self, i, last):
+        ahead = self.buf.shape[0] - 1
+
+        @pl.when(i == 0)
+        def _():
+            for k in range(ahead):
+                start(self.copies(k))
+
+        @pl.when(i + ahead <= last)
+        def _():
+            start(self.copies(i + ahead))
+
+        wait(self.copies(i))
+        return self.buf.at[lax.rem(i, ahead + 1)]
+
+
+def ring_scratch(rows, cols, n):
+    return [pltpu.VMEM((3, rows, cols), F32), pltpu.SemaphoreType.DMA((3, n))]
 
 
 def g_tile(z_ref, z0, c_ref, cs, rb, tabr_ref, tabp_ref, tm, put):
@@ -760,15 +812,16 @@
     return [pltpu.VMEM((vb, width), F32), pltpu.VMEM((lists[0].shape[0], LANES), F32), pltpu.SemaphoreType.DMA((1,))]
 
 
-def g_kernel(half, plan, lane_block, cnt_ref, z_ref, c_ref, tabr_ref, tabp_ref, w_ref, *refs):
-    lists, (g_ref, gt_ref, tz_ref, tm, src, sem) = refs[:-6], refs[-6:]
+def g_kernel(half, plan, lane_block, cnt_ref, z_hbm, c_ref, tabr_ref, tabp_ref, w_ref, *refs):
+    lists, (g_ref, gt_ref, tz_ref, tm, src, sem, zbuf, zsem) = refs[:-8], refs[-8:]
     i = step_id()
-    vb, width = z_ref.shape
+    vb, width = g_ref.shape
+    z_ref = Ring((z_hbm,), 0, zbuf, zsem).turn(i, last_step())
     nrb = vb // LANES
 
     @pl.when(i == 0)
     def _():
-        tz_ref[...] = jnp.zeros(tz_ref.shape, F32)
+        tz_ref[...] = zeros(tz_ref)
 
     slots = most_slots(cnt_ref, i * nrb, nrb)
 
@@ -800,7 +853,7 @@
 
 def g_own(cnt, z, c, tables, w, lists, plan, lane_block):
     half, width = z.shape
-    vb = WIDE
+    vb = 2 * WIDE
     trows = vb // LANES * SLOTS
 
     def row(i, n):
@@ -812,10 +865,10 @@
         grid_spec=pltpu.PrefetchScalarGridSpec(
             num_scalar_prefetch=1,
             grid=(half // vb,),
-            in_specs=[pl.BlockSpec((vb, width), row), one_row(width), pl.BlockSpec((trows, width), row),
+            in_specs=[ANY, one_row(width), pl.BlockSpec((trows, width), row),
                       pl.BlockSpec((trows, width), row), one_row(width)] + [ANY] * len(lists),
             out_specs=(pl.BlockSpec((vb, width), row), pl.BlockSpec((width, vb), lambda i, n: (0, i)), fixed(SUB, width)),
-            scratch_shapes=fill_scratch(vb, width, lists),
+            scratch_shapes=fill_scratch(vb, width, lists) + ring_scratch(vb, width, 1),
         ),
         compiler_params=params(dimension_semantics=ORDERED),
         cost_estimate=cost(LARGE, half * width * 8, half * width),
@@ -823,22 +876,25 @@
     )(cnt, z, c, *tables, w, *lists)
 
 
-def du_kernel(vocab, half, gt_ref, e_ref, out_ref, mine, send, recv, ssem, rsem):
+def du_kernel(vocab, half, gt_ref, left, right, e_ref, out_ref, p_left, p_right, mine, send, recv, ssem, rsem):
     i = step_id()
     core = lax.axis_index('core')
     rows = core_rows(vocab, half)
     tok = out_ref.shape[0]
-    tiles = (last_step() + 1) - 2
+    tiles = last_step() - 1
     cut = (vocab - half) // TILE * TILE
+    links = Links(ssem, rsem)
+    swap = [links.copy(left, p_left, other_core()), links.copy(right, p_right, other_core())]
 
     @pl.when(i == 0)
     def _():
         hello([other_core()])
         meet([other_core()])
+        start(swap)
 
     def copy(k):
         return pltpu.make_async_remote_copy(
-            src_ref=send.at[k], dst_ref=recv.at[k], send_sem=ssem.at[k], recv_sem=rsem.at[k],
+            src_ref=send.at[k], dst_ref=recv.at[k], send_sem=ssem.at[2 + k], recv_sem=rsem.at[2 + k],
             device_id=other_core(), device_id_type=MESH)
 
     @pl.when((i >= 1) & (i <= tiles))
@@ -863,37 +919,42 @@
         copy(i - 2).wait()
         out_ref[...] = mine[i - 2] + recv[i - 2]
 
-
-def du_call(gt, emb, half):
+    @pl.when(i == last_step())
+    def _():
+        wait(swap)
+
+
+def du_call(gt, left, right, emb, half):
     vocab, dim = emb.shape
     tok = gt.shape[0] // 2
-    tiles = dim // WIDE
-    buf = pltpu.VMEM((tiles, tok, WIDE), F32)
-    dma = pltpu.SemaphoreType.DMA((tiles,))
+    n = dim // WIDE
+    buf = pltpu.VMEM((n, tok, WIDE), F32)
+    near = shape(*left.shape)
     return pl.pallas_call(
         functools.partial(du_kernel, vocab, half),
-        out_shape=shape(tok, dim),
-        grid=(tiles + 2,),
-        in_specs=[fixed(*gt.shape),
-                  pl.BlockSpec((half, WIDE), lambda i: (lax.axis_index('core'), jnp.minimum(i, tiles - 1)))],
-        out_specs=pl.BlockSpec((tok, WIDE), lambda i: (0, jnp.maximum(i - 2, 0))),
-        scratch_shapes=[buf, buf, buf, dma, dma],
+        out_shape=(shape(tok, dim), near, near),
+        grid=(n + 2,),
+        in_specs=[fixed(*gt.shape), ANY, ANY,
+                  pl.BlockSpec((half, WIDE), lambda i: (lax.axis_index('core'), jnp.minimum(i, n - 1)))],
+        out_specs=(pl.BlockSpec((tok, WIDE), lambda i: (0, jnp.maximum(i - 2, 0))), ANY, ANY),
+        scratch_shapes=[buf, buf, buf, *dmas(n + 2)],
         compiler_params=comm(2, dimension_semantics=ORDERED),
         cost_estimate=cost(4.0 * half * tok * dim, half * dim * 2),
         name='grad_u',
-    )(gt, emb)
+    )(gt, left, right, emb)
 
 
 def de_kernel(half, b0, nu, plan, lane_block, cnt_ref, *refs):
     u_refs, refs = refs[:nu], refs[nu:]
-    zn_ref, zf_ref, gown_ref, c_ref, tabr_ref, tabp_ref, w_ref = refs[:7]
+    zn, zf, gown_ref, c_ref, tabr_ref, tabp_ref, w_ref = refs[:7]
     lists = refs[7:13]
-    out_ref, part_ref, u_ref, g_ref, tm, src, sem = refs[-7:]
+    out_ref, part_ref, u_ref, g_ref, tm, src, sem, zbuf, zsem = refs[-9:]
     i = step_id()
     vb, mine = gown_ref.shape
     cols = out_ref.shape[1]
     nrb = vb // LANES
     first = (b0 + i) * nrb
+    z_ref = Ring((zn, zf), b0, zbuf, zsem).turn(i, last_step())
 
     @pl.when(i == 0)
     def _():
@@ -903,21 +964,20 @@
             base += ref.shape[0]
 
     def make(full):
-        acc = jnp.dot(gown_ref[...], u_ref[:mine, :], preferred_element_type=F32)
-        c0 = 0
-        for z_ref in (zn_ref, zf_ref):
-            for z0 in range(0, z_ref.shape[1], TILE):
+        for r0 in range(0, vb, TILE):
+            rows = slice(r0, r0 + TILE)
+            acc = jnp.dot(gown_ref[rows, :], u_ref[:mine, :], preferred_element_type=F32)
+            for c0 in range(0, g_ref.shape[1], TILE):
                 cs = slice(c0, c0 + TILE)
 
                 def put(rs, g, t, z):
                     g_ref[rs, cs] = g
 
-                for rb in range(nrb):
-                    g_tile(z_ref, z0, c_ref, cs, rb, tabr_ref, tabp_ref, full, put)
-                acc = acc + jnp.dot(g_ref[:, cs], u_ref[mine + c0:mine + c0 + TILE, :], preferred_element_type=F32)
-                c0 += TILE
-        out_ref[...] = acc[:, :cols]
-        part_ref[...] = acc[:, cols:]
+                for rb in range(r0 // LANES, (r0 + TILE) // LANES):
+                    g_tile(z_ref, c0, c_ref, cs, rb, tabr_ref, tabp_ref, full, put)
+                acc = acc + jnp.dot(g_ref[rows, cs], u_ref[mine + c0:mine + c0 + TILE, :], preferred_element_type=F32)
+            out_ref[rows, :] = acc[:, :cols]
+            part_ref[rows, :] = acc[:, cols:]
 
     slots = most_slots(cnt_ref, first, nrb)
 
@@ -935,16 +995,17 @@
     half, mine = gown.shape
     ccols = us[0].shape[1]
     cols = ccols // 2
-    tot = half // TILE
+    vb = WIDE
+    tot = half // vb
     width = zn.shape[1] + zf.shape[1]
-    trows = TILE // LANES * SLOTS
-
-    def rows(cols_, height=TILE):
+    trows = vb // LANES * SLOTS
+
+    def rows(cols_, height=vb):
         return pl.BlockSpec((height, cols_), lambda i, n: (b0 + i, 0))
 
     in_specs = [fixed(*u.shape) for u in us]
-    in_specs += [rows(zn.shape[1]), rows(zf.shape[1]), rows(mine), one_row(width), rows(width, trows), rows(width, trows),
-                 one_row(width)] + [ANY] * len(lists)
+    in_specs += [ANY, ANY, rows(mine), one_row(width), rows(width, trows), rows(width, trows), one_row(width)]
+    in_specs += [ANY] * len(lists)
     args = [*us, zn, zf, gown, c, *tables, w, *lists]
     aliases = {}
     if prev is not None:
@@ -953,22 +1014,22 @@
         in_specs.append(ANY)
     return pl.pallas_call(
         functools.partial(de_kernel, half, b0, len(us), plan, lane_block),
-        out_shape=(shape(vocab, cols), shape(nb * TILE, cols)),
+        out_shape=(shape(vocab, cols), shape(nb * vb, cols)),
         grid_spec=pltpu.PrefetchScalarGridSpec(
             num_scalar_prefetch=1,
             grid=(nb,),
             in_specs=in_specs,
             out_specs=(
-                pl.BlockSpec((TILE, cols), lambda i, n: (lax.axis_index('core') * tot + b0 + i, 0)),
-                pl.BlockSpec((TILE, cols), lambda i, n: (i, 0)),
+                pl.BlockSpec((vb, cols), lambda i, n: (lax.axis_index('core') * tot + b0 + i, 0)),
+                pl.BlockSpec((vb, cols), lambda i, n: (i, 0)),
             ),
-            scratch_shapes=[pltpu.VMEM((width + mine, ccols), BF16), pltpu.VMEM((TILE, width), BF16),
-                            *fill_scratch(TILE, width, lists)],
+            scratch_shapes=[pltpu.VMEM((width + mine, ccols), BF16), pltpu.VMEM((vb, width), BF16),
+                            *fill_scratch(vb, width, lists), *ring_scratch(vb, width, 2)],
         ),
         input_output_aliases=aliases,
         compiler_params=params(dimension_semantics=ORDERED),
-        cost_estimate=cost(3.0 * nb * TILE * (width + mine) * ccols, nb * TILE * (width * 4 + mine * 2 + ccols * 4),
-                           nb * TILE * width),
+        cost_estimate=cost(3.0 * nb * vb * (width + mine) * ccols, nb * vb * (width * 4 + mine * 2 + ccols * 4),
+                           nb * vb * width),
     )(cnt, *args)
 
 
@@ -1035,43 +1096,56 @@
         part = tok // tps
         cut = tok // 2
         tg = tok // LANES
-        scale = (1.0 + norm_weight).reshape(row_of(norm_weight))
+        weight = norm_weight.reshape(row_of(norm_weight))
         mask = tok_mask.reshape(row_of(tok_mask))
+        ccols = dim // xs
+        dma = pltpu.SemaphoreType.DMA
 
         normed, inv_rms, count = norm(hidden, mask, xs)
         left = shift(normed, 'x', 1)
         right = shift(normed, 'x', -1)
-        lists, y_part, l_part = sort_lists(teach_ids, teach_prob, mask, normed, vocab, vocab * tps)
-
-        z0, m0, s0, u0 = forward(own_kernel, [normed, y_part], [fixed(tok, dim)] * 2, scale, embedding, half, 2 * WIDE,
-                                 chip)
+        lists, y_part = sort_lists(teach_ids, teach_prob, mask, normed, vocab, vocab * tps)
+        l_left = shift(lists, 'x', 1)
+        l_right = shift(lists, 'x', -1)
+        some_lists = (shape(*lists.shape), ANY)
+
+        z0, m0, s0, u0, l_part = forward(
+            own_kernel, [normed, y_part, lists], [ANY] * 3, weight, embedding, half, 2 * WIDE, chip, ccols, 5,
+            [some_lists], [pltpu.VMEM((2, tok, dim), F32), dma((2,)), *dmas(1)])
         full = slice(tok)
         lo, hi = slice(cut), slice(cut, tok)
-        c0, w0, loss0 = stats([lists, l_part], ((full,),), (m0, s0), count, tps, xs, 0)
+        c0, w0, loss0 = stats([lists, l_part], ((full,),), (m0, s0), count, tps, 0)
         own_plan = (lambda g, c: lax.rem(g // tg + c, 2)), (lambda g: lax.rem(g, tg))
         tab0, cnt0 = expand([lists, l_part], *own_plan, w0, vocab, half)
         g0, gt0, tz = g_own(cnt0, z0, c0, tab0, w0, [lists, l_part], *own_plan)
-        du = du_call(gt0, embedding, half)
-
-        my_normed = lax.dynamic_slice(normed, (lax.axis_index('tp') * part, 0), (part, dim))
+        du, p_left, p_right = du_call(gt0, left, right, embedding, half)
+
         square = pltpu.VMEM((n, n, part, dim // 2), F32)
         strip = pltpu.VMEM((n, part, dim // 2), F32)
         short = pltpu.VMEM((n - 1, part, dim // 2), F32)
-        dma = pltpu.SemaphoreType.DMA
-        z1, m1, s1, u1, far0, far1, d_rest, dw = forward(
-            functools.partial(near_kernel, xs, n), [left, right, du.reshape(n, n, part, dim), my_normed],
-            [ANY] * 3 + [fixed(part, dim)], scale, embedding, half, WIDE, 2 * chip,
-            outs=[(shape(cut, dim), ANY)] * 2 + [(shape(part, dim), fixed(part, dim)), (line(dim), one_row(dim))],
-            scratch=[*tokens_scratch(tok, dim), square, square, strip, strip, short, short, dma((4,)),
-                     *dmas(4 + 4 * (n - 1))], cid=3)
-        one = (shape(*lists.shape), ANY)
-        z2, m2, s2, u2, dh, *l_rest = forward(
-            functools.partial(far_kernel, xs, n), [far0, far1, lists, d_rest], [ANY] * 3 + [fixed(part, dim)],
-            scale, embedding, half, WIDE, chip,
-            outs=[(jax.ShapeDtypeStruct((n, n, part, dim), F32), ANY)] + [one] * 6,
-            scratch=[*tokens_scratch(cut, dim), dma((3,)), *dmas(9 + 4 * (n - 1))], cid=6)
-        c1, w1, loss, dw_sum = stats(l_rest, ((full,), (full,), (lo, hi)), (m1, s1, m2, s2), count, tps, xs, 1,
-                                     (dw, tz, loss0))
+        some_far = (shape(cut, dim), ANY)
+        z1, m1, s1, u1, far0, p_far0, far1, p_far1, p_ll, p_lr, d_rest, dw = forward(
+            functools.partial(near_kernel, xs, n),
+            [left, p_left, right, p_right, du.reshape(n, n, part, dim), normed, l_left, l_right], [ANY] * 8,
+            weight, embedding, half, WIDE, 2 * chip, ccols, 3,
+            [some_far] * 4 + [some_lists] * 2 + [(shape(part, dim), fixed(part, dim)), (line(dim), one_row(dim))],
+            [pltpu.VMEM((4, tok, dim), F32), square, square, strip, strip, short, short, pltpu.VMEM((part, dim), F32),
+             dma((7,)), *dmas(6 + 4 * (n - 1))])
+        sums = pltpu.VMEM((dim // LANES + SUB, LANES), F32)
+
+        def many(k):
+            return pltpu.VMEM((k - 1, dim // LANES + SUB, LANES), F32)
+
+        z2, m2, s2, u2, dh, l_far, p_lf, dw_sum, tz_sum = forward(
+            functools.partial(far_kernel, xs, n), [far0, p_far0, far1, p_far1, l_left, l_right, d_rest, dw, tz],
+            [ANY] * 6 + [fixed(part, dim), one_row(dim), fixed(*tz.shape)],
+            weight, embedding, half, WIDE, chip, ccols, 6,
+            [(jax.ShapeDtypeStruct((n, n, part, dim), F32), ANY), some_lists, some_lists,
+             (line(dim), one_row(dim)), (line(LANES), one_row(LANES))],
+            [pltpu.VMEM((4, cut, dim), F32), sums, many(2 * xs), sums, many(tps), dma((5,)),
+             *dmas(3 + 2 * xs - 1 + tps - 1 + 2 * (n - 1) + 8)])
+        l_rest = [l_left, p_ll, l_right, p_lr, l_far, p_lf]
+        c1, w1, loss1 = stats(l_rest, ((full,), (full,), (lo, hi)), (m1, s1, m2, s2), count, tps, 1)
 
         def plan(g, c):
             far = g // (2 * tg) == 2
@@ -1084,7 +1158,7 @@
         rest_plan = plan, lane_block
         tab1, cnt1 = expand(l_rest, *rest_plan, w1, vocab, half)
 
-        nb = half // TILE
+        nb = half // WIDE
         n0 = nb // 2
 
         def grad_e(b0, count_, prev):
@@ -1096,7 +1170,7 @@
         recv1 = shift(send1, 'core', 1)
         grad_hidden = dh_call(dh.reshape(tok, dim), inv_rms)
         out = place([recv0, recv1], out, half)
-        return loss.reshape(()), grad_hidden, out, dw_sum.reshape(dim)
+        return jnp.sum(loss0 + loss1 - tz_sum), grad_hidden, out, dw_sum.reshape(dim)
 
     tokens = ('x', 'core')
     return jax.shard_map(

time: 239 us -> 216 us (0.904)
  Pallas kernels: 224 us -> 202 us
    pallas_call x3, Pallas kernels: 91.9 us -> 80.7 us  [forward(): pl.pallas_call(functools.partial(kernel, vocab, half), out_shape=[shape(h...]
    pallas_call x3, Pallas kernels: 48.7 us -> 44.8 us  [the longest x2 28 us: stats(): pl.pallas_call(functools.partial(stats_kernel, tps, order), out_shape=[li...]
    pallas_call x2, Pallas kernels: 27 us -> 23.7 us  [de_call(): pl.pallas_call(functools.partial(de_kernel, half, b0, len(us), plan, lane...]
    ppermute x4 -> x6, starting transfers between devices: 3.78 us -> 5.44 us  [shift(): return lax.ppermute(x, axis, [(i, (i + by) % size) for i in range(size)])]
  transfers between devices with their start and end apart: 4 -> 6, of which waited for: 2 -> 1; matrix products, arithmetic and copies ran while one was open for 1% -> 0% of each run, Pallas kernels for 32% -> 35%
where the time goes in v4:
time: 216 us; the launch traced here: 214 us
  Pallas kernels  202 us (94%)
  starting transfers between devices  5.44 us (3%)
  local copies, waits for them, and re-layouts  2.87 us (1%)
  waiting for transfers between devices  2.65 us (1%)
    pallas_call x3, Pallas kernels, forward(): pl.pallas_call(functools.partial(kernel, vocab, half), out_shape=[shape(h...  80.7 us
    pallas_call x2, Pallas kernels, stats(): pl.pallas_call(functools.partial(stats_kernel, tps, order), out_shape=[li...  28 us
    pallas_call x2, Pallas kernels, de_call(): pl.pallas_call(functools.partial(de_kernel, half, b0, len(us), plan, lane...  23.7 us
    pallas_call x2, Pallas kernels, expand(): pl.pallas_call(functools.partial(expand_kernel, vocab, half, plan, lane_b...  17.2 us
    pallas_call x1, Pallas kernels, du_call(): pl.pallas_call(functools.partial(du_kernel, vocab, half), out_shape=(shap...  16.8 us
    pallas_call x1, Pallas kernels, g_own(): pl.pallas_call(functools.partial(g_kernel, half, plan, lane_block), out_s...  10.1 us
    pallas_call x1, Pallas kernels, norm(): pl.pallas_call(functools.partial(norm_kernel, xs), out_shape=(shape(tok,...  9.75 us
    pallas_call x1, Pallas kernels, sort_lists(): pl.pallas_call(functools.partial(sort_kernel, vocab, whole), out_shape=(l...  6.66 us
  transfers between devices with their start and end apart: 6, of which 1 were waited for; matrix products, arithmetic and copies ran while one was open for 0% of the time, Pallas kernels for 35%

profile of v4, /device:TPU:1, one launch (start us, length us, event | category | flops | bytes accessed | tf_op | source)
XLA Modules:
  0.0 214.3 jit_solution(15182142648993144562)
XLA Ops:
  0.6 9.7 %norm.1 = (f32[256,2048]{1,0:T(8,128)}, f32[256,1]{1,0:T(8,128)}, f32[1,128]{1,0:T(1,128)}) custom-call(bf16[256,2048]{1,0:T(8,128)(2,1)} %h_ref.1, f32[1,256]{1,0:T(1,128)} %bitcast.11), custom_call_target="tpu_custom_call" | custom-call | flops 1000000000 | bytes 3145728 | tf_op jit(solution)/shard_map/norm/pallas_call | solution.py:184
  10.4 1.8 collective-permute-start.2
  12.2 0.0 collective-permute-start.1
  12.2 6.7 %sort_lists.1 = (f32[512,256]{1,0:T(8,128)}, f32[256,2048]{1,0:T(8,128)}) custom-call(s32[256,256]{1,0:T(8,128)} %ids_ref.1, f32[256,256]{1,0:T(8,128)} %pt_ref.1, f32[1,256]{1,0:T(1,128)} %bitcast.12, f32[256,2048]{1,0:T(8,128)} %get-tuple-element.57.y_hbm.y), custom_call_target="tpu_custom_call" | custom-call | flops 4000000000 | bytes 1048576 | tf_op jit(solution)/shard_map/sort_lists/pallas_call | solution.py:252
  18.9 3.0 %collective-permute-start.3 = (f32[512,256]{1,0:T(8,128)}, f32[512,256]{1,0:T(8,128)S(1)}, u32[]{:S(2)}, u32[]{:S(2)}) collective-permute-start(f32[512,256]{1,0:T(8,128)} %get-tuple-element.58.lists.refs_0_), channel_id=1, source_target_pairs={{0,6},{2,0},{4,2},{6,4},{1,7},{3,1},{5,3},{7,5},{8,14},{10,8},{12,... | collective-permute-start | bytes 1572872 | tf_op jit(solution)/shard_map/ppermute | solution.py:1089
  21.9 0.0 collective-permute-start
  21.9 17.9 %shard_map.93 = (f32[4096,512]{1,0:T(8,128)}, f32[8,512]{1,0:T(8,128)}, f32[8,512]{1,0:T(8,128)}, bf16[512,512]{1,0:T(8,128)(2,1)}, f32[512,256]{1,0:T(8,128)}) custom-call(f32[256,2048]{1,0:T(8,128)} %get-tuple-element.57.y_hbm.y, f32[256,2048]{1,0:T(8,128)} %get-tuple-element.59.ypart, f32[512,256]{1,0:T(8,128)} %get-tuple-element.58.lists.refs_0_, ...), custom_call_target="tpu_custom_call" | custom-call | flops 8589934592 | bytes 29360128 | tf_op jit(solution)/shard_map/pallas_call | solution.py:618
  39.8 15.0 %shard_map.94 = (f32[1,512]{1,0:T(1,128)}, f32[1,512]{1,0:T(1,128)}, f32[1,128]{1,0:T(1,128)}) custom-call(f32[512,256]{1,0:T(8,128)} %get-tuple-element.58.lists.refs_0_, f32[512,256]{1,0:T(8,128)} %get-tuple-element.60.refs_1_, f32[8,512]{1,0:T(8,128)} %get-tuple-element.61.refs_2_, f32[8,512]{1,0:T(8,128)} %get-tuple-element.62.refs_3_, ...), custom_call_target="tpu_custom_call" | custom-call | flops 100000000 | bytes 65536 | tf_op jit(solution)/shard_map/pallas_call | solution.py:694
  54.9 5.5 %shard_map.95 = (s32[256,512]{1,0:T(8,128)}, f32[256,512]{1,0:T(8,128)}, s32[32,128]{1,0:T(8,128)}) custom-call(f32[512,256]{1,0:T(8,128)} %get-tuple-element.58.lists.refs_0_, f32[512,256]{1,0:T(8,128)} %get-tuple-element.60.refs_1_, f32[1,512]{1,0:T(1,128)} %get-tuple-element.65.refs_2_.w_ref), custom_call_target="tpu_custom_call" | custom-call | flops 400000000 | bytes 2097152 | tf_op jit(solution)/shard_map/pallas_call | solution.py:374
  60.4 10.1 %g_own.1 = (bf16[4096,512]{1,0:T(8,128)(2,1)}, bf16[512,4096]{1,0:T(8,128)(2,1)}, f32[8,512]{1,0:T(8,128)}) custom-call(s32[32,128]{1,0:T(8,128)} %get-tuple-element.66.cnt_ref, f32[4096,512]{1,0:T(8,128)} %get-tuple-element.67.z_hbm, f32[1,512]{1,0:T(1,128)} %get-tuple-element.68.c_ref, s32[256,512]{1,0:T(8,128)} %get-tuple-element.69.tabr_ref, ...), custom_call_target="tpu_custom_call" | custom-call | flops 4000000000 | bytes 16777216 | tf_op jit(solution)/shard_map/g_own/pallas_call | solution.py:862
  70.5 0.0 collective-permute-done.2.right
  70.5 0.0 copy-start.2
  70.5 0.0 collective-permute-done.1.left
  70.5 1.3 copy-done.2
  71.9 16.8 %grad_u.1 = (f32[256,2048]{1,0:T(8,128)}, f32[256,2048]{1,0:T(8,128)}, f32[256,2048]{1,0:T(8,128)}) custom-call(bf16[512,4096]{1,0:T(8,128)(2,1)} %get-tuple-element.71.gt_ref, f32[256,2048]{1,0:T(8,128)} %collective-permute-done.1.left, f32[256,2048]{1,0:T(8,128)} %copy-done.2, bf16[8016,2048]{1,0:T(8,128)(2,1)} %e_ref.7), custom_call_target="tpu_custom_call" | custom-call | flops 8589934592 | bytes 16777216 | tf_op jit(solution)/shard_map/grad_u/pallas_call | solution.py:933
  88.7 0.0 collective-permute-done.3.l_right.refs_2_.refs_12_
  88.7 0.0 copy-start
  88.7 0.0 collective-permute-done.l_left.refs_0_.refs_10_
  88.7 0.0 copy-start.1
  88.7 0.8 copy-done
  89.5 0.2 copy-done.1
  89.6 36.7 %shard_map.96 = (f32[4096,1024]{1,0:T(8,128)}, f32[8,1024]{1,0:T(8,128)}, f32[8,1024]{1,0:T(8,128)}, bf16[1024,512]{1,0:T(8,128)(2,1)}, f32[128,2048]{1,0:T(8,12...) custom-call(f32[256,2048]{1,0:T(8,128)} %collective-permute-done.1.l, ...), custom_call_target="tpu_custom_call" | custom-call | flops 17179869184 | bytes 41943040 | tf_op jit(solution)/shard_map/pallas_call | solution.py:618
  126.4 26.1 %shard_map.97 = (f32[4096,512]{1,0:T(8,128)}, f32[8,512]{1,0:T(8,128)}, f32[8,512]{1,0:T(8,128)}, bf16[512,512]{1,0:T(8,128)(2,1)}, f32[4,4,16,2048]{3,2,1,0:T(8...) custom-call(f32[128,2048]{1,0:T(8,128)} %get-tuple-element.77.far0, ...), custom_call_target="tpu_custom_call" | custom-call | flops 8589934592 | bytes 29360128 | tf_op jit(solution)/shard_map/pallas_call | solution.py:618
  152.4 13.0 %shard_map.98 = (f32[1,1536]{1,0:T(1,128)}, f32[1,1536]{1,0:T(1,128)}, f32[1,128]{1,0:T(1,128)}) custom-call(f32[512,256]{1,0:T(8,128)} %copy-done.1, f32[512,256]{1,0:T(8,128)} %get-tuple-element.75.refs_1_.refs_11_, f32[512,256]{1,0:T(8,128)} %copy-done, f32[512,256]{1,0:T(8,128)} %get-tuple-element.76.refs_3_.refs_13_, ...), custom_call_target="tpu_custom_call" | custom-call | flops 100000000 | bytes 65536 | tf_op jit(solution)/shard_map/pallas_call | solution.py:694
  165.4 11.7 %shard_map.99 = (s32[256,1536]{1,0:T(8,128)}, f32[256,1536]{1,0:T(8,128)}, s32[32,128]{1,0:T(8,128)}) custom-call(f32[512,256]{1,0:T(8,128)} %copy-done.1, f32[512,256]{1,0:T(8,128)} %get-tuple-element.75.refs_1_.refs_11_, f32[512,256]{1,0:T(8,128)} %copy-done, f32[512,256]{1,0:T(8,128)} %get-tuple-element.76.refs_3_.refs_13_, ...), custom_call_target="tpu_custom_call" | custom-call | flops 1200000000 | bytes 6291456 | tf_op jit(solution)/shard_map/pallas_call | solution.py:374
  177.1 11.9 %shard_map.100 = (f32[8016,256]{1,0:T(8,128)}, f32[2048,256]{1,0:T(8,128)}) custom-call(s32[32,128]{1,0:T(8,128)} %get-tuple-element.95.cnt_ref, bf16[512,512]{1,0:T(8,128)(2,1)} %get-tuple-element.96.refs_0_, bf16[1024,512]{1,0:T(8,128)(2,1)} %get-tuple-element.97.refs_1_, bf16[512,512]{1,0:T(8,128)(2,1)} %get-tuple-element.98.refs_2_, ...), custom_call_target="tpu_custom_call" | custom-call | flops 6442450944 | bytes 18874368 | tf_op jit(solution)/shard_map/pallas_call | solution.py:1015
  189.0 11.8 %shard_map.101 = (f32[8016,256]{1,0:T(8,128)}, f32[2048,256]{1,0:T(8,128)}) custom-call(s32[32,128]{1,0:T(8,128)} %get-tuple-element.95.cnt_ref, bf16[512,512]{1,0:T(8,128)(2,1)} %get-tuple-element.96.refs_0_, bf16[1024,512]{1,0:T(8,128)(2,1)} %get-tuple-element.97.refs_1_, ...), custom_call_target="tpu_custom_call", output_to_operand_aliasing={{0}: (17, {})} | custom-call | flops 6442450944 | bytes 18874368 | tf_op jit(solution)/shard_map/pallas_call | solution.py:1015
  200.8 0.0 copy-start.5
  200.8 0.0 copy-start.6
  200.8 0.0 copy-start.7
  200.8 0.3 collective-permute-start.5
  201.1 0.3 collective-permute-start.4
  201.4 3.7 %grad_h.1 = bf16[256,2048]{1,0:T(8,128)(2,1)} custom-call(f32[256,2048]{1,0:T(8,128)} %bitcast.5, f32[256,1]{1,0:T(8,128)} %get-tuple-element.93.inv_ref), custom_call_target="tpu_custom_call" | custom-call | flops 100000000 | bytes 3145728 | tf_op jit(solution)/shard_map/grad_h/pallas_call | solution.py:1069
  205.1 0.0 copy-done.5
  205.1 0.0 copy-done.6
  205.2 0.0 copy-done.7
  205.2 0.6 subtract_reduce_fusion
  205.8 0.0 collective-permute-done.5.b_ref
  205.8 0.0 copy-start.3
  205.8 2.6 %collective-permute-done.4.a_ref = f32[2048,256]{1,0:T(8,128)} collective-permute-done((f32[2048,256]{1,0:T(8,128)}, f32[2048,256]{1,0:T(8,128)}, u32[]{:S(2)}, u32[]{:S(2)}) %collective-permute-start.4) | collective-permute-done | bytes 2097184 | tf_op jit(solution)/shard_map/ppermute | solution.py:1089
  208.4 0.0 copy-done.3
  208.4 0.0 copy-start.4
  208.4 5.3 %place.1 = f32[8016,256]{1,0:T(8,128)} custom-call(f32[2048,256]{1,0:T(8,128)} %collective-permute-done.4.a_ref, f32[2048,256]{1,0:T(8,128)} %copy-done.3, f32[8016,256]{1,0:T(8,128)} %get-tuple-element.108.prev_ref), custom_call_target="tpu_custom_call", output_to_operand_aliasing={{}: (2, {})} | custom-call | flops 100000000 | bytes 8208384 | tf_op jit(solution)/shard_map/place/pallas_call | solution.py:1048
  213.7 0.0 copy-done.4
  213.7 0.6 copy.15
Async XLA Ops:
  10.4 60.1 %collective-permute-start.2 = (f32[256,2048]{1,0:T(8,128)}, f32[256,2048]{1,0:T(8,128)S(1)}, u32[]{:S(2)}, u32[]{:S(2)}) collective-permute-start(f32[256,2048]{1,0:T(8,128)} %get-tuple-element.57.y_hbm.y), channel_id=1, source_target_pairs={{0,6},{2,0},{4,2},{6,4},{1,7},{3,1},{5,3},{7,5},{8,14},{10,8},{12,... | collective-permute-start | bytes 6291464 | tf_op jit(solution)/shard_map/ppermute | solution.py:1089
  12.2 58.3 %collective-permute-start.1 = (f32[256,2048]{1,0:T(8,128)}, f32[256,2048]{1,0:T(8,128)}, u32[]{:S(2)}, u32[]{:S(2)}) collective-permute-start(f32[256,2048]{1,0:T(8,128)} %get-tuple-element.57.y_hbm.y), channel_id=1, source_target_pairs={{0,2},{2,4},{4,6},{6,0},{1,3},{3,5},{5,7},{7,1},{8,10},{10,12},{12... | collective-permute-start | bytes 6291464 | tf_op jit(solution)/shard_map/ppermute | solution.py:1089
  18.9 69.8 %collective-permute-start.3 = (f32[512,256]{1,0:T(8,128)}, f32[512,256]{1,0:T(8,128)S(1)}, u32[]{:S(2)}, u32[]{:S(2)}) collective-permute-start(f32[512,256]{1,0:T(8,128)} %get-tuple-element.58.lists.refs_0_), channel_id=1, source_target_pairs={{0,6},{2,0},{4,2},{6,4},{1,7},{3,1},{5,3},{7,5},{8,14},{10,8},{12,... | collective-permute-start | bytes 1572872 | tf_op jit(solution)/shard_map/ppermute | solution.py:1089
  21.9 66.8 %collective-permute-start = (f32[512,256]{1,0:T(8,128)}, f32[512,256]{1,0:T(8,128)S(1)}, u32[]{:S(2)}, u32[]{:S(2)}) collective-permute-start(f32[512,256]{1,0:T(8,128)} %get-tuple-element.58.lists.refs_0_), channel_id=1, source_target_pairs={{0,2},{2,4},{4,6},{6,0},{1,3},{3,5},{5,7},{7,1},{8,10},{10,12},{12... | collective-permute-start | bytes 1572872 | tf_op jit(solution)/shard_map/ppermute | solution.py:1089
  70.5 1.3 copy-start.2
  88.7 0.8 copy-start
  88.7 0.9 copy-start.1
  200.8 4.4 %copy-start.5 = (f32[1,128]{1,0:T(1,128)S(1)}, f32[1,128]{1,0:T(1,128)}, u32[]{:S(2)}) copy-start(f32[1,128]{1,0:T(1,128)} %get-tuple-element.64) | copy-start | bytes 1540
  200.8 4.3 %copy-start.6 = (f32[1,128]{1,0:T(1,128)S(1)}, f32[1,128]{1,0:T(1,128)}, u32[]{:S(2)}) copy-start(f32[1,128]{1,0:T(1,128)} %get-tuple-element.91) | copy-start | bytes 1540
  200.8 4.3 %copy-start.7 = (f32[1,128]{1,0:T(1,128)S(1)}, f32[1,128]{1,0:T(1,128)}, u32[]{:S(2)}) copy-start(f32[1,128]{1,0:T(1,128)} %get-tuple-element.90) | copy-start | bytes 1540
  200.8 4.9 %collective-permute-start.5 = (f32[2048,256]{1,0:T(8,128)}, f32[2048,256]{1,0:T(8,128)S(1)}, u32[]{:S(2)}, u32[]{:S(2)}) collective-permute-start(f32[2048,256]{1,0:T(8,128)} %get-tuple-element.107), channel_id=1, source_target_pairs={{0,1},{1,0},{2,3},{3,2},{4,5},{5,4},{6,7},{7,6},{8,9},{9,8},{10,11... | collective-permute-start | bytes 6291464 | tf_op jit(solution)/shard_map/ppermute | solution.py:1089
  201.1 7.3 %collective-permute-start.4 = (f32[2048,256]{1,0:T(8,128)}, f32[2048,256]{1,0:T(8,128)}, u32[]{:S(2)}, u32[]{:S(2)}) collective-permute-start(f32[2048,256]{1,0:T(8,128)} %get-tuple-element.105), channel_id=1, source_target_pairs={{0,1},{1,0},{2,3},{3,2},{4,5},{5,4},{6,7},{7,6},{8,9},{9,8},{10,11... | collective-permute-start | bytes 6291464 | tf_op jit(solution)/shard_map/ppermute | solution.py:1089
  205.8 2.6 %copy-start.3 = (f32[2048,256]{1,0:T(8,128)}, f32[2048,256]{1,0:T(8,128)S(1)}, u32[]{:S(2)}) copy-start(f32[2048,256]{1,0:T(8,128)S(1)} %collective-permute-done.5.b_ref) | copy-start | bytes 6291460
  208.4 5.3 %copy-start.4 = (f32[1,2048]{1,0:T(1,128)S(1)}, f32[1,2048]{1,0:T(1,128)}, u32[]{:S(2)}) copy-start(f32[1,2048]{1,0:T(1,128)} %get-tuple-element.109) | copy-start | bytes 24580
